TPU v7x, 256 devices: a whole 4x4x8 slice. The times are simulated.
256 devices in a mesh: mem: 16 (over z, core), dom: 16 (over x, y).
Axes of the slice: x: 4, y: 4, z: 8, core: 2. Of those that a mesh axis runs over, the one named last changes fastest.
Arguments:
- prior_ensemble: float32 [64, 4, 2048, 512], P('mem', None, 'dom'), may hold values from -6 to 6
- spreading_factor: float32 [4], replicated, may hold values from 0.05 to 0.24
- tendency_matrix: float32 [4, 4], replicated, may hold values from -0.6 to 0.6
- measured_data: float32 [16, 8192], P('dom', 'mem'), may hold values from -6 to 6
- inverse_error: float32 [16, 8192], P('dom', 'mem'), may hold values from 0.1 to 1
- assigned_subregion: int32 [16, 8192, 1], P('dom', 'mem'), may hold values from 0 to 31; in each aligned block of 512 rows (0 to 511, 512 to 1023, ..., all dimensions but the last counted through in order) at most 32 rows name the same one
- measured_entry: int32 [16, 8192], P('dom', 'mem'), may hold values from 0 to 8191
- taper_index: int32 [16, 8192], P('dom', 'mem'), may hold values from 0 to 63
- taper_factors: float32 [64], replicated, may hold values from 0.2 to 1
Outputs:
- analysis: float32 [64, 4, 2048, 512], P('mem', None, 'dom')
Inputs may be any that keep to these rules, and one draw needn't show every extreme that they name: `assigned_subregion`: in the rows of one device no patch is named by more than 32 rows, a bound that some block reaches.
All inputs are finite; a program needn't handle non-finite values.
Results may differ from a plain program's by a relative error of at most 0.0003.
Values sent between devices are 32-bit elements; how exact they have to be, the bound alone decides.
No kernel may reach another device: no remote copies, remote signals or barrier semaphores. Data moves between devices by JAX's collectives and lax.ppermute only.
A program may use at most 64 MiB of HBM per device.

v0:
```python
import jax
import jax.numpy as jnp
from jax import lax
from jax.sharding import PartitionSpec as P

PATCH = 2048
NS_ITERS = 5


HIGH = lax.Precision.HIGHEST


def padded(block, sides, width):
    for axis, dim in sides:
        count = lax.axis_size(axis)
        forward = [(i, i + 1) for i in range(count - 1)]
        backward = [(target, source) for source, target in forward]
        low = lax.ppermute(
            lax.slice_in_dim(block, block.shape[dim] - width, None, axis=dim), axis, forward
        )
        high = lax.ppermute(lax.slice_in_dim(block, 0, width, axis=dim), axis, backward)
        block = jnp.concatenate([low, block, high], axis=dim)
    return block


def side_by_side(arrays, axis, split_dim, concat_dim, along):
    widths = [a.shape[along] for a in arrays]
    both = jnp.concatenate(arrays, axis=along)
    filled = lax.all_to_all(both, axis, split_axis=split_dim, concat_axis=concat_dim, tiled=True)
    return tuple(jnp.split(filled, [sum(widths[:k]) for k in range(1, len(widths))], axis=along))


def laplacian_update(haloed_ensemble, ensemble, spreading_factor, tendency_matrix):
    subdomain_lines = ensemble.shape[2]
    beside = jnp.pad(ensemble, ((0, 0), (0, 0), (0, 0), (1, 1)))
    laplace = (
        haloed_ensemble[:, :, 2:]
        + haloed_ensemble[:, :, :subdomain_lines]
        + beside[:, :, :, 2:]
        + beside[:, :, :, :-2]
        - 4.0 * ensemble
    )
    mixing = jnp.einsum("vw,kwxy->kvxy", tendency_matrix, ensemble, precision=HIGH)
    return ensemble + spreading_factor[None, :, None, None] * laplace + mixing


def transforms(gram, drive, member_count):
    identity_m = jnp.eye(member_count, dtype=jnp.float32)
    system = (member_count - 1.0) * identity_m + gram
    norm_value = jnp.sqrt(jnp.sum(system * system, axis=(-2, -1)))
    iterate = system / norm_value[..., None, None]
    inverse = jnp.broadcast_to(identity_m, system.shape)
    for sweep_no in range(NS_ITERS):
        middle = 1.5 * identity_m - 0.5 * jnp.einsum(
            "...ij,...jk->...ik", inverse, iterate, precision=HIGH
        )
        iterate = jnp.einsum("...ij,...jk->...ik", iterate, middle, precision=HIGH)
        inverse = jnp.einsum("...ij,...jk->...ik", middle, inverse, precision=HIGH)
    root = inverse / jnp.sqrt(norm_value)[..., None, None]
    inner = jnp.einsum("...ij,...j->...i", root, drive, precision=HIGH)
    offset = jnp.einsum("...ij,...j->...i", root, inner, precision=HIGH)
    return offset[..., :, None] + jnp.sqrt(member_count - 1.0) * root


def slot_ranks(patch_ids, patch_count):
    onehot = (patch_ids[..., None] == jnp.arange(patch_count, dtype=jnp.int32)).astype(jnp.int32)
    before = jnp.cumsum(onehot, axis=-2) - onehot
    return jnp.sum(before * onehot, axis=-1)


def shards(
    prior_ensemble,
    spreading_factor,
    tendency_matrix,
    measured_data,
    inverse_error,
    assigned_subregion,
    measured_entry,
    taper_index,
    taper_factors,
):
    ensemble_share, prognostic_number, subdomain_lines, eastward_span = prior_ensemble.shape
    groups = lax.axis_size("mem")
    members = ensemble_share * groups
    cells_dev = subdomain_lines * eastward_span // groups
    per_device = cells_dev // PATCH
    per_tile = per_device * groups
    haloed_ensemble = padded(prior_ensemble, (("dom", 2),), 1)
    advanced_ensemble = laplacian_update(
        haloed_ensemble, prior_ensemble, spreading_factor, tendency_matrix
    )
    moved = lax.all_to_all(
        advanced_ensemble.reshape(ensemble_share, prognostic_number, groups, cells_dev),
        "mem",
        split_axis=2,
        concat_axis=0,
        tiled=True,
    )
    ensemble = moved.reshape(members, prognostic_number, cells_dev)
    patch_ids = assigned_subregion.reshape(-1)
    obs_rows = patch_ids.shape[0]
    capacity = 2 * obs_rows // per_tile
    table_levels = taper_factors.shape[0]
    picks = (
        taper_index.reshape(-1)[:, None] == jnp.arange(table_levels, dtype=jnp.int32)[None, :]
    ).astype(jnp.float32)
    weight = inverse_error.reshape(-1) * jnp.dot(picks, taper_factors, precision=HIGH)
    values = measured_data.reshape(-1)
    columns = measured_entry.reshape(-1).astype(jnp.float32)
    target = patch_ids * capacity + slot_ranks(patch_ids, per_tile)

    def place_rows(field):
        return (
            jnp.zeros((per_tile * capacity,), jnp.float32)
            .at[target]
            .set(field)
            .reshape(groups, per_device * capacity)
        )

    received = side_by_side(
        (place_rows(values), place_rows(weight), place_rows(columns)), "mem", 0, 0, 1
    )

    def arrange(field):
        return (
            field.reshape(groups, per_device, capacity)
            .transpose(1, 0, 2)
            .reshape(per_device, groups * capacity)
        )

    slot_value = arrange(received[0])
    slot_weight = arrange(received[1])
    slot_column = arrange(received[2])
    centre = jnp.mean(ensemble, axis=0)
    deviation = ensemble - centre[None]
    column_ids = slot_column.astype(jnp.int32)
    flat_index = (
        column_ids // PATCH * cells_dev
        + jnp.arange(per_device, dtype=jnp.int32)[:, None] * PATCH
        + column_ids % PATCH
    )
    flat_index = flat_index.reshape(-1)
    flat_dev = deviation.reshape(members, prognostic_number * cells_dev)
    obs_dev = jnp.take(flat_dev, flat_index, axis=1).reshape(members, per_device, -1)
    innovation = slot_value - jnp.take(centre.reshape(-1), flat_index).reshape(per_device, -1)
    weighted = obs_dev * slot_weight[None]
    gram = jnp.einsum("kps,jps->pkj", weighted, obs_dev, precision=HIGH)
    drive = jnp.einsum("kps,ps->pk", weighted, innovation, precision=HIGH)
    coeffs = transforms(gram, drive, members)
    dev_blocks = deviation.reshape(members, prognostic_number, per_device, PATCH)
    mixed = jnp.einsum("pjk,jvpt->kvpt", coeffs, dev_blocks, precision=HIGH)
    analysed = centre.reshape(1, prognostic_number, per_device, PATCH) + mixed
    outgoing = analysed.reshape(groups, ensemble_share, prognostic_number, cells_dev)
    returned = lax.all_to_all(outgoing, "mem", split_axis=0, concat_axis=3, tiled=True)
    return returned.reshape(ensemble_share, prognostic_number, subdomain_lines, eastward_span)


def solution(mesh):
    in_specs = (
        P("mem", None, "dom", None),
        P(),
        P(),
        P("dom", "mem"),
        P("dom", "mem"),
        P("dom", "mem", None),
        P("dom", "mem"),
        P("dom", "mem"),
        P(),
    )
    out_specs = P("mem", None, "dom", None)
    return jax.shard_map(shards, mesh=mesh, in_specs=in_specs, out_specs=out_specs, check_vma=False)
```

profile of v0, /device:TPU:29, one launch (start us, length us, event | category | flops | bytes accessed | tf_op | source)
XLA Modules:
  0.0 336.3 jit_solution(7137485965120842503)
XLA Ops:
  0.0 0.7 fusion.34
  0.7 1.2 reduce-window.6
  1.9 0.2 slice_reduce_fusion
  2.1 0.8 fusion.30
  2.9 0.7 compare_select_fusion.2
  3.6 1.0 fusion.18
  4.6 0.7 mul.134
  5.3 2.4 scatter_custom_fusion.1
  7.8 0.7 convert_element_type.53
  8.5 2.4 scatter_custom_fusion.2
  11.0 2.6 scatter_custom_fusion
  13.7 0.1 pad_maximum_fusion.2
  13.8 0.6 all_to_all.33
  14.4 9.2 %all-to-all-start.1 = ((f32[16,1,192]{2,1,0:T(1,128)}), f32[16,1,192]{2,1,0:T(1,128)S(1)}, u32[]{:S(2)}, u32[]{:S(2)}) async-start(f32[16,1,192]{2,1,0:T(1,128)} %all_to_all.33), calls=%async_computation.1 | async-start | bytes 32768 | tf_op jit(solution)/shard_map/all_to_all | solution.py:29
  23.5 1.1 fusion.59
  24.6 2.4 collective-permute-start
  27.0 5.5 %collective-permute-start.1 = (f32[4,4,1,512]{3,2,1,0:T(1,128)S(1)}, f32[4,4,1,512]{3,2,1,0:T(1,128)S(1)}, u32[]{:S(2)}, u32[]{:S(2)}) collective-permute-start(f32[4,4,1,512]{3,2,1,0:T(1,128)S(1)} %get-tuple-element.8), channel_id=1, source_target_pairs={{0,1},{1,2},{2,3},{3,4},{4,5},{5,6},{6,7},{7,8},{8,9},{9,10},{10,1... | collective-permute-start | bytes 98312 | tf_op jit(solution)/shard_map/ppermute | solution.py:18
  32.5 12.1 %fusion.8 = f32[4,128,512,4]{2,3,1,0:T(4,128)S(1)} fusion(f32[4,4,128,512]{3,2,1,0:T(8,128)} %param.9, f32[4,4]{1,0:T(4,128)S(1)} %copy-done), kind=kOutput, calls=%fused_computation.19 | convolution fusion | flops 50331648 | bytes 8388672 | tf_op jit(solution)/shard_map/vw,kwxy->kvxy/dot_general | solution.py:43
  44.6 5.9 %fusion.5 = f32[4,4,128,512]{3,2,1,0:T(8,128)} fusion(f32[4,4,128,512]{3,2,1,0:T(8,128)S(1)} %copy-done.2, f32[4,4,1,512]{3,2,1,0:T(1,128)S(1)} %collective-permute-done.1, f32[4,4,1,512]{3,2,1,0:T(1,128)S(1)} %collective-permute-done, f32[4,128,512,4]{2,3,1,0:T(4,128)S(1)} %fusion.8, f32[4]{0:T(128)S(1)} %copy-done.3), kind=kLoop, calls=%fused_computation.12 | loop fusion | flops 10485760 | bytes 12648464 | tf_op jit(solution)/shard_map/add | solution.py:44
  50.5 4.9 %reshape.269 = f32[4,4,16,4096]{3,2,1,0:T(8,128)} reshape(f32[4,4,128,512]{3,2,1,0:T(8,128)} %fusion.5) | data formatting | bytes 8388608 | tf_op jit(solution)/shard_map/reshape | solution.py:93
  55.4 6.9 %copy.82 = f32[4,4,16,4096]{3,1,0,2:T(4,128)} copy(f32[4,4,16,4096]{3,2,1,0:T(8,128)} %reshape.269) | data formatting | bytes 8388608 | tf_op jit(solution)/shard_map/reshape | solution.py:93
  62.3 7.8 %all-to-all-start = ((f32[4,4,16,4096]{3,1,0,2:T(4,128)}), f32[4,4,16,4096]{3,1,0,2:T(4,128)}, u32[]{:S(2)}, u32[]{:S(2)}) async-start(f32[4,4,16,4096]{3,1,0,2:T(4,128)} %copy.82), calls=%async_computation | async-start | bytes 8388608 | tf_op jit(solution)/shard_map/all_to_all | solution.py:92
  70.2 0.1 fusion.60
  70.3 0.1 convert_element_type.56
  70.4 0.1 convert_element_type.59
  70.5 0.1 convert_element_type.58
  70.6 0.1 reshape.279
  70.7 0.1 reshape.280
  70.7 0.1 reshape.278
  70.8 0.1 mul.140
  71.0 92.7 %all-to-all-done = f32[4,4,16,4096]{3,1,0,2:T(4,128)} async-done(((f32[4,4,16,4096]{3,1,0,2:T(4,128)}), f32[4,4,16,4096]{3,1,0,2:T(4,128)}, u32[]{:S(2)}, u32[]{:S(2)}) %all-to-all-start) | async-done | bytes 4194336 | tf_op jit(solution)/shard_map/all_to_all | solution.py:92
  163.6 2.6 bitcast_reduce_fusion
  166.3 6.2 %gather_fusion.1 = f32[1024]{0:T(1024)S(1)} fusion(f32[16384]{0:T(1024)S(1)} %bitcast.129, s32[1024]{0:T(1024)S(1)} %broadcast_clamp_fusion), kind=kCustom, calls=%fused_computation.1 | custom fusion | bytes 12288 | tf_op jit(solution)/shard_map/jit(_take)/gather | solution.py:145
  172.5 4.6 %copy.106 = f32[8,8,4,4096]{3,1,2,0:T(8,128)S(1)} copy(f32[8,8,4,4096]{3,2,1,0:T(4,128)} %bitcast.54) | data formatting | bytes 8388608
  177.0 2.3 broadcast_subtract_fusion
  179.4 6.9 %copy.87 = f32[64,16384]{0,1:T(8,128)} copy(f32[64,16384]{1,0:T(8,128)} %broadcast_subtract_fusion) | data formatting | bytes 8388608 | tf_op jit(solution)/shard_map/sub | solution.py:135
  186.3 6.2 %gather_fusion = f32[1024,64]{1,0:T(8,128)S(1)} fusion(f32[64,16384]{0,1:T(8,128)} %copy.87, s32[1024]{0:T(1024)S(1)} %broadcast_clamp_fusion), kind=kCustom, calls=%fused_computation | custom fusion | bytes 528384 | tf_op jit(solution)/shard_map/jit(_take)/gather | solution.py:144
  192.5 0.2 copy.88
  192.6 0.1 subtract_bitcast_fusion
  192.7 0.5 multiply_reduce_fusion
  193.2 0.3 fusion.15
  193.5 0.3 fusion.43
  193.8 0.2 fusion.37
  194.0 0.2 fusion.14
  194.2 0.2 fusion.62
  194.4 0.2 fusion.61
  194.6 0.2 fusion.13
  194.8 0.2 fusion.64
  195.0 0.2 fusion.63
  195.2 0.2 fusion.12
  195.4 0.2 fusion.66
  195.6 0.2 fusion.65
  195.8 0.3 convolution_bitcast_fusion.1
  196.1 0.2 fusion.11
  196.3 0.2 convolution_divide_fusion
  196.5 0.2 convolution_bitcast_fusion
  196.7 0.2 fusion.67
  197.0 7.1 %reshape.270 = f32[64,4,2,2048]{3,2,1,0:T(2,128)} reshape(f32[16,4,4,1,4096]{4,2,1,0,3:T(4,128)} %bitcast.4) | data formatting | bytes 8388608 | tf_op jit(solution)/shard_map/reshape | solution.py:99
  204.1 9.2 %bitcast_add_fusion = f32[64,4,2,2048]{3,0,1,2:T(8,128)S(1)} fusion(f32[64,4,2,2048]{3,2,1,0:T(2,128)} %reshape.270, f32[4,2,2048]{2,0,1:T(4,128)S(1)} %bitcast.134, f32[2,64,64]{2,1,0:T(8,128)S(1)} %convolution_divide_fusion, f32[2,64]{1,0:T(2,128)S(1)} %bitcast.143), kind=kOutput, calls=%fused_computation.16 | convolution fusion | flops 807419904 | bytes 8487424 | tf_op jit(solution)/shard_map/pjk,jvpt->kvpt/dot_general | solution.py:151
  213.3 5.2 %copy.92 = f32[64,4,2,2048]{3,2,1,0:T(2,128)} copy(f32[64,4,2,2048]{3,0,1,2:T(8,128)S(1)} %bitcast_add_fusion) | data formatting | bytes 8388608 | tf_op jit(solution)/shard_map/add | solution.py:152
  218.5 7.1 %reshape.281 = f32[16,4,4,4096]{3,2,1,0:T(4,128)} reshape(f32[64,4,2,2048]{3,2,1,0:T(2,128)} %copy.92) | data formatting | bytes 8388608 | tf_op jit(solution)/shard_map/reshape | solution.py:153
  225.7 101.3 %all_to_all.42 = f32[16,4,4,4096]{3,2,1,0:T(4,128)S(1)} all-to-all(f32[16,4,4,4096]{3,2,1,0:T(4,128)} %reshape.281), channel_id=1, replica_groups=mesh['mem'=16,'dom'=16] {'mem'}, dimensions={0} | all-to-all | bytes 8388608 | tf_op jit(solution)/shard_map/all_to_all | solution.py:154
  327.0 4.4 %copy.93 = f32[1,4,4,16,4096]{4,3,2,1,0:T(8,128)} copy(f32[1,4,4,16,4096]{4,2,1,3,0:T(4,128)S(1)} %bitcast.132) | data formatting | bytes 8388608 | tf_op jit(solution)/shard_map/all_to_all | solution.py:154
  331.4 4.9 %reshape.282 = f32[4,4,128,512]{3,2,1,0:T(8,128)} reshape(f32[1,4,4,16,4096]{4,3,2,1,0:T(8,128)} %copy.93) | data formatting | bytes 8388608 | tf_op jit(solution)/shard_map/reshape | solution.py:155
  (32 shorter events, 0.5 us)
Async XLA Ops:
  0.0 32.5 %copy-start = (f32[4,4]{1,0:T(4,128)S(1)}, f32[4,4]{1,0:T(4,128)}, u32[]{:S(2)}) copy-start(f32[4,4]{1,0:T(4,128)} %param.11) | copy-start | bytes 196
  14.4 47.9 %all-to-all-start.1 = ((f32[16,1,192]{2,1,0:T(1,128)}), f32[16,1,192]{2,1,0:T(1,128)S(1)}, u32[]{:S(2)}, u32[]{:S(2)}) async-start(f32[16,1,192]{2,1,0:T(1,128)} %all_to_all.33), calls=%async_computation.1 | async-start | bytes 32768 | tf_op jit(solution)/shard_map/all_to_all | solution.py:29
  24.6 20.0 %collective-permute-start = (f32[4,4,1,512]{3,2,1,0:T(1,128)S(1)}, f32[4,4,1,512]{3,2,1,0:T(1,128)S(1)}, u32[]{:S(2)}, u32[]{:S(2)}) collective-permute-start(f32[4,4,1,512]{3,2,1,0:T(1,128)S(1)} %get-tuple-element.7), channel_id=1, source_target_pairs={{1,0},{2,1},{3,2},{4,3},{5,4},{6,5},{7,6},{8,7},{9,8},{10,9},{11,1... | collective-permute-start | bytes 98312 | tf_op jit(solution)/shard_map/ppermute | solution.py:21
  27.0 17.6 %copy-start.2 = (f32[4,4,128,512]{3,2,1,0:T(8,128)S(1)}, f32[4,4,128,512]{3,2,1,0:T(8,128)}, u32[]{:S(2)}) copy-start(f32[4,4,128,512]{3,2,1,0:T(8,128)} %param.9) | copy-start | bytes 12582916
  27.0 17.6 %copy-start.3 = (f32[4]{0:T(128)S(1)}, f32[4]{0:T(128)}, u32[]{:S(2)}) copy-start(f32[4]{0:T(128)} %param.10) | copy-start | bytes 52
  27.0 17.6 %collective-permute-start.1 = (f32[4,4,1,512]{3,2,1,0:T(1,128)S(1)}, f32[4,4,1,512]{3,2,1,0:T(1,128)S(1)}, u32[]{:S(2)}, u32[]{:S(2)}) collective-permute-start(f32[4,4,1,512]{3,2,1,0:T(1,128)S(1)} %get-tuple-element.8), channel_id=1, source_target_pairs={{0,1},{1,2},{2,3},{3,4},{4,5},{5,6},{6,7},{7,8},{8,9},{9,10},{10,1... | collective-permute-start | bytes 98312 | tf_op jit(solution)/shard_map/ppermute | solution.py:18
  62.3 101.3 %all-to-all-start = ((f32[4,4,16,4096]{3,1,0,2:T(4,128)}), f32[4,4,16,4096]{3,1,0,2:T(4,128)}, u32[]{:S(2)}, u32[]{:S(2)}) async-start(f32[4,4,16,4096]{3,1,0,2:T(4,128)} %copy.82), calls=%async_computation | async-start | bytes 8388608 | tf_op jit(solution)/shard_map/all_to_all | solution.py:92
  327.0 9.3 %copy-start.1 = (f32[4,4]{1,0:T(4,128)S(1)}, f32[4,4]{1,0:T(4,128)}, u32[]{:S(2)}) copy-start(f32[4,4]{1,0:T(4,128)} %param.11) | copy-start | bytes 196
where the time goes:
time: 337 us; the launch traced here: 336 us
  blocking collectives  101 us (30%)
  waiting for transfers between devices  92.7 us (28%)
  local copies, waits for them, and re-layouts  75 us (22%)
  matrix products  26.3 us (8%)
  starting transfers between devices  24.8 us (7%)
  other arithmetic  15.9 us (5%)
    all_to_all x1, blocking collectives, shards(): lax.all_to_all(outgoing, 'mem', split_axis=0, concat_axis=3, tiled=True)  101 us
    all_to_all x1, waiting for transfers between devices, shards(): lax.all_to_all(advanced_ensemble.reshape(ensemble_share, prognostic_numbe...  92.7 us
    dot_general x1, matrix products, laplacian_update(): jnp.einsum('vw,kwxy->kvxy', tendency_matrix, ensemble, precision=HIGH)  12.1 us
    reshape x2, local copies, waits for them, and re-layouts, shards(): advanced_ensemble.reshape(ensemble_share, prognostic_number, groups, cell...  11.8 us
    dot_general x1, matrix products, shards(): mixed = jnp.einsum('pjk,jvpt->kvpt', coeffs, dev_blocks, precision=HIGH)  9.16 us
    all_to_all x1, starting transfers between devices, side_by_side(): lax.all_to_all(both, axis, split_axis=split_dim, concat_axis=concat_dim,...  9.15 us
    all_to_all x1, starting transfers between devices, shards(): lax.all_to_all(advanced_ensemble.reshape(ensemble_share, prognostic_numbe...  7.79 us
    scatter x3, local copies, waits for them, and re-layouts, place_rows(): return jnp.zeros((per_tile * capacity,), jnp.float32).at[target].set(fiel...  7.48 us
  transfers between devices with their start and end apart: 4, of which 1 were waited for; matrix products, arithmetic and copies ran while one was open for 9% of the time, Pallas kernels for 0%

commit v1 on v0

v1 whole, which is shorter than its diff:
```python
import functools

import jax
import jax.numpy as jnp
from jax import lax
from jax.experimental import pallas as pl
from jax.experimental.pallas import tpu as pltpu
from jax.sharding import PartitionSpec as P


F32 = jnp.float32
BF16 = jnp.bfloat16
HIGH = lax.Precision.HIGHEST
NS_ITERS = 5
CHIPS = 8
SHARE = 4
VARS = 4
LINES = 128
WIDTH = 512
HALF = 32
CAP = 32
OBS = 512
BLOCK = SHARE * VARS * 4 * 8
MB = 1 << 20


def params(mib):
    return pltpu.CompilerParams(vmem_limit_bytes=mib * MB)


def vmem():
    return pl.BlockSpec(memory_space=pltpu.VMEM)


def smem():
    return pl.BlockSpec(memory_space=pltpu.SMEM)


def after():
    return pl.BlockSpec(memory_space=pl.ANY)


def base_row(chunk, chip):
    if chunk == 0:
        return 32 + 8 * chip
    return 8 * chip + jnp.where(chip >= 4, 64, 0)


def stencil_kernel(chunk, place, spread, mix, *refs):
    if chunk == 1:
        _, low, high, x, *outs = refs
    else:
        x, *outs, first, last = refs
        for v in range(VARS):
            first[0, v] = x[0, v, 0:1, :]
            last[0, v] = x[0, v, LINES - 1 : LINES, :]
    chip, core = place[0], place[1]
    row = lax.broadcasted_iota(jnp.int32, (8, WIDTH), 0)
    lane = lax.broadcasted_iota(jnp.int32, (8, WIDTH), 1)
    for d in range(CHIPS):
        target = lax.rem(chip + d, CHIPS)
        base = pl.multiple_of(base_row(chunk, target), 8)
        if chunk == 0:
            before = pl.multiple_of(base - 8, 8)
            behind = pl.multiple_of(base + 8, 8)
        else:
            before = pl.multiple_of(jnp.maximum(base - 8, 0), 8)
            behind = pl.multiple_of(jnp.minimum(base + 8, LINES - 8), 8)
        tiles = [x[0, v, pl.ds(base, 8), :] for v in range(VARS)]
        for v in range(VARS):
            t = tiles[v]
            prev = pltpu.roll(x[0, v, pl.ds(before, 8), :], 1, 0)
            nxt = pltpu.roll(x[0, v, pl.ds(behind, 8), :], 7, 0)
            if chunk == 1:
                prev = jnp.where(base == 0, jnp.broadcast_to(low[0, v], (8, WIDTH)), prev)
                nxt = jnp.where(base == LINES - 8, jnp.broadcast_to(high[0, v], (8, WIDTH)), nxt)
            up = jnp.where(row == 0, prev, pltpu.roll(t, 1, 0))
            down = jnp.where(row == 7, nxt, pltpu.roll(t, 7, 0))
            left = jnp.where(lane == 0, 0.0, pltpu.roll(t, 1, 1))
            right = jnp.where(lane == WIDTH - 1, 0.0, pltpu.roll(t, WIDTH - 1, 1))
            laplace = down + up + right + left - 4.0 * t
            mixing = mix[v, 0] * tiles[0]
            for w in range(1, VARS):
                mixing = mixing + mix[v, w] * tiles[w]
            res = t + spread[v] * laplace + mixing
            res = jnp.where(core == 1, pltpu.roll(res, 4, 0), res)
            for q in range(4):
                outs[d][pl.ds((v * 4 + q) * 8, 8), :] = res[:, q * 128 : (q + 1) * 128]


def stencil(chunk, place, spread, mix, x, extra):
    per = BLOCK // SHARE
    halo_spec = pl.BlockSpec((1, VARS, 1, WIDTH), lambda m: (m, 0, 0, 0))
    out_specs = [pl.BlockSpec((per, 128), lambda m: (m, 0))] * CHIPS
    out_shape = [jax.ShapeDtypeStruct((BLOCK, 128), F32)] * CHIPS
    extra_specs = [after(), halo_spec, halo_spec]
    if chunk == 0:
        out_specs += [halo_spec] * 2
        out_shape += [jax.ShapeDtypeStruct((SHARE, VARS, 1, WIDTH), F32)] * 2
        extra_specs = []
    return pl.pallas_call(
        functools.partial(stencil_kernel, chunk),
        grid=(SHARE,),
        in_specs=[smem(), smem(), smem()]
        + extra_specs
        + [pl.BlockSpec((1, VARS, LINES, WIDTH), lambda m: (m, 0, 0, 0))],
        out_specs=out_specs,
        out_shape=out_shape,
        compiler_params=params(16),
        cost_estimate=pl.CostEstimate(flops=20_000_000, bytes_accessed=6 * MB, transcendentals=0),
    )(place, spread, mix, *extra, x)


def parts3(x):
    a = x.astype(BF16)
    r = x - a.astype(F32)
    b = r.astype(BF16)
    c = (r - b.astype(F32)).astype(BF16)
    return a, b, c


def nt(a, b):
    return lax.dot_general(a, b, (((1,), (1,)), ((), ())), preferred_element_type=F32)


def obs_kernel(_, pid, tidx, entry, value, inv, table, out):
    ids = pid[...]
    sub = lax.broadcasted_iota(jnp.int32, (32, OBS), 0)
    named = sub == jnp.broadcast_to(ids, (32, OBS))
    onehot = jnp.where(named, 1.0, 0.0)
    earlier = jnp.where(
        lax.broadcasted_iota(jnp.int32, (OBS, OBS), 0) < lax.broadcasted_iota(jnp.int32, (OBS, OBS), 1),
        1.0, 0.0,
    ).astype(BF16)
    before = jnp.dot(onehot.astype(BF16), earlier, preferred_element_type=F32)
    rank = jnp.sum(before * onehot, axis=0, keepdims=True).astype(jnp.int32)
    inner = (ids >= 8) & (ids < 24)
    group = jnp.where(inner, 2 * (ids - 8), jnp.where(ids < 8, 2 * ids + 1, 2 * (ids - 16) + 1))
    target = group * CAP + rank
    levels = table.shape[1]
    look = jnp.where(
        lax.broadcasted_iota(jnp.int32, (levels, OBS), 0) == jnp.broadcast_to(tidx[...], (levels, OBS)),
        1.0, 0.0,
    ).astype(BF16)
    taper = sum(
        jnp.dot(jnp.broadcast_to(p, (16, levels)), look, preferred_element_type=F32)
        for p in parts3(table[...])
    )
    weight = inv[...] * taper[0:1]
    c = entry[...]
    place = (c & 0x1800) | ((c & 0x180) << 2) | ((c & 0x600) >> 2) | (c & 0x7F)
    r8 = lax.broadcasted_iota(jnp.int32, (16, OBS), 0)
    fields = jnp.where(
        r8 == 0, jnp.broadcast_to(value[...], (16, OBS)),
        jnp.where(r8 == 1, jnp.broadcast_to(weight, (16, OBS)),
                  jnp.where(r8 == 2, jnp.broadcast_to(place.astype(F32), (16, OBS)), 0.0)),
    )
    pieces = parts3(fields)
    for k in range(2):
        slots = jnp.where(
            lax.broadcasted_iota(jnp.int32, (OBS, OBS), 0) + k * OBS == jnp.broadcast_to(target, (OBS, OBS)),
            1.0, 0.0,
        ).astype(BF16)
        placed = nt(pieces[0], slots) + nt(pieces[1], slots) + nt(pieces[2], slots)
        out[:, pl.ds(k * OBS, OBS)] = placed[0:8]


def place_obs(behind, pid, tidx, entry, value, inv, table):
    return pl.pallas_call(
        obs_kernel,
        in_specs=[after()] + [vmem()] * 6,
        out_specs=vmem(),
        out_shape=jax.ShapeDtypeStruct((8, 2 * OBS), F32),
        compiler_params=params(16),
        cost_estimate=pl.CostEstimate(flops=20_000_000, bytes_accessed=MB, transcendentals=0),
        name="place_obs",
    )(behind, pid, tidx, entry, value, inv, table)


def gather_members_kernel(_, *refs):
    blocks, (keep, send) = refs[:CHIPS], refs[CHIPS:]
    for g in range(64):
        vl, r = g // 4, g % 4
        for d in range(CHIPS):
            keep[g, pl.ds(SHARE * d, SHARE), :] = blocks[d][pl.ds(vl * 8 + r, SHARE, stride=128), :]
            send[g, pl.ds(SHARE * d, SHARE), :] = blocks[d][pl.ds(vl * 8 + 4 + r, SHARE, stride=128), :]


def gather_members(behind, blocks):
    half = jax.ShapeDtypeStruct((64, HALF, 128), F32)
    return pl.pallas_call(
        gather_members_kernel,
        in_specs=[after()] + [vmem()] * CHIPS,
        out_specs=[vmem()] * 2,
        out_shape=[half] * 2,
        compiler_params=params(16),
        cost_estimate=pl.CostEstimate(flops=20_000_000, bytes_accessed=4 * MB, transcendentals=0),
    )(behind, *blocks)


def spread_members_kernel(keep, came, *outs):
    for d in range(CHIPS):
        for m in range(SHARE):
            for vl in range(16):
                at = (m * 16 + vl) * 8
                start = vl * 128 + d * SHARE + m
                outs[d][pl.ds(at, 4), :] = keep[pl.ds(start, 4, stride=HALF), :]
                outs[d][pl.ds(at + 4, 4), :] = came[pl.ds(start, 4, stride=HALF), :]


def spread_members(keep, came):
    return pl.pallas_call(
        spread_members_kernel,
        in_specs=[vmem()] * 2,
        out_specs=[vmem()] * CHIPS,
        out_shape=[jax.ShapeDtypeStruct((BLOCK, 128), F32)] * CHIPS,
        compiler_params=params(16),
        cost_estimate=pl.CostEstimate(flops=20_000_000, bytes_accessed=4 * MB, transcendentals=0),
    )(keep.reshape(64 * HALF, 128), came.reshape(64 * HALF, 128))


def high(a, b):
    return jnp.dot(a, b, precision=HIGH, preferred_element_type=F32)


def analysis_kernel(keep, came, obs, out_keep, out_send, parts, centres, acc):
    members = 2 * HALF
    acc[...] = jnp.zeros_like(acc)
    cell = lax.broadcasted_iota(jnp.int32, (256, OBS), 0)
    where_obs = obs[2:3, :].astype(jnp.int32)

    def select(t, _):
        g = 2 * t
        cols = [jnp.concatenate([keep[g + h], came[g + h]], axis=0) for h in range(2)]
        block = jnp.concatenate(cols, axis=1)
        centre = jnp.sum(block, axis=0, keepdims=True) * (1.0 / members)
        dev = block - centre
        hi = dev.astype(BF16)
        lo = (dev - hi.astype(F32)).astype(BF16)
        c1 = centre.astype(BF16)
        rest = centre - c1.astype(F32)
        c2 = rest.astype(BF16)
        c3 = rest - c2.astype(F32)
        row = lax.broadcasted_iota(jnp.int32, (16, 256), 0)
        crows = jnp.where(
            row == 0, jnp.broadcast_to(c1.astype(F32), (16, 256)),
            jnp.where(row == 1, jnp.broadcast_to(c2.astype(F32), (16, 256)),
                      jnp.where(row == 2, jnp.broadcast_to(c3, (16, 256)), 0.0)),
        ).astype(BF16)
        both = jnp.concatenate([hi, lo], axis=0)
        parts[t] = both
        centres[t] = jnp.broadcast_to(centre, (8, 256))
        chosen = jnp.where(cell == jnp.broadcast_to(where_obs - t * 256, (256, OBS)), 1.0, 0.0).astype(BF16)
        acc[...] += jnp.dot(jnp.concatenate([both, crows], axis=0), chosen, preferred_element_type=F32)
        return 0

    lax.fori_loop(0, 32, select, 0)
    columns = acc[0:members] + acc[members : 2 * members]
    centre_obs = acc[128:129] + acc[129:130] + acc[130:131]
    innovation = obs[0:1, :] - centre_obs
    weight = obs[1:2, :]
    weighted = columns * weight
    pair = (((1,), (1,)), ((), ()))
    gram = lax.dot_general(weighted, columns, pair, precision=HIGH, preferred_element_type=F32)
    drive = lax.dot_general(
        jnp.broadcast_to(weight * innovation, (8, OBS)), columns, pair, precision=HIGH, preferred_element_type=F32
    )
    eye = jnp.where(
        lax.broadcasted_iota(jnp.int32, (members, members), 0) == lax.broadcasted_iota(jnp.int32, (members, members), 1),
        1.0, 0.0,
    )
    system = (members - 1.0) * eye + gram
    norm = jnp.sqrt(jnp.sum(jnp.sum(system * system, axis=1, keepdims=True), axis=0, keepdims=True))
    y = system / norm
    z = 1.5 * eye - 0.5 * y
    y = high(y, z)
    for sweep in range(1, NS_ITERS):
        mid = 1.5 * eye - 0.5 * high(z, y)
        if sweep < NS_ITERS - 1:
            y = high(y, mid)
        z = high(mid, z)
    root = z / jnp.sqrt(norm)
    offset = high(high(drive, root), root)
    coeff = offset[0:1, :] + jnp.sqrt(members - 1.0) * root
    spread = jnp.where(
        lax.broadcasted_iota(jnp.int32, (members, 256), 0)
        == (lax.broadcasted_iota(jnp.int32, (members, 256), 1) & (members - 1)),
        1.0, 0.0,
    )
    four = high(coeff, spread)
    four_hi = four.astype(BF16)
    four_lo = four - four_hi.astype(F32)
    lanes = lax.broadcasted_iota(jnp.int32, (members, 256), 1)
    left = jnp.where(lanes < 128, four_hi.astype(F32), four_lo).astype(BF16)

    def transform(t, _):
        g = 2 * t
        both = parts[t]
        res = jnp.dot(left, jnp.concatenate([both, both], axis=0), preferred_element_type=F32)
        res = res + jnp.broadcast_to(centres[t][0:1], (members, 256))
        for h in range(2):
            out_keep[g + h] = res[0:HALF, h * 128 : (h + 1) * 128]
            out_send[g + h] = res[HALF:members, h * 128 : (h + 1) * 128]
        return 0

    lax.fori_loop(0, 32, transform, 0)


def analysis(keep, came, obs):
    half = jax.ShapeDtypeStruct((64, HALF, 128), F32)
    return pl.pallas_call(
        analysis_kernel,
        in_specs=[vmem()] * 3,
        out_specs=[vmem()] * 2,
        out_shape=[half] * 2,
        scratch_shapes=[
            pltpu.VMEM((32, 128, 256), BF16),
            pltpu.VMEM((32, 8, 256), F32),
            pltpu.VMEM((144, OBS), F32),
        ],
        compiler_params=params(24),
        cost_estimate=pl.CostEstimate(flops=100_000_000, bytes_accessed=4 * MB, transcendentals=0),
    )(keep, came, obs)


def grid_kernel(place, *refs):
    blocks, out = refs[:-1], refs[-1]
    chip, core = place[0], place[1]
    for chunk in range(2):
        for d in range(CHIPS):
            base = pl.multiple_of(base_row(chunk, lax.rem(chip + d, CHIPS)), 8)
            src = blocks[chunk * CHIPS + d]
            for v in range(VARS):
                for q in range(4):
                    val = src[pl.ds((v * 4 + q) * 8, 8), :]
                    val = jnp.where(core == 1, pltpu.roll(val, 4, 0), val)
                    out[0, v, pl.ds(base, 8), q * 128 : (q + 1) * 128] = val


def to_grid(place, blocks):
    per = BLOCK // SHARE
    return pl.pallas_call(
        grid_kernel,
        grid=(SHARE,),
        in_specs=[smem()] + [pl.BlockSpec((per, 128), lambda m: (m, 0))] * (2 * CHIPS),
        out_specs=pl.BlockSpec((1, VARS, LINES, WIDTH), lambda m: (m, 0, 0, 0)),
        out_shape=jax.ShapeDtypeStruct((SHARE, VARS, LINES, WIDTH), F32),
        compiler_params=params(16),
        cost_estimate=pl.CostEstimate(flops=5_000_000, bytes_accessed=8 * MB, transcendentals=0),
        name="to_grid",
    )(place, *blocks)


def hop(block, d):
    n = 2 * CHIPS
    return lax.ppermute(block, "mem", [(i, (i + 2 * d) % n) for i in range(n)])


ORDER = (4, 3, 5, 2, 6, 1, 7)


def exchange(blocks, sign):
    got = list(blocks)
    for d in ORDER:
        got[d] = hop(blocks[d], sign * d)
    return got


def swap(x):
    return lax.ppermute(x, "mem", [(i, i ^ 1) for i in range(2 * CHIPS)])


def shards(
    prior_ensemble,
    spreading_factor,
    tendency_matrix,
    measured_data,
    inverse_error,
    assigned_subregion,
    measured_entry,
    taper_index,
    taper_factors,
):
    me = lax.axis_index("mem")
    place = jnp.stack([me // 2, me % 2]).astype(jnp.int32)
    x = prior_ensemble

    *sent_a, first, last = stencil(0, place, spreading_factor, tendency_matrix, x, ())
    got_a = exchange(sent_a, 1)

    placed = place_obs(
        sent_a[0], assigned_subregion.reshape(1, OBS), taper_index, measured_entry, measured_data,
        inverse_error, taper_factors.reshape(1, -1),
    )
    outgoing = placed[0:3].reshape(3, 16, 64).transpose(1, 0, 2).reshape(16, 192)
    incoming = lax.all_to_all(outgoing, "mem", split_axis=0, concat_axis=0, tiled=True)
    slots = incoming.reshape(16, 3, 2, CAP).transpose(2, 1, 0, 3).reshape(2, 3, OBS)
    slots = jnp.pad(slots, ((0, 0), (0, 5), (0, 0)))

    count = lax.axis_size("dom")
    forward = [(i, i + 1) for i in range(count - 1)]
    backward = [(b, a) for a, b in forward]
    low = lax.ppermute(last, "dom", forward)
    high_row = lax.ppermute(first, "dom", backward)
    sent_b = stencil(1, place, spreading_factor, tendency_matrix, x, (placed, low, high_row))
    got_b = exchange(sent_b, 1)

    back = []
    behind = sent_b[0]
    for chunk, got in enumerate((got_a, got_b)):
        keep, send = gather_members(behind, got)
        came = swap(send)
        out_keep, out_send = analysis(keep, came, slots[chunk])
        returned = swap(out_send)
        outs = spread_members(out_keep, returned)
        back.extend(exchange(outs, -1))
        behind = outs[0]
    return to_grid(place, back)


def solution(mesh):
    in_specs = (
        P("mem", None, "dom", None),
        P(),
        P(),
        P("dom", "mem"),
        P("dom", "mem"),
        P("dom", "mem", None),
        P("dom", "mem"),
        P("dom", "mem"),
        P(),
    )
    out_specs = P("mem", None, "dom", None)

    return jax.shard_map(shards, mesh=mesh, in_specs=in_specs, out_specs=out_specs, check_vma=False)
```

time: 337 us -> 278 us (0.82)
  blocking collectives: 101 us -> 12.7 us
  local copies, waits for them, and re-layouts: 75 us -> 6.74 us
  waiting for transfers between devices: 92.7 us -> 144 us
  Pallas kernels: 0 us -> 43.9 us
  starting transfers between devices: 24.8 us -> 67.8 us
  matrix products: 26.3 us -> 0 us
  other arithmetic: 15.9 us -> 0.12 us
    ppermute x2 -> x34, waiting for transfers between devices: 0.01 us -> 144 us  [the longest x28 142 us: hop(): return lax.ppermute(block, 'mem', [(i, (i + 2 * d) % n) for i in range(n)])]
    all_to_all x2 -> x0, waiting for transfers between devices: 92.7 us -> none  [the longest x1 92.7 us: shards(): lax.all_to_all(advanced_ensemble.reshape(ensemble_share, prognostic_numbe...]
    all_to_all x1, blocking collectives: 101 us -> 12.7 us  [shards(): lax.all_to_all(outgoing, 'mem', split_axis=0, concat_axis=0, tiled=True)]
    ppermute x2 -> x34, starting transfers between devices: 7.84 us -> 67.8 us  [the longest x28 58.5 us: hop(): return lax.ppermute(block, 'mem', [(i, (i + 2 * d) % n) for i in range(n)])]
    pallas_call x0 -> x10, Pallas kernels: none -> 43.9 us  [the longest x2 27.9 us: analysis(): pl.pallas_call(analysis_kernel, in_specs=[vmem()] * 3, out_specs=[vmem()]...]
    reshape x11 -> x5, local copies, waits for them, and re-layouts: 31.5 us -> 0.29 us  [the longest x3 0.19 us: shards(): incoming.reshape(16, 3, 2, CAP).transpose(2, 1, 0, 3).reshape(2, 3, OBS)]
    dot_general x21 -> x0, matrix products: 26.3 us -> none  [the longest x1 12.1 us: laplacian_update(): jnp.einsum('vw,kwxy->kvxy', tendency_matrix, ensemble, precision=HIGH)]
    all_to_all x2 -> x0, starting transfers between devices: 16.9 us -> none  [the longest x1 9.15 us: side_by_side(): lax.all_to_all(both, axis, split_axis=split_dim, concat_axis=concat_dim,...]
  transfers between devices with their start and end apart: 4 -> 34, of which waited for: 1 -> 20; matrix products, arithmetic and copies ran while one was open for 9% -> 0% of each run, Pallas kernels for 0% -> 3%
where the time goes in v1:
time: 278 us; the launch traced here: 276 us
  waiting for transfers between devices  144 us (52%)
  starting transfers between devices  67.8 us (24%)
  Pallas kernels  43.9 us (16%)
  blocking collectives  12.7 us (5%)
  local copies, waits for them, and re-layouts  6.74 us (2%)
    ppermute x28, waiting for transfers between devices, hop(): return lax.ppermute(block, 'mem', [(i, (i + 2 * d) % n) for i in range(n)])  142 us
    ppermute x28, starting transfers between devices, hop(): return lax.ppermute(block, 'mem', [(i, (i + 2 * d) % n) for i in range(n)])  58.5 us
    pallas_call x2, Pallas kernels, analysis(): pl.pallas_call(analysis_kernel, in_specs=[vmem()] * 3, out_specs=[vmem()]...  27.9 us
    all_to_all x1, blocking collectives, shards(): lax.all_to_all(outgoing, 'mem', split_axis=0, concat_axis=0, tiled=True)  12.7 us
    unnamed x34, local copies, waits for them, and re-layouts  6.35 us
  transfers between devices with their start and end apart: 34, of which 20 were waited for; matrix products, arithmetic and copies ran while one was open for 0% of the time, Pallas kernels for 3%

profile of v1, /device:TPU:29, one launch (start us, length us, event | category | flops | bytes accessed | tf_op | source)
XLA Modules:
  0.0 275.9 jit_solution(16621683414007895872)
XLA Ops:
  0.1 2.2 copy-done
  2.3 0.7 copy-done.2
  3.0 0.7 copy-done.8
  3.7 2.6 shard_map.91
  6.3 1.7 collective-permute-start.2
  8.0 3.0 %collective-permute-start.3 = (f32[512,128]{1,0:T(8,128)S(1)}, f32[512,128]{1,0:T(8,128)S(1)}, u32[]{:S(2)}, u32[]{:S(2)}) collective-permute-start(f32[512,128]{1,0:T(8,128)S(1)} %get-tuple-element.52), channel_id=1, source_target_pairs={{0,64},{16,80},{32,96},{48,112},{64,128},{80,144},{96,160},{112,17... | collective-permute-start | bytes 786440 | tf_op jit(solution)/shard_map/ppermute | solution.py:356
  11.0 2.5 collective-permute-start
  13.4 2.8 %collective-permute-start.1 = (f32[4,4,1,512]{3,2,1,0:T(1,128)S(1)}, f32[4,4,1,512]{3,2,1,0:T(1,128)S(1)}, u32[]{:S(2)}, u32[]{:S(2)}) collective-permute-start(f32[4,4,1,512]{3,2,1,0:T(1,128)S(1)} %get-tuple-element.49), channel_id=1, source_target_pairs={{1,0},{2,1},{3,2},{4,3},{5,4},{6,5},{7,6},{8,7},{9,8},{10,9},{11,1... | collective-permute-start | bytes 98312 | tf_op jit(solution)/shard_map/ppermute | solution.py:404
  16.3 3.8 %collective-permute-start.4 = (f32[512,128]{1,0:T(8,128)S(1)}, f32[512,128]{1,0:T(8,128)S(1)}, u32[]{:S(2)}, u32[]{:S(2)}) collective-permute-start(f32[512,128]{1,0:T(8,128)S(1)} %get-tuple-element.53), channel_id=1, source_target_pairs={{0,96},{16,112},{32,128},{48,144},{64,160},{80,176},{96,192},{112,... | collective-permute-start | bytes 786440 | tf_op jit(solution)/shard_map/ppermute | solution.py:356
  20.1 0.6 collective-permute-start.5
  20.7 4.4 %collective-permute-start.6 = (f32[512,128]{1,0:T(8,128)S(1)}, f32[512,128]{1,0:T(8,128)S(1)}, u32[]{:S(2)}, u32[]{:S(2)}) collective-permute-start(f32[512,128]{1,0:T(8,128)S(1)} %get-tuple-element.55), channel_id=1, source_target_pairs={{0,160},{16,176},{32,192},{48,208},{64,224},{80,240},{96,0},{112,1... | collective-permute-start | bytes 786440 | tf_op jit(solution)/shard_map/ppermute | solution.py:356
  25.0 2.4 collective-permute-start.7
  27.4 4.2 %collective-permute-start.8 = (f32[512,128]{1,0:T(8,128)S(1)}, f32[512,128]{1,0:T(8,128)S(1)}, u32[]{:S(2)}, u32[]{:S(2)}) collective-permute-start(f32[512,128]{1,0:T(8,128)S(1)} %get-tuple-element.57), channel_id=1, source_target_pairs={{0,224},{16,240},{32,0},{48,16},{64,32},{80,48},{96,64},{112,80},{... | collective-permute-start | bytes 786440 | tf_op jit(solution)/shard_map/ppermute | solution.py:356
  31.6 1.2 place_obs.1.refs_0_
  32.8 2.8 %shard_map.92 = (f32[512,128]{1,0:T(8,128)S(1)}, f32[512,128]{1,0:T(8,128)S(1)}, f32[512,128]{1,0:T(8,128)S(1)}, f32[512,128]{1,0:T(8,128)S(1)}, f32[512,128]{1,...) custom-call(s32[2]{0:T(128)S(1)} %pad_add_fusion.place, f32[4]{0:T(128)S(1)} %copy-done.8, ...), custom_call_target="tpu_custom_call" | custom-call | flops 20000000 | bytes 6291456 | tf_op jit(solution)/shard_map/pallas_call | solution.py:101
  35.7 0.7 copy-done.13
  36.3 0.7 copy-done.14
  37.0 0.7 copy-done.15
  37.7 0.7 copy-done.16
  38.5 7.8 %collective-permute-done.4.refs_3_ = f32[512,128]{1,0:T(8,128)S(1)} collective-permute-done((f32[512,128]{1,0:T(8,128)S(1)}, f32[512,128]{1,0:T(8,128)S(1)}, u32[]{:S(2)}, u32[]{:S(2)}) %collective-permute-start.4) | collective-permute-done | bytes 262176 | tf_op jit(solution)/shard_map/ppermute | solution.py:356
  46.3 5.1 %collective-permute-done.5.refs_4_ = f32[512,128]{1,0:T(8,128)S(1)} collective-permute-done((f32[512,128]{1,0:T(8,128)S(1)}, f32[512,128]{1,0:T(8,128)S(1)}, u32[]{:S(2)}, u32[]{:S(2)}) %collective-permute-start.5) | collective-permute-done | bytes 262176 | tf_op jit(solution)/shard_map/ppermute | solution.py:356
  51.3 1.1 collective-permute-done.6.refs_5_
  52.4 12.0 %collective-permute-done.7.refs_6_ = f32[512,128]{1,0:T(8,128)S(1)} collective-permute-done((f32[512,128]{1,0:T(8,128)S(1)}, f32[512,128]{1,0:T(8,128)S(1)}, u32[]{:S(2)}, u32[]{:S(2)}) %collective-permute-start.7) | collective-permute-done | bytes 262176 | tf_op jit(solution)/shard_map/ppermute | solution.py:356
  64.4 2.7 collective-permute-done.8.refs_7_
  67.1 1.4 shard_map.93
  68.5 1.6 collective-permute-start.9
  70.3 12.7 %all_to_all.10 = f32[16,1,192]{2,1,0:T(1,128)S(1)} all-to-all(f32[16,1,192]{2,1,0:T(1,128)S(1)} %all_to_all.8), channel_id=1, replica_groups=mesh['mem'=16,'dom'=16] {'mem'}, dimensions={0} | all-to-all | bytes 24576 | tf_op jit(solution)/shard_map/all_to_all | solution.py:396
  83.3 14.0 %shard_map.94 = (f32[64,32,128]{2,1,0:T(8,128)S(1)}, f32[64,32,128]{2,1,0:T(8,128)S(1)}) custom-call(f32[64,32,128]{2,1,0:T(8,128)S(1)} %get-tuple-element.58.keep, f32[64,32,128]{2,1,0:T(8,128)S(1)} %collective-permute-done.9.came, f32[8,512]{1,0:T(8,128)S(1)} %get-tuple-element.90.obs), custom_call_target="tpu_custom_call" | custom-call | flops 100000000 | bytes 4194304 | tf_op jit(solution)/shard_map/pallas_call | solution.py:311
  97.2 0.4 collective-permute-start.10
  97.9 0.3 collective-permute-start.19
  98.3 2.1 collective-permute-start.20
  100.3 3.3 %collective-permute-start.21 = (f32[512,128]{1,0:T(8,128)}, f32[512,128]{1,0:T(8,128)S(1)}, u32[]{:S(2)}, u32[]{:S(2)}) collective-permute-start(f32[512,128]{1,0:T(8,128)} %copy-done.13), channel_id=1, source_target_pairs={{0,128},{16,144},{32,160},{48,176},{64,192},{80,208},{96,224},{112... | collective-permute-start | bytes 786440 | tf_op jit(solution)/shard_map/ppermute | solution.py:356
  103.6 3.7 %collective-permute-done.18.refs_1_ = f32[512,128]{1,0:T(8,128)S(1)} collective-permute-done((f32[512,128]{1,0:T(8,128)}, f32[512,128]{1,0:T(8,128)S(1)}, u32[]{:S(2)}, u32[]{:S(2)}) %collective-permute-start.18) | collective-permute-done | bytes 262176 | tf_op jit(solution)/shard_map/ppermute | solution.py:356
  107.3 5.7 %collective-permute-done.19.refs_2_ = f32[512,128]{1,0:T(8,128)S(1)} collective-permute-done((f32[512,128]{1,0:T(8,128)}, f32[512,128]{1,0:T(8,128)S(1)}, u32[]{:S(2)}, u32[]{:S(2)}) %collective-permute-start.19) | collective-permute-done | bytes 262176 | tf_op jit(solution)/shard_map/ppermute | solution.py:356
  113.3 6.1 %collective-permute-start.24 = (f32[512,128]{1,0:T(8,128)}, f32[512,128]{1,0:T(8,128)S(1)}, u32[]{:S(2)}, u32[]{:S(2)}) collective-permute-start(f32[512,128]{1,0:T(8,128)} %copy-done.10), channel_id=1, source_target_pairs={{0,224},{16,240},{32,0},{48,16},{64,32},{80,48},{96,64},{112,80},{... | collective-permute-start | bytes 786440 | tf_op jit(solution)/shard_map/ppermute | solution.py:356
  119.5 1.8 shard_map.95
  121.2 12.5 %collective-permute-done.20.refs_3_ = f32[512,128]{1,0:T(8,128)S(1)} collective-permute-done((f32[512,128]{1,0:T(8,128)}, f32[512,128]{1,0:T(8,128)S(1)}, u32[]{:S(2)}, u32[]{:S(2)}) %collective-permute-start.20) | collective-permute-done | bytes 262176 | tf_op jit(solution)/shard_map/ppermute | solution.py:356
  133.7 6.3 %collective-permute-done.21.refs_4_ = f32[512,128]{1,0:T(8,128)S(1)} collective-permute-done((f32[512,128]{1,0:T(8,128)}, f32[512,128]{1,0:T(8,128)S(1)}, u32[]{:S(2)}, u32[]{:S(2)}) %collective-permute-start.21) | collective-permute-done | bytes 262176 | tf_op jit(solution)/shard_map/ppermute | solution.py:356
  140.0 5.6 %collective-permute-done.23.refs_6_ = f32[512,128]{1,0:T(8,128)S(1)} collective-permute-done((f32[512,128]{1,0:T(8,128)}, f32[512,128]{1,0:T(8,128)S(1)}, u32[]{:S(2)}, u32[]{:S(2)}) %collective-permute-start.23) | collective-permute-done | bytes 262176 | tf_op jit(solution)/shard_map/ppermute | solution.py:356
  145.6 3.8 %collective-permute-done.24.refs_7_ = f32[512,128]{1,0:T(8,128)S(1)} collective-permute-done((f32[512,128]{1,0:T(8,128)}, f32[512,128]{1,0:T(8,128)S(1)}, u32[]{:S(2)}, u32[]{:S(2)}) %collective-permute-start.24) | collective-permute-done | bytes 262176 | tf_op jit(solution)/shard_map/ppermute | solution.py:356
  149.4 1.4 shard_map.96
  150.7 1.5 collective-permute-start.25
  152.3 2.3 collective-permute-done.25.came
  154.5 14.0 %shard_map.97 = (f32[64,32,128]{2,1,0:T(8,128)S(1)}, f32[64,32,128]{2,1,0:T(8,128)S(1)}) custom-call(f32[64,32,128]{2,1,0:T(8,128)S(1)} %get-tuple-element.77.keep, f32[64,32,128]{2,1,0:T(8,128)S(1)} %collective-permute-done.25.came, f32[8,512]{1,0:T(8,128)S(1)} %get-tuple-element.89.obs), custom_call_target="tpu_custom_call" | custom-call | flops 100000000 | bytes 4194304 | tf_op jit(solution)/shard_map/pallas_call | solution.py:311
  168.5 0.4 collective-permute-start.26
  168.9 2.3 collective-permute-start.11
  171.3 2.0 collective-permute-start.12
  173.3 0.9 collective-permute-start.13
  174.1 3.6 %collective-permute-start.14 = (f32[512,128]{1,0:T(8,128)S(1)}, f32[512,128]{1,0:T(8,128)S(1)}, u32[]{:S(2)}, u32[]{:S(2)}) collective-permute-start(f32[512,128]{1,0:T(8,128)S(1)} %get-tuple-element.66), channel_id=1, source_target_pairs={{0,128},{16,144},{32,160},{48,176},{64,192},{80,208},{96,224},{112... | collective-permute-start | bytes 786440 | tf_op jit(solution)/shard_map/ppermute | solution.py:356
  177.8 1.8 shard_map.98
  179.6 3.2 %collective-permute-start.16 = (f32[512,128]{1,0:T(8,128)S(1)}, f32[512,128]{1,0:T(8,128)S(1)}, u32[]{:S(2)}, u32[]{:S(2)}) collective-permute-start(f32[512,128]{1,0:T(8,128)S(1)} %get-tuple-element.68), channel_id=1, source_target_pairs={{0,64},{16,80},{32,96},{48,112},{64,128},{80,144},{96,160},{112,17... | collective-permute-start | bytes 786440 | tf_op jit(solution)/shard_map/ppermute | solution.py:356
  182.9 8.3 %collective-permute-done.12.refs_2_ = f32[512,128]{1,0:T(8,128)S(1)} collective-permute-done((f32[512,128]{1,0:T(8,128)S(1)}, f32[512,128]{1,0:T(8,128)S(1)}, u32[]{:S(2)}, u32[]{:S(2)}) %collective-permute-start.12) | collective-permute-done | bytes 262176 | tf_op jit(solution)/shard_map/ppermute | solution.py:356
  191.2 24.8 %collective-permute-done.13.refs_3_ = f32[512,128]{1,0:T(8,128)S(1)} collective-permute-done((f32[512,128]{1,0:T(8,128)S(1)}, f32[512,128]{1,0:T(8,128)S(1)}, u32[]{:S(2)}, u32[]{:S(2)}) %collective-permute-start.13) | collective-permute-done | bytes 262176 | tf_op jit(solution)/shard_map/ppermute | solution.py:356
  216.0 5.6 %collective-permute-start.28 = (f32[512,128]{1,0:T(8,128)S(1)}, f32[512,128]{1,0:T(8,128)S(1)}, u32[]{:S(2)}, u32[]{:S(2)}) collective-permute-start(f32[512,128]{1,0:T(8,128)S(1)} %get-tuple-element.83), channel_id=1, source_target_pairs={{0,192},{16,208},{32,224},{48,240},{64,0},{80,16},{96,32},{112,48}... | collective-permute-start | bytes 786440 | tf_op jit(solution)/shard_map/ppermute | solution.py:356
  221.6 2.6 collective-permute-start.30
  224.2 0.5 collective-permute-done.17.refs_7_
  225.0 3.3 %collective-permute-start.32 = (f32[512,128]{1,0:T(8,128)S(1)}, f32[512,128]{1,0:T(8,128)S(1)}, u32[]{:S(2)}, u32[]{:S(2)}) collective-permute-start(f32[512,128]{1,0:T(8,128)S(1)} %get-tuple-element.87), channel_id=1, source_target_pairs={{0,64},{16,80},{32,96},{48,112},{64,128},{80,144},{96,160},{112,17... | collective-permute-start | bytes 786440 | tf_op jit(solution)/shard_map/ppermute | solution.py:356
  228.3 1.4 collective-permute-done.28.refs_10_
  229.7 2.1 collective-permute-start.33
  231.8 17.7 %collective-permute-done.29.refs_11_ = f32[512,128]{1,0:T(8,128)S(1)} collective-permute-done((f32[512,128]{1,0:T(8,128)S(1)}, f32[512,128]{1,0:T(8,128)S(1)}, u32[]{:S(2)}, u32[]{:S(2)}) %collective-permute-start.29) | collective-permute-done | bytes 262176 | tf_op jit(solution)/shard_map/ppermute | solution.py:356
  249.5 6.9 %collective-permute-done.31.refs_13_ = f32[512,128]{1,0:T(8,128)S(1)} collective-permute-done((f32[512,128]{1,0:T(8,128)S(1)}, f32[512,128]{1,0:T(8,128)S(1)}, u32[]{:S(2)}, u32[]{:S(2)}) %collective-permute-start.31) | collective-permute-done | bytes 262176 | tf_op jit(solution)/shard_map/ppermute | solution.py:356
  256.4 10.9 %collective-permute-done.32.refs_14_ = f32[512,128]{1,0:T(8,128)S(1)} collective-permute-done((f32[512,128]{1,0:T(8,128)S(1)}, f32[512,128]{1,0:T(8,128)S(1)}, u32[]{:S(2)}, u32[]{:S(2)}) %collective-permute-start.32) | collective-permute-done | bytes 262176 | tf_op jit(solution)/shard_map/ppermute | solution.py:356
  267.3 5.5 %collective-permute-done.33.refs_15_ = f32[512,128]{1,0:T(8,128)S(1)} collective-permute-done((f32[512,128]{1,0:T(8,128)S(1)}, f32[512,128]{1,0:T(8,128)S(1)}, u32[]{:S(2)}, u32[]{:S(2)}) %collective-permute-start.33) | collective-permute-done | bytes 262176 | tf_op jit(solution)/shard_map/ppermute | solution.py:356
  272.8 3.1 %to_grid.1 = f32[4,4,128,512]{3,2,1,0:T(8,128)} custom-call(s32[2]{0:T(128)S(1)} %pad_add_fusion.place, f32[512,128]{1,0:T(8,128)S(1)} %get-tuple-element.62._.refs_0_, f32[512,128]{1,0:T(8,128)S(1)} %collective-permute-done.11.refs_1_, f32[512,128]{1,0:T(8,128)S(1)} %collective-permute-done.12.refs_2_, f32[512,128]{1,0:T(8,128)S(1)} %collective-permute-done.13.refs_3_, ...), custom_call_target="tpu_custom_call" | custom-call | flops 5000000 | bytes 8388608 | tf_op jit(solution)/shard_map/to_grid/pallas_call | solution.py:342
  (59 shorter events, 1.5 us)
Async XLA Ops:
  0.0 31.6 %copy-start.9 = (f32[64]{0:T(128)S(1)}, f32[64]{0:T(128)}, u32[]{:S(2)}) copy-start(f32[64]{0:T(128)} %param.17) | copy-start | bytes 772
  0.0 31.6 %copy-start.4 = (s32[1,512]{1,0:T(1,128)S(1)}, s32[1,512]{1,0:T(1,128)}, u32[]{:S(2)}) copy-start(s32[1,512]{1,0:T(1,128)} %tidx.1) | copy-start | bytes 6148
  0.0 31.6 %copy-start.5 = (s32[1,512]{1,0:T(1,128)S(1)}, s32[1,512]{1,0:T(1,128)}, u32[]{:S(2)}) copy-start(s32[1,512]{1,0:T(1,128)} %entry.1) | copy-start | bytes 6148
  0.0 31.6 %copy-start.3 = (s32[1,512,1]{1,2,0:T(1,128)S(1)}, s32[1,512,1]{1,2,0:T(1,128)}, u32[]{:S(2)}) copy-start(s32[1,512,1]{1,2,0:T(1,128)} %param.14) | copy-start | bytes 6148
  0.0 31.6 %copy-start.7 = (f32[1,512]{1,0:T(1,128)S(1)}, f32[1,512]{1,0:T(1,128)}, u32[]{:S(2)}) copy-start(f32[1,512]{1,0:T(1,128)} %inv.1) | copy-start | bytes 6148
  0.0 31.6 %copy-start.6 = (f32[1,512]{1,0:T(1,128)S(1)}, f32[1,512]{1,0:T(1,128)}, u32[]{:S(2)}) copy-start(f32[1,512]{1,0:T(1,128)} %value.1) | copy-start | bytes 6148
  0.1 2.2 copy-start
  2.3 0.7 copy-start.2
  3.0 0.7 copy-start.8
  3.7 29.2 %copy-start.1 = (f32[4,4,128,512]{3,2,1,0:T(8,128)S(1)}, f32[4,4,128,512]{3,2,1,0:T(8,128)}, u32[]{:S(2)}) copy-start(f32[4,4,128,512]{3,2,1,0:T(8,128)} %refs_3_.1) | copy-start | bytes 12582916
  6.3 18.8 %collective-permute-start.2 = (f32[512,128]{1,0:T(8,128)S(1)}, f32[512,128]{1,0:T(8,128)S(1)}, u32[]{:S(2)}, u32[]{:S(2)}) collective-permute-start(f32[512,128]{1,0:T(8,128)S(1)} %get-tuple-element.51), channel_id=1, source_target_pairs={{0,32},{16,48},{32,64},{48,80},{64,96},{80,112},{96,128},{112,144}... | collective-permute-start | bytes 786440 | tf_op jit(solution)/shard_map/ppermute | solution.py:356
  8.0 19.4 %collective-permute-start.3 = (f32[512,128]{1,0:T(8,128)S(1)}, f32[512,128]{1,0:T(8,128)S(1)}, u32[]{:S(2)}, u32[]{:S(2)}) collective-permute-start(f32[512,128]{1,0:T(8,128)S(1)} %get-tuple-element.52), channel_id=1, source_target_pairs={{0,64},{16,80},{32,96},{48,112},{64,128},{80,144},{96,160},{112,17... | collective-permute-start | bytes 786440 | tf_op jit(solution)/shard_map/ppermute | solution.py:356
  11.0 9.1 %collective-permute-start = (f32[4,4,1,512]{3,2,1,0:T(1,128)S(1)}, f32[4,4,1,512]{3,2,1,0:T(1,128)S(1)}, u32[]{:S(2)}, u32[]{:S(2)}) collective-permute-start(f32[4,4,1,512]{3,2,1,0:T(1,128)S(1)} %get-tuple-element.48), channel_id=1, source_target_pairs={{0,1},{1,2},{2,3},{3,4},{4,5},{5,6},{6,7},{7,8},{8,9},{9,10},{10,1... | collective-permute-start | bytes 98312 | tf_op jit(solution)/shard_map/ppermute | solution.py:403
  13.4 7.2 %collective-permute-start.1 = (f32[4,4,1,512]{3,2,1,0:T(1,128)S(1)}, f32[4,4,1,512]{3,2,1,0:T(1,128)S(1)}, u32[]{:S(2)}, u32[]{:S(2)}) collective-permute-start(f32[4,4,1,512]{3,2,1,0:T(1,128)S(1)} %get-tuple-element.49), channel_id=1, source_target_pairs={{1,0},{2,1},{3,2},{4,3},{5,4},{6,5},{7,6},{8,7},{9,8},{10,9},{11,1... | collective-permute-start | bytes 98312 | tf_op jit(solution)/shard_map/ppermute | solution.py:404
  16.3 30.0 %collective-permute-start.4 = (f32[512,128]{1,0:T(8,128)S(1)}, f32[512,128]{1,0:T(8,128)S(1)}, u32[]{:S(2)}, u32[]{:S(2)}) collective-permute-start(f32[512,128]{1,0:T(8,128)S(1)} %get-tuple-element.53), channel_id=1, source_target_pairs={{0,96},{16,112},{32,128},{48,144},{64,160},{80,176},{96,192},{112,... | collective-permute-start | bytes 786440 | tf_op jit(solution)/shard_map/ppermute | solution.py:356
  20.1 31.3 %collective-permute-start.5 = (f32[512,128]{1,0:T(8,128)S(1)}, f32[512,128]{1,0:T(8,128)S(1)}, u32[]{:S(2)}, u32[]{:S(2)}) collective-permute-start(f32[512,128]{1,0:T(8,128)S(1)} %get-tuple-element.54), channel_id=1, source_target_pairs={{0,128},{16,144},{32,160},{48,176},{64,192},{80,208},{96,224},{112... | collective-permute-start | bytes 786440 | tf_op jit(solution)/shard_map/ppermute | solution.py:356
  20.7 31.7 %collective-permute-start.6 = (f32[512,128]{1,0:T(8,128)S(1)}, f32[512,128]{1,0:T(8,128)S(1)}, u32[]{:S(2)}, u32[]{:S(2)}) collective-permute-start(f32[512,128]{1,0:T(8,128)S(1)} %get-tuple-element.55), channel_id=1, source_target_pairs={{0,160},{16,176},{32,192},{48,208},{64,224},{80,240},{96,0},{112,1... | collective-permute-start | bytes 786440 | tf_op jit(solution)/shard_map/ppermute | solution.py:356
  25.0 39.3 %collective-permute-start.7 = (f32[512,128]{1,0:T(8,128)S(1)}, f32[512,128]{1,0:T(8,128)S(1)}, u32[]{:S(2)}, u32[]{:S(2)}) collective-permute-start(f32[512,128]{1,0:T(8,128)S(1)} %get-tuple-element.56), channel_id=1, source_target_pairs={{0,192},{16,208},{32,224},{48,240},{64,0},{80,16},{96,32},{112,48}... | collective-permute-start | bytes 786440 | tf_op jit(solution)/shard_map/ppermute | solution.py:356
  27.4 39.7 %collective-permute-start.8 = (f32[512,128]{1,0:T(8,128)S(1)}, f32[512,128]{1,0:T(8,128)S(1)}, u32[]{:S(2)}, u32[]{:S(2)}) collective-permute-start(f32[512,128]{1,0:T(8,128)S(1)} %get-tuple-element.57), channel_id=1, source_target_pairs={{0,224},{16,240},{32,0},{48,16},{64,32},{80,48},{96,64},{112,80},{... | collective-permute-start | bytes 786440 | tf_op jit(solution)/shard_map/ppermute | solution.py:356
  35.7 0.7 copy-start.13
  36.3 0.7 copy-start.14
  37.0 0.7 copy-start.15
  37.7 0.7 copy-start.16
  38.5 31.6 %copy-start.10 = (f32[512,128]{1,0:T(8,128)}, f32[512,128]{1,0:T(8,128)S(1)}, u32[]{:S(2)}) copy-start(f32[512,128]{1,0:T(8,128)S(1)} %get-tuple-element.76) | copy-start | bytes 786436
  38.5 31.7 %copy-start.11 = (f32[512,128]{1,0:T(8,128)}, f32[512,128]{1,0:T(8,128)S(1)}, u32[]{:S(2)}) copy-start(f32[512,128]{1,0:T(8,128)S(1)} %get-tuple-element.75) | copy-start | bytes 786436
  38.5 31.7 %copy-start.12 = (f32[512,128]{1,0:T(8,128)}, f32[512,128]{1,0:T(8,128)S(1)}, u32[]{:S(2)}) copy-start(f32[512,128]{1,0:T(8,128)S(1)} %get-tuple-element.74) | copy-start | bytes 786436
  68.5 14.8 %collective-permute-start.9 = (f32[64,32,128]{2,1,0:T(8,128)S(1)}, f32[64,32,128]{2,1,0:T(8,128)S(1)}, u32[]{:S(2)}, u32[]{:S(2)}) collective-permute-start(f32[64,32,128]{2,1,0:T(8,128)S(1)} %get-tuple-element.59), channel_id=1, source_target_pairs={{0,16},{16,0},{32,48},{48,32},{64,80},{80,64},{96,112},{112,96},{1... | collective-permute-start | bytes 3145736 | tf_op jit(solution)/shard_map/ppermute | solution.py:370
  97.2 16.1 %collective-permute-start.10 = (f32[64,32,128]{2,1,0:T(8,128)S(1)}, f32[64,32,128]{2,1,0:T(8,128)S(1)}, u32[]{:S(2)}, u32[]{:S(2)}) collective-permute-start(f32[64,32,128]{2,1,0:T(8,128)S(1)} %get-tuple-element.61), channel_id=1, source_target_pairs={{0,16},{16,0},{32,48},{48,32},{64,80},{80,64},{96,112},{112,96},{1... | collective-permute-start | bytes 3145736 | tf_op jit(solution)/shard_map/ppermute | solution.py:370
  97.6 9.7 %collective-permute-start.18 = (f32[512,128]{1,0:T(8,128)}, f32[512,128]{1,0:T(8,128)S(1)}, u32[]{:S(2)}, u32[]{:S(2)}) collective-permute-start(f32[512,128]{1,0:T(8,128)} %copy-done.16), channel_id=1, source_target_pairs={{0,32},{16,48},{32,64},{48,80},{64,96},{80,112},{96,128},{112,144}... | collective-permute-start | bytes 786440 | tf_op jit(solution)/shard_map/ppermute | solution.py:356
  97.9 15.1 %collective-permute-start.19 = (f32[512,128]{1,0:T(8,128)}, f32[512,128]{1,0:T(8,128)S(1)}, u32[]{:S(2)}, u32[]{:S(2)}) collective-permute-start(f32[512,128]{1,0:T(8,128)} %copy-done.15), channel_id=1, source_target_pairs={{0,64},{16,80},{32,96},{48,112},{64,128},{80,144},{96,160},{112,17... | collective-permute-start | bytes 786440 | tf_op jit(solution)/shard_map/ppermute | solution.py:356
  98.3 35.4 %collective-permute-start.20 = (f32[512,128]{1,0:T(8,128)}, f32[512,128]{1,0:T(8,128)S(1)}, u32[]{:S(2)}, u32[]{:S(2)}) collective-permute-start(f32[512,128]{1,0:T(8,128)} %copy-done.14), channel_id=1, source_target_pairs={{0,96},{16,112},{32,128},{48,144},{64,160},{80,176},{96,192},{112,... | collective-permute-start | bytes 786440 | tf_op jit(solution)/shard_map/ppermute | solution.py:356
  100.3 39.7 %collective-permute-start.21 = (f32[512,128]{1,0:T(8,128)}, f32[512,128]{1,0:T(8,128)S(1)}, u32[]{:S(2)}, u32[]{:S(2)}) collective-permute-start(f32[512,128]{1,0:T(8,128)} %copy-done.13), channel_id=1, source_target_pairs={{0,128},{16,144},{32,160},{48,176},{64,192},{80,208},{96,224},{112... | collective-permute-start | bytes 786440 | tf_op jit(solution)/shard_map/ppermute | solution.py:356
  107.3 32.7 %collective-permute-start.22 = (f32[512,128]{1,0:T(8,128)}, f32[512,128]{1,0:T(8,128)S(1)}, u32[]{:S(2)}, u32[]{:S(2)}) collective-permute-start(f32[512,128]{1,0:T(8,128)} %copy-done.12), channel_id=1, source_target_pairs={{0,160},{16,176},{32,192},{48,208},{64,224},{80,240},{96,0},{112,1... | collective-permute-start | bytes 786440 | tf_op jit(solution)/shard_map/ppermute | solution.py:356
  113.0 32.6 %collective-permute-start.23 = (f32[512,128]{1,0:T(8,128)}, f32[512,128]{1,0:T(8,128)S(1)}, u32[]{:S(2)}, u32[]{:S(2)}) collective-permute-start(f32[512,128]{1,0:T(8,128)} %copy-done.11), channel_id=1, source_target_pairs={{0,192},{16,208},{32,224},{48,240},{64,0},{80,16},{96,32},{112,48}... | collective-permute-start | bytes 786440 | tf_op jit(solution)/shard_map/ppermute | solution.py:356
  113.3 36.0 %collective-permute-start.24 = (f32[512,128]{1,0:T(8,128)}, f32[512,128]{1,0:T(8,128)S(1)}, u32[]{:S(2)}, u32[]{:S(2)}) collective-permute-start(f32[512,128]{1,0:T(8,128)} %copy-done.10), channel_id=1, source_target_pairs={{0,224},{16,240},{32,0},{48,16},{64,32},{80,48},{96,64},{112,80},{... | collective-permute-start | bytes 786440 | tf_op jit(solution)/shard_map/ppermute | solution.py:356
  150.7 3.8 %collective-permute-start.25 = (f32[64,32,128]{2,1,0:T(8,128)S(1)}, f32[64,32,128]{2,1,0:T(8,128)S(1)}, u32[]{:S(2)}, u32[]{:S(2)}) collective-permute-start(f32[64,32,128]{2,1,0:T(8,128)S(1)} %get-tuple-element.78), channel_id=1, source_target_pairs={{0,16},{16,0},{32,48},{48,32},{64,80},{80,64},{96,112},{112,96},{1... | collective-permute-start | bytes 3145736 | tf_op jit(solution)/shard_map/ppermute | solution.py:370
  168.5 9.3 %collective-permute-start.26 = (f32[64,32,128]{2,1,0:T(8,128)S(1)}, f32[64,32,128]{2,1,0:T(8,128)S(1)}, u32[]{:S(2)}, u32[]{:S(2)}) collective-permute-start(f32[64,32,128]{2,1,0:T(8,128)S(1)} %get-tuple-element.80), channel_id=1, source_target_pairs={{0,16},{16,0},{32,48},{48,32},{64,80},{80,64},{96,112},{112,96},{1... | collective-permute-start | bytes 3145736 | tf_op jit(solution)/shard_map/ppermute | solution.py:370
  168.9 10.7 %collective-permute-start.11 = (f32[512,128]{1,0:T(8,128)S(1)}, f32[512,128]{1,0:T(8,128)S(1)}, u32[]{:S(2)}, u32[]{:S(2)}) collective-permute-start(f32[512,128]{1,0:T(8,128)S(1)} %get-tuple-element.63), channel_id=1, source_target_pairs={{0,224},{16,240},{32,0},{48,16},{64,32},{80,48},{96,64},{112,80},{... | collective-permute-start | bytes 786440 | tf_op jit(solution)/shard_map/ppermute | solution.py:356
  171.3 19.9 %collective-permute-start.12 = (f32[512,128]{1,0:T(8,128)S(1)}, f32[512,128]{1,0:T(8,128)S(1)}, u32[]{:S(2)}, u32[]{:S(2)}) collective-permute-start(f32[512,128]{1,0:T(8,128)S(1)} %get-tuple-element.64), channel_id=1, source_target_pairs={{0,192},{16,208},{32,224},{48,240},{64,0},{80,16},{96,32},{112,48}... | collective-permute-start | bytes 786440 | tf_op jit(solution)/shard_map/ppermute | solution.py:356
  173.3 42.7 %collective-permute-start.13 = (f32[512,128]{1,0:T(8,128)S(1)}, f32[512,128]{1,0:T(8,128)S(1)}, u32[]{:S(2)}, u32[]{:S(2)}) collective-permute-start(f32[512,128]{1,0:T(8,128)S(1)} %get-tuple-element.65), channel_id=1, source_target_pairs={{0,160},{16,176},{32,192},{48,208},{64,224},{80,240},{96,0},{112,1... | collective-permute-start | bytes 786440 | tf_op jit(solution)/shard_map/ppermute | solution.py:356
  174.1 41.8 %collective-permute-start.14 = (f32[512,128]{1,0:T(8,128)S(1)}, f32[512,128]{1,0:T(8,128)S(1)}, u32[]{:S(2)}, u32[]{:S(2)}) collective-permute-start(f32[512,128]{1,0:T(8,128)S(1)} %get-tuple-element.66), channel_id=1, source_target_pairs={{0,128},{16,144},{32,160},{48,176},{64,192},{80,208},{96,224},{112... | collective-permute-start | bytes 786440 | tf_op jit(solution)/shard_map/ppermute | solution.py:356
  177.8 43.8 %collective-permute-start.15 = (f32[512,128]{1,0:T(8,128)S(1)}, f32[512,128]{1,0:T(8,128)S(1)}, u32[]{:S(2)}, u32[]{:S(2)}) collective-permute-start(f32[512,128]{1,0:T(8,128)S(1)} %get-tuple-element.67), channel_id=1, source_target_pairs={{0,96},{16,112},{32,128},{48,144},{64,160},{80,176},{96,192},{112,... | collective-permute-start | bytes 786440 | tf_op jit(solution)/shard_map/ppermute | solution.py:356
  179.6 42.0 %collective-permute-start.16 = (f32[512,128]{1,0:T(8,128)S(1)}, f32[512,128]{1,0:T(8,128)S(1)}, u32[]{:S(2)}, u32[]{:S(2)}) collective-permute-start(f32[512,128]{1,0:T(8,128)S(1)} %get-tuple-element.68), channel_id=1, source_target_pairs={{0,64},{16,80},{32,96},{48,112},{64,128},{80,144},{96,160},{112,17... | collective-permute-start | bytes 786440 | tf_op jit(solution)/shard_map/ppermute | solution.py:356
  191.2 33.6 %collective-permute-start.17 = (f32[512,128]{1,0:T(8,128)S(1)}, f32[512,128]{1,0:T(8,128)S(1)}, u32[]{:S(2)}, u32[]{:S(2)}) collective-permute-start(f32[512,128]{1,0:T(8,128)S(1)} %get-tuple-element.69), channel_id=1, source_target_pairs={{0,32},{16,48},{32,64},{48,80},{64,96},{80,112},{96,128},{112,144}... | collective-permute-start | bytes 786440 | tf_op jit(solution)/shard_map/ppermute | solution.py:356
  216.0 9.0 %collective-permute-start.27 = (f32[512,128]{1,0:T(8,128)S(1)}, f32[512,128]{1,0:T(8,128)S(1)}, u32[]{:S(2)}, u32[]{:S(2)}) collective-permute-start(f32[512,128]{1,0:T(8,128)S(1)} %get-tuple-element.82), channel_id=1, source_target_pairs={{0,224},{16,240},{32,0},{48,16},{64,32},{80,48},{96,64},{112,80},{... | collective-permute-start | bytes 786440 | tf_op jit(solution)/shard_map/ppermute | solution.py:356
  216.0 13.7 %collective-permute-start.28 = (f32[512,128]{1,0:T(8,128)S(1)}, f32[512,128]{1,0:T(8,128)S(1)}, u32[]{:S(2)}, u32[]{:S(2)}) collective-permute-start(f32[512,128]{1,0:T(8,128)S(1)} %get-tuple-element.83), channel_id=1, source_target_pairs={{0,192},{16,208},{32,224},{48,240},{64,0},{80,16},{96,32},{112,48}... | collective-permute-start | bytes 786440 | tf_op jit(solution)/shard_map/ppermute | solution.py:356
  221.6 27.9 %collective-permute-start.29 = (f32[512,128]{1,0:T(8,128)S(1)}, f32[512,128]{1,0:T(8,128)S(1)}, u32[]{:S(2)}, u32[]{:S(2)}) collective-permute-start(f32[512,128]{1,0:T(8,128)S(1)} %get-tuple-element.84), channel_id=1, source_target_pairs={{0,160},{16,176},{32,192},{48,208},{64,224},{80,240},{96,0},{112,1... | collective-permute-start | bytes 786440 | tf_op jit(solution)/shard_map/ppermute | solution.py:356
  221.6 27.8 %collective-permute-start.30 = (f32[512,128]{1,0:T(8,128)S(1)}, f32[512,128]{1,0:T(8,128)S(1)}, u32[]{:S(2)}, u32[]{:S(2)}) collective-permute-start(f32[512,128]{1,0:T(8,128)S(1)} %get-tuple-element.85), channel_id=1, source_target_pairs={{0,128},{16,144},{32,160},{48,176},{64,192},{80,208},{96,224},{112... | collective-permute-start | bytes 786440 | tf_op jit(solution)/shard_map/ppermute | solution.py:356
  224.8 31.6 %collective-permute-start.31 = (f32[512,128]{1,0:T(8,128)S(1)}, f32[512,128]{1,0:T(8,128)S(1)}, u32[]{:S(2)}, u32[]{:S(2)}) collective-permute-start(f32[512,128]{1,0:T(8,128)S(1)} %get-tuple-element.86), channel_id=1, source_target_pairs={{0,96},{16,112},{32,128},{48,144},{64,160},{80,176},{96,192},{112,... | collective-permute-start | bytes 786440 | tf_op jit(solution)/shard_map/ppermute | solution.py:356
  225.0 42.3 %collective-permute-start.32 = (f32[512,128]{1,0:T(8,128)S(1)}, f32[512,128]{1,0:T(8,128)S(1)}, u32[]{:S(2)}, u32[]{:S(2)}) collective-permute-start(f32[512,128]{1,0:T(8,128)S(1)} %get-tuple-element.87), channel_id=1, source_target_pairs={{0,64},{16,80},{32,96},{48,112},{64,128},{80,144},{96,160},{112,17... | collective-permute-start | bytes 786440 | tf_op jit(solution)/shard_map/ppermute | solution.py:356
  229.7 43.1 %collective-permute-start.33 = (f32[512,128]{1,0:T(8,128)S(1)}, f32[512,128]{1,0:T(8,128)S(1)}, u32[]{:S(2)}, u32[]{:S(2)}) collective-permute-start(f32[512,128]{1,0:T(8,128)S(1)} %get-tuple-element.88), channel_id=1, source_target_pairs={{0,32},{16,48},{32,64},{48,80},{64,96},{80,112},{96,128},{112,144}... | collective-permute-start | bytes 786440 | tf_op jit(solution)/shard_map/ppermute | solution.py:356

commit v2 on v1

v2 whole, which is shorter than its diff:
```python
import functools

import jax
import jax.numpy as jnp
from jax import lax
from jax.experimental import pallas as pl
from jax.experimental.pallas import tpu as pltpu
from jax.sharding import PartitionSpec as P


F32 = jnp.float32
BF16 = jnp.bfloat16
HIGH = lax.Precision.HIGHEST
NS_ITERS = 5
CHIPS = 8
SHARE = 4
VARS = 4
LINES = 128
WIDTH = 512
HALF = 32
CAP = 32
OBS = 512
BLOCK = SHARE * VARS * 4 * 8
MB = 1 << 20


ALL_VMEM = 67_043_328


def params(mib=None):
    return pltpu.CompilerParams(vmem_limit_bytes=ALL_VMEM if mib is None else mib * MB)


def vmem():
    return pl.BlockSpec(memory_space=pltpu.VMEM)


def base_row(chunk, chip):
    if chunk == 0:
        return 32 + 8 * chip
    return 8 * chip + jnp.where(chip >= 4, 64, 0)


def stencil_kernel(chunk, dists, part, *refs):
    low = high = obs_in = placed = None
    if part == "first":
        *obs_in, spread_in, mix_in, x = refs[:9]
        refs = refs[9:]
    elif part == "b":
        low, high, spread_in, mix_in, x = refs[:5]
        refs = refs[5:]
    else:
        placed, spread_in, mix_in, x = refs[:4]
        refs = refs[4:]
    outs, refs = refs[: len(dists)], refs[len(dists) :]
    if part == "first":
        placed, *refs = refs
    if part == "rest":
        first_out, last_out, *refs = refs
    win, spread, mix, sems, scalar_sems = refs
    chip = lax.axis_index("mem") // 2
    bases, starts, copies = [], [], []
    for k, d in enumerate(dists):
        base = pl.multiple_of(base_row(chunk, lax.rem(chip + d, CHIPS)), 8)
        start = base - 8 if chunk == 0 else jnp.clip(base - 8, 0, LINES - 24)
        start = pl.multiple_of(start, 8)
        copy = pltpu.make_async_copy(x.at[:, :, pl.ds(start, 24), :], win.at[k], sems.at[k])
        copy.start()
        bases.append(base)
        starts.append(start)
        copies.append(copy)
    scalars = [
        pltpu.make_async_copy(spread_in, spread, scalar_sems.at[0]),
        pltpu.make_async_copy(mix_in, mix, scalar_sems.at[1]),
    ]
    for copy in scalars:
        copy.start()
    edges = []
    if part == "rest":
        edges = [
            pltpu.make_async_copy(x.at[:, :, pl.ds(0, 8), :], first_out, sems.at[len(dists)]),
            pltpu.make_async_copy(x.at[:, :, pl.ds(LINES - 8, 8), :], last_out, sems.at[len(dists) + 1]),
        ]
        for copy in edges:
            copy.start()
    row = lax.broadcasted_iota(jnp.int32, (8, WIDTH), 0)
    lane = lax.broadcasted_iota(jnp.int32, (8, WIDTH), 1)
    if part == "first":
        placed[...] = place_obs(*obs_in)
    if chunk == 0:
        for k, d in enumerate(dists):
            lanes = pl.multiple_of(lax.rem(chip + d, CHIPS) * 128, 128)
            outs[k][BLOCK : BLOCK + 8, :] = placed[:, pl.ds(lanes, 128)]
    for copy in scalars:
        copy.wait()
    for k in range(len(dists)):
        base, out = bases[k], outs[k]
        copies[k].wait()
        if chunk == 0:
            here, before, behind = 8, 0, 16
        else:
            here = pl.multiple_of(base - starts[k], 8)
            before = pl.multiple_of(jnp.maximum(here - 8, 0), 8)
            behind = pl.multiple_of(jnp.minimum(here + 8, 16), 8)

        def member(m, _, k=k, base=base, out=out, here=here, before=before, behind=behind):
            tiles = [win[k, m, v, pl.ds(here, 8), :] for v in range(VARS)]
            for v in range(VARS):
                t = tiles[v]
                prev = pltpu.roll(win[k, m, v, pl.ds(before, 8), :], 1, 0)
                nxt = pltpu.roll(win[k, m, v, pl.ds(behind, 8), :], 7, 0)
                if chunk == 1:
                    prev = jnp.where(base == 0, pltpu.roll(low[m, v], 1, 0), prev)
                    nxt = jnp.where(base == LINES - 8, pltpu.roll(high[m, v], 7, 0), nxt)
                up = jnp.where(row == 0, prev, pltpu.roll(t, 1, 0))
                down = jnp.where(row == 7, nxt, pltpu.roll(t, 7, 0))
                left = jnp.where(lane == 0, 0.0, pltpu.roll(t, 1, 1))
                right = jnp.where(lane == WIDTH - 1, 0.0, pltpu.roll(t, WIDTH - 1, 1))
                laplace = down + up + right + left - 4.0 * t
                mixing = mix[v, 0] * tiles[0]
                for w in range(1, VARS):
                    mixing = mixing + mix[v, w] * tiles[w]
                res = t + spread[v] * laplace + mixing
                for q in range(4):
                    at = pl.multiple_of(m * 128 + (v * 4 + q) * 8, 8)
                    out[pl.ds(at, 8), :] = res[:, q * 128 : (q + 1) * 128]
            return 0

        lax.fori_loop(0, SHARE, member, 0)
    for copy in edges:
        copy.wait()


def hbm():
    return pl.BlockSpec(memory_space=pltpu.HBM)


def stencil(chunk, dists, part, extra, spread, mix, x):
    n = len(dists)
    rows = BLOCK + 8 if chunk == 0 else BLOCK
    more = []
    if part == "first":
        more = [jax.ShapeDtypeStruct((8, 2 * OBS), F32)]
    if part == "rest":
        more = [jax.ShapeDtypeStruct((SHARE, VARS, 8, WIDTH), F32)] * 2
    res = pl.pallas_call(
        functools.partial(stencil_kernel, chunk, dists, part),
        in_specs=[vmem()] * len(extra) + [hbm()] * 3,
        out_specs=[vmem()] * (n + len(more)),
        out_shape=[jax.ShapeDtypeStruct((rows, 128), F32)] * n + more,
        scratch_shapes=[
            pltpu.VMEM((n, SHARE, VARS, 24, WIDTH), F32),
            pltpu.SMEM((VARS,), F32),
            pltpu.SMEM((VARS, VARS), F32),
            pltpu.SemaphoreType.DMA((n + 2,)),
            pltpu.SemaphoreType.DMA((2,)),
        ],
        compiler_params=params(),
        cost_estimate=pl.CostEstimate(flops=2_500_000 * n, bytes_accessed=n * MB, transcendentals=0),
    )(*extra, spread, mix, x)
    return dict(zip(dists, res[:n])), res[n:]


def parts3(x):
    a = x.astype(BF16)
    r = x - a.astype(F32)
    b = r.astype(BF16)
    c = (r - b.astype(F32)).astype(BF16)
    return a, b, c


def nt(a, b):
    return lax.dot_general(a, b, (((1,), (1,)), ((), ())), preferred_element_type=F32)


def place_obs(pid, tidx, entry, value, inv, table):
    ids = pid[...]
    sub = lax.broadcasted_iota(jnp.int32, (32, OBS), 0)
    named = sub == jnp.broadcast_to(ids, (32, OBS))
    onehot = jnp.where(named, 1.0, 0.0)
    earlier = jnp.where(
        lax.broadcasted_iota(jnp.int32, (OBS, OBS), 0) < lax.broadcasted_iota(jnp.int32, (OBS, OBS), 1),
        1.0, 0.0,
    ).astype(BF16)
    before = jnp.dot(onehot.astype(BF16), earlier, preferred_element_type=F32)
    rank = jnp.sum(before * onehot, axis=0, keepdims=True).astype(jnp.int32)
    inner = (ids >= 8) & (ids < 24)
    group = jnp.where(inner, 2 * (ids - 8), jnp.where(ids < 8, 2 * ids + 1, 2 * (ids - 16) + 1))
    target = group * CAP + rank
    levels = table.shape[1]
    look = jnp.where(
        lax.broadcasted_iota(jnp.int32, (levels, OBS), 0) == jnp.broadcast_to(tidx[...], (levels, OBS)),
        1.0, 0.0,
    ).astype(BF16)
    taper = sum(
        jnp.dot(jnp.broadcast_to(p, (16, levels)), look, preferred_element_type=F32)
        for p in parts3(table[...])
    )
    weight = inv[...] * taper[0:1]
    c = entry[...]
    place = (c & 0x1800) | ((c & 0x180) << 2) | ((c & 0x600) >> 2) | (c & 0x7F)
    r8 = lax.broadcasted_iota(jnp.int32, (16, OBS), 0)
    fields = jnp.where(
        r8 == 0, jnp.broadcast_to(value[...], (16, OBS)),
        jnp.where(r8 == 1, jnp.broadcast_to(weight, (16, OBS)),
                  jnp.where(r8 == 2, jnp.broadcast_to(place.astype(F32), (16, OBS)), 0.0)),
    )
    pieces = parts3(fields)
    halves = []
    for k in range(2):
        slots = jnp.where(
            lax.broadcasted_iota(jnp.int32, (OBS, OBS), 0) + k * OBS == jnp.broadcast_to(target, (OBS, OBS)),
            1.0, 0.0,
        ).astype(BF16)
        placed = nt(pieces[0], slots) + nt(pieces[1], slots) + nt(pieces[2], slots)
        halves.append(placed[0:8])
    return jnp.concatenate(halves, axis=1)


def gather_members_kernel(chunk, *refs):
    blocks, (keep, send) = refs[:CHIPS], refs[CHIPS:]
    core = lax.axis_index("mem") % 2
    own = 4 * core
    for g in range(64):
        vl, r = g // 4, g % 4
        for d in range(CHIPS):
            keep[g, pl.ds(SHARE * d, SHARE), :] = blocks[d][pl.ds(vl * 8 + r + own, SHARE, stride=128), :]
            send[g, pl.ds(SHARE * d, SHARE), :] = blocks[d][pl.ds(vl * 8 + r + 4 - own, SHARE, stride=128), :]
    if chunk == 0:
        quarter = lax.broadcasted_iota(jnp.int32, (8, 128), 1) // CAP
        for out, whose in ((keep, core), (send, 1 - core)):
            for q in range(4):
                first = whose * 64 + (q // 2) * CAP
                packed = jnp.zeros((8, 128), F32)
                for k in range(4):
                    tile = blocks[(q % 2) * 4 + k][BLOCK : BLOCK + 8, :]
                    moved = pltpu.roll(tile, (k * CAP - first) & 127, 1)
                    packed = jnp.where(quarter == k, moved, packed)
                out[64, pl.ds(q * 8, 8), :] = packed


def gather_members(chunk, blocks):
    half = jax.ShapeDtypeStruct((65 if chunk == 0 else 64, HALF, 128), F32)
    return pl.pallas_call(
        functools.partial(gather_members_kernel, chunk),
        in_specs=[vmem()] * CHIPS,
        out_specs=[vmem()] * 2,
        out_shape=[half] * 2,
        compiler_params=params(16),
        cost_estimate=pl.CostEstimate(flops=20_000_000, bytes_accessed=4 * MB, transcendentals=0),
    )(*blocks)


def spread_members_kernel(keep, came, *outs):
    own = 4 * (lax.axis_index("mem") % 2)
    for d in range(CHIPS):
        for m in range(SHARE):
            for vl in range(16):
                at = (m * 16 + vl) * 8
                start = vl * 128 + d * SHARE + m
                outs[d][pl.ds(at + own, 4), :] = keep[pl.ds(start, 4, stride=HALF), :]
                outs[d][pl.ds(at + 4 - own, 4), :] = came[pl.ds(start, 4, stride=HALF), :]


def spread_members(keep, came):
    return pl.pallas_call(
        spread_members_kernel,
        in_specs=[vmem()] * 2,
        out_specs=[vmem()] * CHIPS,
        out_shape=[jax.ShapeDtypeStruct((BLOCK, 128), F32)] * CHIPS,
        compiler_params=params(16),
        cost_estimate=pl.CostEstimate(flops=20_000_000, bytes_accessed=4 * MB, transcendentals=0),
    )(keep.reshape(64 * HALF, 128), came.reshape(64 * HALF, 128))


def high(a, b):
    return jnp.dot(a, b, precision=HIGH, preferred_element_type=F32)


def analysis_kernel(chunk, keep, came, *refs):
    if chunk == 0:
        out_keep, out_send, later, parts, centres, acc = refs
        tiles = [[half[64, q * 8 : (q + 1) * 8, :] for half in (keep, came) for q in pair] for pair in ((0, 1), (2, 3))]
        obs = jnp.concatenate(tiles[0], axis=1)
        later[...] = jnp.concatenate(tiles[1], axis=1)
    else:
        obs_in, out_keep, out_send, parts, centres, acc = refs
        obs = obs_in[...]
    members = 2 * HALF
    acc[...] = jnp.zeros_like(acc)
    cell = lax.broadcasted_iota(jnp.int32, (256, OBS), 0)
    where_obs = obs[2:3, :].astype(jnp.int32)

    def select(t, _):
        g = 2 * t
        cols = [jnp.concatenate([keep[g + h], came[g + h]], axis=0) for h in range(2)]
        block = jnp.concatenate(cols, axis=1)
        centre = jnp.sum(block, axis=0, keepdims=True) * (1.0 / members)
        dev = block - centre
        hi = dev.astype(BF16)
        lo = (dev - hi.astype(F32)).astype(BF16)
        c1 = centre.astype(BF16)
        rest = centre - c1.astype(F32)
        c2 = rest.astype(BF16)
        c3 = rest - c2.astype(F32)
        row = lax.broadcasted_iota(jnp.int32, (16, 256), 0)
        crows = jnp.where(
            row == 0, jnp.broadcast_to(c1.astype(F32), (16, 256)),
            jnp.where(row == 1, jnp.broadcast_to(c2.astype(F32), (16, 256)),
                      jnp.where(row == 2, jnp.broadcast_to(c3, (16, 256)), 0.0)),
        ).astype(BF16)
        both = jnp.concatenate([hi, lo], axis=0)
        parts[t] = both
        centres[t] = jnp.broadcast_to(centre, (8, 256))
        chosen = jnp.where(cell == jnp.broadcast_to(where_obs - t * 256, (256, OBS)), 1.0, 0.0).astype(BF16)
        acc[...] += jnp.dot(jnp.concatenate([both, crows], axis=0), chosen, preferred_element_type=F32)
        return 0

    lax.fori_loop(0, 32, select, 0)
    columns = acc[0:members] + acc[members : 2 * members]
    centre_obs = acc[128:129] + acc[129:130] + acc[130:131]
    innovation = obs[0:1, :] - centre_obs
    weight = obs[1:2, :]
    weighted = columns * weight
    pair = (((1,), (1,)), ((), ()))
    gram = lax.dot_general(weighted, columns, pair, precision=HIGH, preferred_element_type=F32)
    drive = lax.dot_general(
        jnp.broadcast_to(weight * innovation, (8, OBS)), columns, pair, precision=HIGH, preferred_element_type=F32
    )
    eye = jnp.where(
        lax.broadcasted_iota(jnp.int32, (members, members), 0) == lax.broadcasted_iota(jnp.int32, (members, members), 1),
        1.0, 0.0,
    )
    system = (members - 1.0) * eye + gram
    norm = jnp.sqrt(jnp.sum(jnp.sum(system * system, axis=1, keepdims=True), axis=0, keepdims=True))
    y = system / norm
    z = 1.5 * eye - 0.5 * y
    y = high(y, z)
    for sweep in range(1, NS_ITERS):
        mid = 1.5 * eye - 0.5 * high(z, y)
        if sweep < NS_ITERS - 1:
            y = high(y, mid)
        z = high(mid, z)
    root = z / jnp.sqrt(norm)
    offset = high(high(drive, root), root)
    coeff = offset[0:1, :] + jnp.sqrt(members - 1.0) * root
    spread = jnp.where(
        lax.broadcasted_iota(jnp.int32, (members, 256), 0)
        == (lax.broadcasted_iota(jnp.int32, (members, 256), 1) & (members - 1)),
        1.0, 0.0,
    )
    four = high(coeff, spread)
    four_hi = four.astype(BF16)
    four_lo = four - four_hi.astype(F32)
    lanes = lax.broadcasted_iota(jnp.int32, (members, 256), 1)
    left = jnp.where(lanes < 128, four_hi.astype(F32), four_lo).astype(BF16)

    def transform(t, _):
        g = 2 * t
        both = parts[t]
        res = jnp.dot(left, jnp.concatenate([both, both], axis=0), preferred_element_type=F32)
        res = res + jnp.broadcast_to(centres[t][0:1], (members, 256))
        for h in range(2):
            out_keep[g + h] = res[0:HALF, h * 128 : (h + 1) * 128]
            out_send[g + h] = res[HALF:members, h * 128 : (h + 1) * 128]
        return 0

    lax.fori_loop(0, 32, transform, 0)


def analysis(chunk, keep, came, obs):
    half = jax.ShapeDtypeStruct((64, HALF, 128), F32)
    later = [jax.ShapeDtypeStruct((8, OBS), F32)] if chunk == 0 else []
    return pl.pallas_call(
        functools.partial(analysis_kernel, chunk),
        in_specs=[vmem()] * (2 + len(obs)),
        out_specs=[vmem()] * (2 + len(later)),
        out_shape=[half] * 2 + later,
        scratch_shapes=[
            pltpu.VMEM((32, 128, 256), BF16),
            pltpu.VMEM((32, 8, 256), F32),
            pltpu.VMEM((144, OBS), F32),
        ],
        compiler_params=params(24),
        cost_estimate=pl.CostEstimate(flops=100_000_000, bytes_accessed=4 * MB, transcendentals=0),
    )(keep, came, *obs)


def assemble_kernel(chunk, dists, *refs):
    *refs, out, tiles, sems = refs
    blocks = refs[-len(dists) :]
    chip = lax.axis_index("mem") // 2
    copies = []
    for k, d in enumerate(dists):
        for m in range(SHARE):
            for v in range(VARS):
                for q in range(4):
                    at = (m * 16 + v * 4 + q) * 8
                    tiles[k, m, v, :, q * 128 : (q + 1) * 128] = blocks[k][at : at + 8, :]
        base = pl.multiple_of(base_row(chunk, lax.rem(chip + d, CHIPS)), 8)
        copy = pltpu.make_async_copy(tiles.at[k], out.at[:, :, pl.ds(base, 8), :], sems.at[k])
        copy.start()
        copies.append(copy)
    for copy in copies:
        copy.wait()


def assemble(chunk, dists, grid, blocks):
    n = len(dists)
    kept = [] if grid is None else [grid]
    return pl.pallas_call(
        functools.partial(assemble_kernel, chunk, dists),
        in_specs=[hbm()] * len(kept) + [vmem()] * n,
        out_specs=hbm(),
        out_shape=jax.ShapeDtypeStruct((SHARE, VARS, LINES, WIDTH), F32),
        scratch_shapes=[pltpu.VMEM((n, SHARE, VARS, 8, WIDTH), F32), pltpu.SemaphoreType.DMA((n,))],
        input_output_aliases={0: 0} if kept else {},
        compiler_params=params(8),
        cost_estimate=pl.CostEstimate(flops=1_000_000 * n, bytes_accessed=n * MB // 2, transcendentals=0),
    )(*kept, *[blocks[d] for d in dists])


def hop(block, d):
    n = 2 * CHIPS
    return lax.ppermute(block, "mem", [(i, (i + 2 * d) % n) for i in range(n)])


ORDER = (4, 3, 5, 2, 6, 1, 7)
ALL = ORDER + (0,)
PIECES = ((4, 0, 5), (3, 6, 7), (2, 1))


def exchange(blocks, dists, sign):
    got = {}
    for d in dists:
        if d == 0:
            got[d] = blocks[d]
            continue
        got[d] = hop(blocks[d], sign * d)
    return got


def swap(x):
    return lax.ppermute(x, "mem", [(i, i ^ 1) for i in range(2 * CHIPS)])


def shards(
    prior_ensemble,
    spreading_factor,
    tendency_matrix,
    measured_data,
    inverse_error,
    assigned_subregion,
    measured_entry,
    taper_index,
    taper_factors,
):
    x = prior_ensemble
    physics = (spreading_factor, tendency_matrix, x)

    obs = (
        assigned_subregion.reshape(1, OBS), taper_index, measured_entry, measured_data,
        inverse_error, taper_factors.reshape(1, -1),
    )
    sent, (placed,) = stencil(0, ALL[:1], "first", obs, *physics)
    got_a = exchange(sent, ALL[:1], 1)
    sent, _ = stencil(0, ALL[1:3], "next", (placed,), *physics)
    got_a |= exchange(sent, ALL[1:3], 1)
    sent, (first, last) = stencil(0, ALL[3:], "rest", (placed,), *physics)
    got_a |= exchange(sent, ALL[3:], 1)

    count = lax.axis_size("dom")
    forward = [(i, i + 1) for i in range(count - 1)]
    backward = [(b, a) for a, b in forward]
    low = lax.ppermute(last, "dom", forward)
    high_row = lax.ppermute(first, "dom", backward)
    sent_b, _ = stencil(1, ALL, "b", (low, high_row), *physics)
    got_b = exchange(sent_b, ALL, 1)

    back, slots = [], []
    for chunk, got in enumerate((got_a, got_b)):
        keep, send = gather_members(chunk, [got[d] for d in range(CHIPS)])
        came = swap(send)
        out_keep, out_send, *slots = analysis(chunk, keep, came, slots)
        returned = swap(out_send)
        outs = spread_members(out_keep, returned)
        back.append(exchange(dict(enumerate(outs)), ALL, -1))
    grid = assemble(0, ALL, None, back[0])
    for dists in PIECES:
        grid = assemble(1, dists, grid, back[1])
    return grid


def solution(mesh):
    in_specs = (
        P("mem", None, "dom", None),
        P(),
        P(),
        P("dom", "mem"),
        P("dom", "mem"),
        P("dom", "mem", None),
        P("dom", "mem"),
        P("dom", "mem"),
        P(),
    )
    out_specs = P("mem", None, "dom", None)

    return jax.shard_map(shards, mesh=mesh, in_specs=in_specs, out_specs=out_specs, check_vma=False)
```

time: 278 us -> 260 us (0.935)
  waiting for transfers between devices: 144 us -> 119 us
  Pallas kernels: 43.9 us -> 58.1 us
  blocking collectives: 12.7 us -> 0 us
  starting transfers between devices: 67.8 us -> 76.4 us
  local copies, waits for them, and re-layouts: 6.74 us -> 3.56 us
    ppermute x28, waiting for transfers between devices: 142 us -> 119 us  [hop(): return lax.ppermute(block, 'mem', [(i, (i + 2 * d) % n) for i in range(n)])]
    pallas_call x8 -> x12, Pallas kernels: 40.4 us -> 55.4 us  [the longest x2 28 us: analysis(): pl.pallas_call(functools.partial(analysis_kernel, chunk), in_specs=[vmem(...]
    all_to_all x1 -> x0, blocking collectives: 12.7 us -> none  [shards(): lax.all_to_all(outgoing, 'mem', split_axis=0, concat_axis=0, tiled=True)]
    ppermute x28, starting transfers between devices: 58.5 us -> 68.6 us  [hop(): return lax.ppermute(block, 'mem', [(i, (i + 2 * d) % n) for i in range(n)])]
    unnamed x34 -> x8, local copies, waits for them, and re-layouts: 6.35 us -> 3.56 us
  transfers between devices with their start and end apart: 34 -> 34, of which waited for: 20 -> 17; matrix products, arithmetic and copies ran while one was open for 0% -> 0% of each run, Pallas kernels for 3% -> 19%
where the time goes in v2:
time: 260 us; the launch traced here: 257 us
  waiting for transfers between devices  119 us (46%)
  starting transfers between devices  76.4 us (29%)
  Pallas kernels  58.1 us (22%)
  local copies, waits for them, and re-layouts  3.56 us (1%)
    ppermute x28, waiting for transfers between devices, hop(): return lax.ppermute(block, 'mem', [(i, (i + 2 * d) % n) for i in range(n)])  119 us
    ppermute x28, starting transfers between devices, hop(): return lax.ppermute(block, 'mem', [(i, (i + 2 * d) % n) for i in range(n)])  68.6 us
    pallas_call x2, Pallas kernels, analysis(): pl.pallas_call(functools.partial(analysis_kernel, chunk), in_specs=[vmem(...  28 us
    pallas_call x4, Pallas kernels, stencil(): pl.pallas_call(functools.partial(stencil_kernel, chunk, dists, part), in_...  19.2 us
  transfers between devices with their start and end apart: 34, of which 17 were waited for; matrix products, arithmetic and copies ran while one was open for 0% of the time, Pallas kernels for 19%

profile of v2, /device:TPU:29, one launch (start us, length us, event | category | flops | bytes accessed | tf_op | source)
XLA Modules:
  0.0 257.1 jit_solution(2269248223651507393)
XLA Ops:
  0.0 3.2 %shard_map.91 = (f32[520,128]{1,0:T(8,128)}, f32[8,1024]{1,0:T(8,128)}) custom-call(s32[1,512]{1,0:T(1,128)} %bitcast.10, s32[1,512]{1,0:T(1,128)} %refs_1_.3, s32[1,512]{1,0:T(1,128)} %refs_2_.4, f32[1,512]{1,0:T(1,128)} %refs_3_.4, f32[1,512]{1,0:T(1,128)} %refs_4_.2, f32[1,64]{1,0:T(1,128)} %bitcast.11, f32[4]{0:T(128)} %refs_2_.7, f32[4,4]{1,0:T(4,128)} %refs_3_.7, ...), custom_call_target="tpu_custom_call" | custom-call | flops 2500000 | bytes 1048576 | tf_op jit(solution)/shard_map/pallas_call | solution.py:146
  3.2 5.5 %shard_map.92 = (f32[520,128]{1,0:T(8,128)}, f32[520,128]{1,0:T(8,128)}, f32[520,128]{1,0:T(8,128)}, f32[520,128]{1,0:T(8,128)}, f32[520,128]{1,0:T(8,128)}, /*i...) custom-call(f32[8,1024]{1,0:T(8,128)} %get-tuple-element.49.refs_0_, f32[4]{0:T(128)} %refs_2_.7, f32[4,4]{1,0:T(4,128)} %refs_3_.7, ...), custom_call_target="tpu_custom_call" | custom-call | flops 12500000 | bytes 5242880 | tf_op jit(solution)/shard_map/pallas_call | solution.py:146
  8.6 2.5 collective-permute-start.16
  11.1 2.8 %collective-permute-start.17 = (f32[4,4,8,512]{3,2,1,0:T(8,128)}, f32[4,4,8,512]{3,2,1,0:T(8,128)}, u32[]{:S(2)}, u32[]{:S(2)}) collective-permute-start(f32[4,4,8,512]{3,2,1,0:T(8,128)} %get-tuple-element.71), channel_id=1, source_target_pairs={{1,0},{2,1},{3,2},{4,3},{5,4},{6,5},{7,6},{8,7},{9,8},{10,9},{11,1... | collective-permute-start | bytes 786440 | tf_op jit(solution)/shard_map/ppermute | solution.py:476
  13.9 7.0 %collective-permute-start.3 = (f32[520,128]{1,0:T(8,128)}, f32[520,128]{1,0:T(8,128)}, u32[]{:S(2)}, u32[]{:S(2)}) collective-permute-start(f32[520,128]{1,0:T(8,128)} %get-tuple-element.54), channel_id=1, source_target_pairs={{0,128},{16,144},{32,160},{48,176},{64,192},{80,208},{96,224},{112... | collective-permute-start | bytes 798728 | tf_op jit(solution)/shard_map/ppermute | solution.py:425
  20.9 3.5 %shard_map.93 = (f32[520,128]{1,0:T(8,128)}, f32[520,128]{1,0:T(8,128)}) custom-call(f32[8,1024]{1,0:T(8,128)} %get-tuple-element.49.refs_0_, f32[4]{0:T(128)} %refs_2_.7, f32[4,4]{1,0:T(4,128)} %refs_3_.7, f32[4,4,128,512]{3,2,1,0:T(8,128)} %refs_4_.3), custom_call_target="tpu_custom_call" | custom-call | flops 5000000 | bytes 2097152 | tf_op jit(solution)/shard_map/pallas_call | solution.py:146
  24.5 1.7 collective-permute-start.2
  26.2 2.8 %collective-permute-start.4 = (f32[520,128]{1,0:T(8,128)}, f32[520,128]{1,0:T(8,128)}, u32[]{:S(2)}, u32[]{:S(2)}) collective-permute-start(f32[520,128]{1,0:T(8,128)} %get-tuple-element.55), channel_id=1, source_target_pairs={{0,160},{16,176},{32,192},{48,208},{64,224},{80,240},{96,0},{112,1... | collective-permute-start | bytes 798728 | tf_op jit(solution)/shard_map/ppermute | solution.py:425
  29.0 0.7 collective-permute-start
  29.8 0.0 collective-permute-done.17.refs_1_
  29.8 0.5 collective-permute-start.1
  30.3 7.4 %collective-permute-start.5 = (f32[520,128]{1,0:T(8,128)}, f32[520,128]{1,0:T(8,128)}, u32[]{:S(2)}, u32[]{:S(2)}) collective-permute-start(f32[520,128]{1,0:T(8,128)} %get-tuple-element.56), channel_id=1, source_target_pairs={{0,192},{16,208},{32,224},{48,240},{64,0},{80,16},{96,32},{112,48}... | collective-permute-start | bytes 798728 | tf_op jit(solution)/shard_map/ppermute | solution.py:425
  37.7 11.7 %collective-permute-done.2.refs_3_ = f32[520,128]{1,0:T(8,128)S(1)} collective-permute-done((f32[520,128]{1,0:T(8,128)}, f32[520,128]{1,0:T(8,128)S(1)}, u32[]{:S(2)}, u32[]{:S(2)}) %collective-permute-start.2) | collective-permute-done | bytes 266272 | tf_op jit(solution)/shard_map/ppermute | solution.py:425
  49.4 0.7 copy-done.1
  50.1 7.1 %shard_map.98 = (f32[512,128]{1,0:T(8,128)}, f32[512,128]{1,0:T(8,128)}, f32[512,128]{1,0:T(8,128)}, f32[512,128]{1,0:T(8,128)}, f32[512,128]{1,0:T(8,128)}, /*i...) custom-call(f32[4,4,8,512]{3,2,1,0:T(8,128)} %collective-permute-done.16.refs_0_, ...), custom_call_target="tpu_custom_call" | custom-call | flops 20000000 | bytes 8388608 | tf_op jit(solution)/shard_map/pallas_call | solution.py:146
  57.2 0.0 collective-permute-done.4.refs_5_
  57.2 1.5 collective-permute-start.18
  58.7 0.7 collective-permute-start.19
  59.4 1.7 collective-permute-done.1.refs_2_
  61.1 9.1 %collective-permute-start.20 = (f32[512,128]{1,0:T(8,128)}, f32[512,128]{1,0:T(8,128)S(1)}, u32[]{:S(2)}, u32[]{:S(2)}) collective-permute-start(f32[512,128]{1,0:T(8,128)} %get-tuple-element.75), channel_id=1, source_target_pairs={{0,96},{16,112},{32,128},{48,144},{64,160},{80,176},{96,192},{112,... | collective-permute-start | bytes 786440 | tf_op jit(solution)/shard_map/ppermute | solution.py:425
  70.2 0.9 copy-done
  71.2 0.9 copy-done.2
  72.1 2.7 %shard_map.94 = (f32[65,32,128]{2,1,0:T(8,128)S(1)}, f32[65,32,128]{2,1,0:T(8,128)S(1)}) custom-call(f32[520,128]{1,0:T(8,128)S(1)} %copy-done, f32[520,128]{1,0:T(8,128)} %collective-permute-done.refs_1_, f32[520,128]{1,0:T(8,128)} %collective-permute-done.1.refs_2_, f32[520,128]{1,0:T(8,128)S(1)} %copy-done.2, f32[520,128]{1,0:T(8,128)} %collective-permute-done.3.refs_4_, ...), custom_call_target="tpu_custom_call" | custom-call | flops 20000000 | bytes 4194304 | tf_op jit(solution)/shard_map/pallas_call | solution.py:244
  74.9 1.0 collective-permute-start.7
  75.9 2.9 %collective-permute-start.21 = (f32[512,128]{1,0:T(8,128)}, f32[512,128]{1,0:T(8,128)S(1)}, u32[]{:S(2)}, u32[]{:S(2)}) collective-permute-start(f32[512,128]{1,0:T(8,128)} %get-tuple-element.76), channel_id=1, source_target_pairs={{0,128},{16,144},{32,160},{48,176},{64,192},{80,208},{96,224},{112... | collective-permute-start | bytes 786440 | tf_op jit(solution)/shard_map/ppermute | solution.py:425
  78.8 0.0 collective-permute-done.18.refs_1_
  78.8 4.7 %collective-permute-start.22 = (f32[512,128]{1,0:T(8,128)}, f32[512,128]{1,0:T(8,128)S(1)}, u32[]{:S(2)}, u32[]{:S(2)}) collective-permute-start(f32[512,128]{1,0:T(8,128)} %get-tuple-element.77), channel_id=1, source_target_pairs={{0,160},{16,176},{32,192},{48,208},{64,224},{80,240},{96,0},{112,1... | collective-permute-start | bytes 786440 | tf_op jit(solution)/shard_map/ppermute | solution.py:425
  83.5 3.0 %collective-permute-done.19.refs_2_ = f32[512,128]{1,0:T(8,128)S(1)} collective-permute-done((f32[512,128]{1,0:T(8,128)}, f32[512,128]{1,0:T(8,128)S(1)}, u32[]{:S(2)}, u32[]{:S(2)}) %collective-permute-start.19) | collective-permute-done | bytes 262176 | tf_op jit(solution)/shard_map/ppermute | solution.py:425
  86.6 16.7 %collective-permute-done.20.refs_3_ = f32[512,128]{1,0:T(8,128)S(1)} collective-permute-done((f32[512,128]{1,0:T(8,128)}, f32[512,128]{1,0:T(8,128)S(1)}, u32[]{:S(2)}, u32[]{:S(2)}) %collective-permute-start.20) | collective-permute-done | bytes 262176 | tf_op jit(solution)/shard_map/ppermute | solution.py:425
  103.2 2.4 collective-permute-done.21.refs_4_
  105.7 4.5 %collective-permute-done.22.refs_5_ = f32[512,128]{1,0:T(8,128)S(1)} collective-permute-done((f32[512,128]{1,0:T(8,128)}, f32[512,128]{1,0:T(8,128)S(1)}, u32[]{:S(2)}, u32[]{:S(2)}) %collective-permute-start.22) | collective-permute-done | bytes 262176 | tf_op jit(solution)/shard_map/ppermute | solution.py:425
  110.2 11.2 %collective-permute-done.23.refs_6_ = f32[512,128]{1,0:T(8,128)S(1)} collective-permute-done((f32[512,128]{1,0:T(8,128)}, f32[512,128]{1,0:T(8,128)S(1)}, u32[]{:S(2)}, u32[]{:S(2)}) %collective-permute-start.23) | collective-permute-done | bytes 262176 | tf_op jit(solution)/shard_map/ppermute | solution.py:425
  121.4 3.9 %collective-permute-done.24.refs_7_ = f32[512,128]{1,0:T(8,128)S(1)} collective-permute-done((f32[512,128]{1,0:T(8,128)}, f32[512,128]{1,0:T(8,128)S(1)}, u32[]{:S(2)}, u32[]{:S(2)}) %collective-permute-start.24) | collective-permute-done | bytes 262176 | tf_op jit(solution)/shard_map/ppermute | solution.py:425
  125.4 0.9 copy-done.3
  126.3 1.4 shard_map.99
  127.7 0.9 collective-permute-start.25
  128.6 14.0 %shard_map.95 = (f32[64,32,128]{2,1,0:T(8,128)S(1)}, f32[64,32,128]{2,1,0:T(8,128)S(1)}, f32[8,512]{1,0:T(8,128)S(1)}) custom-call(f32[65,32,128]{2,1,0:T(8,128)S(1)} %get-tuple-element.58.keep, f32[65,32,128]{2,1,0:T(8,128)S(1)} %collective-permute-done.7.came), custom_call_target="tpu_custom_call" | custom-call | flops 100000000 | bytes 4194304 | tf_op jit(solution)/shard_map/pallas_call | solution.py:374
  142.6 0.0 collective-permute-start.8
  142.7 14.0 %shard_map.100 = (f32[64,32,128]{2,1,0:T(8,128)S(1)}, f32[64,32,128]{2,1,0:T(8,128)S(1)}) custom-call(f32[64,32,128]{2,1,0:T(8,128)S(1)} %get-tuple-element.80.keep, f32[64,32,128]{2,1,0:T(8,128)S(1)} %collective-permute-done.25.came, f32[8,512]{1,0:T(8,128)S(1)} %get-tuple-element.82.refs_0_), custom_call_target="tpu_custom_call" | custom-call | flops 100000000 | bytes 4194304 | tf_op jit(solution)/shard_map/pallas_call | solution.py:374
  156.6 0.5 collective-permute-start.26
  157.2 1.4 shard_map.96
  158.5 2.7 %collective-permute-start.9 = (f32[512,128]{1,0:T(8,128)S(1)}, f32[512,128]{1,0:T(8,128)S(1)}, u32[]{:S(2)}, u32[]{:S(2)}) collective-permute-start(f32[512,128]{1,0:T(8,128)S(1)} %get-tuple-element.62), channel_id=1, source_target_pairs={{0,128},{16,144},{32,160},{48,176},{64,192},{80,208},{96,224},{112... | collective-permute-start | bytes 786440 | tf_op jit(solution)/shard_map/ppermute | solution.py:425
  161.2 4.2 %collective-permute-start.10 = (f32[512,128]{1,0:T(8,128)S(1)}, f32[512,128]{1,0:T(8,128)S(1)}, u32[]{:S(2)}, u32[]{:S(2)}) collective-permute-start(f32[512,128]{1,0:T(8,128)S(1)} %get-tuple-element.63), channel_id=1, source_target_pairs={{0,160},{16,176},{32,192},{48,208},{64,224},{80,240},{96,0},{112,1... | collective-permute-start | bytes 786440 | tf_op jit(solution)/shard_map/ppermute | solution.py:425
  165.4 3.8 %collective-permute-start.12 = (f32[512,128]{1,0:T(8,128)S(1)}, f32[512,128]{1,0:T(8,128)S(1)}, u32[]{:S(2)}, u32[]{:S(2)}) collective-permute-start(f32[512,128]{1,0:T(8,128)S(1)} %get-tuple-element.65), channel_id=1, source_target_pairs={{0,192},{16,208},{32,224},{48,240},{64,0},{80,16},{96,32},{112,48}... | collective-permute-start | bytes 786440 | tf_op jit(solution)/shard_map/ppermute | solution.py:425
  169.2 5.2 %collective-permute-done.9.refs_0_ = f32[512,128]{1,0:T(8,128)S(1)} collective-permute-done((f32[512,128]{1,0:T(8,128)S(1)}, f32[512,128]{1,0:T(8,128)S(1)}, u32[]{:S(2)}, u32[]{:S(2)}) %collective-permute-start.9) | collective-permute-done | bytes 262176 | tf_op jit(solution)/shard_map/ppermute | solution.py:425
  174.4 4.9 %collective-permute-start.14 = (f32[512,128]{1,0:T(8,128)S(1)}, f32[512,128]{1,0:T(8,128)S(1)}, u32[]{:S(2)}, u32[]{:S(2)}) collective-permute-start(f32[512,128]{1,0:T(8,128)S(1)} %get-tuple-element.67), channel_id=1, source_target_pairs={{0,224},{16,240},{32,0},{48,16},{64,32},{80,48},{96,64},{112,80},{... | collective-permute-start | bytes 786440 | tf_op jit(solution)/shard_map/ppermute | solution.py:425
  179.2 12.1 %collective-permute-done.10.refs_1_ = f32[512,128]{1,0:T(8,128)S(1)} collective-permute-done((f32[512,128]{1,0:T(8,128)S(1)}, f32[512,128]{1,0:T(8,128)S(1)}, u32[]{:S(2)}, u32[]{:S(2)}) %collective-permute-start.10) | collective-permute-done | bytes 262176 | tf_op jit(solution)/shard_map/ppermute | solution.py:425
  191.3 0.3 collective-permute-start.15
  191.6 1.4 shard_map.101
  193.0 0.3 collective-permute-done.11.refs_2_
  193.3 6.7 %collective-permute-start.27 = (f32[512,128]{1,0:T(8,128)S(1)}, f32[512,128]{1,0:T(8,128)S(1)}, u32[]{:S(2)}, u32[]{:S(2)}) collective-permute-start(f32[512,128]{1,0:T(8,128)S(1)} %get-tuple-element.85), channel_id=1, source_target_pairs={{0,128},{16,144},{32,160},{48,176},{64,192},{80,208},{96,224},{112... | collective-permute-start | bytes 786440 | tf_op jit(solution)/shard_map/ppermute | solution.py:425
  199.9 4.7 %collective-permute-done.12.refs_3_ = f32[512,128]{1,0:T(8,128)S(1)} collective-permute-done((f32[512,128]{1,0:T(8,128)S(1)}, f32[512,128]{1,0:T(8,128)S(1)}, u32[]{:S(2)}, u32[]{:S(2)}) %collective-permute-start.12) | collective-permute-done | bytes 262176 | tf_op jit(solution)/shard_map/ppermute | solution.py:425
  204.6 4.5 %collective-permute-start.29 = (f32[512,128]{1,0:T(8,128)S(1)}, f32[512,128]{1,0:T(8,128)S(1)}, u32[]{:S(2)}, u32[]{:S(2)}) collective-permute-start(f32[512,128]{1,0:T(8,128)S(1)} %get-tuple-element.88), channel_id=1, source_target_pairs={{0,160},{16,176},{32,192},{48,208},{64,224},{80,240},{96,0},{112,1... | collective-permute-start | bytes 786440 | tf_op jit(solution)/shard_map/ppermute | solution.py:425
  209.1 1.0 collective-permute-start.30
  210.1 0.2 collective-permute-done.15.refs_6_
  210.2 1.4 collective-permute-start.31
  211.6 10.4 %collective-permute-done.27.refs_1_ = f32[512,128]{1,0:T(8,128)S(1)} collective-permute-done((f32[512,128]{1,0:T(8,128)S(1)}, f32[512,128]{1,0:T(8,128)S(1)}, u32[]{:S(2)}, u32[]{:S(2)}) %collective-permute-start.27) | collective-permute-done | bytes 262176 | tf_op jit(solution)/shard_map/ppermute | solution.py:425
  222.0 16.2 %collective-permute-done.28.refs_3_ = f32[512,128]{1,0:T(8,128)S(1)} collective-permute-done((f32[512,128]{1,0:T(8,128)S(1)}, f32[512,128]{1,0:T(8,128)S(1)}, u32[]{:S(2)}, u32[]{:S(2)}) %collective-permute-start.28) | collective-permute-done | bytes 262176 | tf_op jit(solution)/shard_map/ppermute | solution.py:425
  238.2 1.4 shard_map.97.refs_0_
  239.6 0.9 shard_map.102.refs_0_
  240.5 9.0 %collective-permute-done.30.refs_2_ = f32[512,128]{1,0:T(8,128)S(1)} collective-permute-done((f32[512,128]{1,0:T(8,128)S(1)}, f32[512,128]{1,0:T(8,128)S(1)}, u32[]{:S(2)}, u32[]{:S(2)}) %collective-permute-start.30) | collective-permute-done | bytes 262176 | tf_op jit(solution)/shard_map/ppermute | solution.py:425
  249.5 5.6 %collective-permute-done.31.refs_3_ = f32[512,128]{1,0:T(8,128)S(1)} collective-permute-done((f32[512,128]{1,0:T(8,128)S(1)}, f32[512,128]{1,0:T(8,128)S(1)}, u32[]{:S(2)}, u32[]{:S(2)}) %collective-permute-start.31) | collective-permute-done | bytes 262176 | tf_op jit(solution)/shard_map/ppermute | solution.py:425
  255.1 0.9 shard_map.103.refs_0_
  256.1 0.8 shard_map.104
  (26 shorter events, 0.1 us)
Async XLA Ops:
  8.6 20.4 %collective-permute-start.16 = (f32[4,4,8,512]{3,2,1,0:T(8,128)}, f32[4,4,8,512]{3,2,1,0:T(8,128)}, u32[]{:S(2)}, u32[]{:S(2)}) collective-permute-start(f32[4,4,8,512]{3,2,1,0:T(8,128)} %get-tuple-element.70), channel_id=1, source_target_pairs={{0,1},{1,2},{2,3},{3,4},{4,5},{5,6},{6,7},{7,8},{8,9},{9,10},{10,1... | collective-permute-start | bytes 786440 | tf_op jit(solution)/shard_map/ppermute | solution.py:475
  11.1 18.6 %collective-permute-start.17 = (f32[4,4,8,512]{3,2,1,0:T(8,128)}, f32[4,4,8,512]{3,2,1,0:T(8,128)}, u32[]{:S(2)}, u32[]{:S(2)}) collective-permute-start(f32[4,4,8,512]{3,2,1,0:T(8,128)} %get-tuple-element.71), channel_id=1, source_target_pairs={{1,0},{2,1},{3,2},{4,3},{5,4},{6,5},{7,6},{8,7},{9,8},{10,9},{11,1... | collective-permute-start | bytes 786440 | tf_op jit(solution)/shard_map/ppermute | solution.py:476
  13.9 16.4 %collective-permute-start.3 = (f32[520,128]{1,0:T(8,128)}, f32[520,128]{1,0:T(8,128)}, u32[]{:S(2)}, u32[]{:S(2)}) collective-permute-start(f32[520,128]{1,0:T(8,128)} %get-tuple-element.54), channel_id=1, source_target_pairs={{0,128},{16,144},{32,160},{48,176},{64,192},{80,208},{96,224},{112... | collective-permute-start | bytes 798728 | tf_op jit(solution)/shard_map/ppermute | solution.py:425
  24.5 24.9 %collective-permute-start.2 = (f32[520,128]{1,0:T(8,128)}, f32[520,128]{1,0:T(8,128)S(1)}, u32[]{:S(2)}, u32[]{:S(2)}) collective-permute-start(f32[520,128]{1,0:T(8,128)} %get-tuple-element.53), channel_id=1, source_target_pairs={{0,96},{16,112},{32,128},{48,144},{64,160},{80,176},{96,192},{112,... | collective-permute-start | bytes 798728 | tf_op jit(solution)/shard_map/ppermute | solution.py:425
  26.2 31.0 %collective-permute-start.4 = (f32[520,128]{1,0:T(8,128)}, f32[520,128]{1,0:T(8,128)}, u32[]{:S(2)}, u32[]{:S(2)}) collective-permute-start(f32[520,128]{1,0:T(8,128)} %get-tuple-element.55), channel_id=1, source_target_pairs={{0,160},{16,176},{32,192},{48,208},{64,224},{80,240},{96,0},{112,1... | collective-permute-start | bytes 798728 | tf_op jit(solution)/shard_map/ppermute | solution.py:425
  29.0 29.7 %collective-permute-start = (f32[520,128]{1,0:T(8,128)}, f32[520,128]{1,0:T(8,128)}, u32[]{:S(2)}, u32[]{:S(2)}) collective-permute-start(f32[520,128]{1,0:T(8,128)} %get-tuple-element.51), channel_id=1, source_target_pairs={{0,32},{16,48},{32,64},{48,80},{64,96},{80,112},{96,128},{112,144}... | collective-permute-start | bytes 798728 | tf_op jit(solution)/shard_map/ppermute | solution.py:425
  29.8 31.4 %collective-permute-start.1 = (f32[520,128]{1,0:T(8,128)}, f32[520,128]{1,0:T(8,128)}, u32[]{:S(2)}, u32[]{:S(2)}) collective-permute-start(f32[520,128]{1,0:T(8,128)} %get-tuple-element.52), channel_id=1, source_target_pairs={{0,64},{16,80},{32,96},{48,112},{64,128},{80,144},{96,160},{112,17... | collective-permute-start | bytes 798728 | tf_op jit(solution)/shard_map/ppermute | solution.py:425
  30.3 39.9 %collective-permute-start.5 = (f32[520,128]{1,0:T(8,128)}, f32[520,128]{1,0:T(8,128)}, u32[]{:S(2)}, u32[]{:S(2)}) collective-permute-start(f32[520,128]{1,0:T(8,128)} %get-tuple-element.56), channel_id=1, source_target_pairs={{0,192},{16,208},{32,224},{48,240},{64,0},{80,16},{96,32},{112,48}... | collective-permute-start | bytes 798728 | tf_op jit(solution)/shard_map/ppermute | solution.py:425
  49.4 0.7 copy-start.1
  50.1 20.1 %collective-permute-start.6 = (f32[520,128]{1,0:T(8,128)}, f32[520,128]{1,0:T(8,128)}, u32[]{:S(2)}, u32[]{:S(2)}) collective-permute-start(f32[520,128]{1,0:T(8,128)} %get-tuple-element.57), channel_id=1, source_target_pairs={{0,224},{16,240},{32,0},{48,16},{64,32},{80,48},{96,64},{112,80},{... | collective-permute-start | bytes 798728 | tf_op jit(solution)/shard_map/ppermute | solution.py:425
  57.2 21.6 %collective-permute-start.18 = (f32[512,128]{1,0:T(8,128)}, f32[512,128]{1,0:T(8,128)S(1)}, u32[]{:S(2)}, u32[]{:S(2)}) collective-permute-start(f32[512,128]{1,0:T(8,128)} %get-tuple-element.73), channel_id=1, source_target_pairs={{0,32},{16,48},{32,64},{48,80},{64,96},{80,112},{96,128},{112,144}... | collective-permute-start | bytes 786440 | tf_op jit(solution)/shard_map/ppermute | solution.py:425
  58.7 27.8 %collective-permute-start.19 = (f32[512,128]{1,0:T(8,128)}, f32[512,128]{1,0:T(8,128)S(1)}, u32[]{:S(2)}, u32[]{:S(2)}) collective-permute-start(f32[512,128]{1,0:T(8,128)} %get-tuple-element.74), channel_id=1, source_target_pairs={{0,64},{16,80},{32,96},{48,112},{64,128},{80,144},{96,160},{112,17... | collective-permute-start | bytes 786440 | tf_op jit(solution)/shard_map/ppermute | solution.py:425
  61.1 42.1 %collective-permute-start.20 = (f32[512,128]{1,0:T(8,128)}, f32[512,128]{1,0:T(8,128)S(1)}, u32[]{:S(2)}, u32[]{:S(2)}) collective-permute-start(f32[512,128]{1,0:T(8,128)} %get-tuple-element.75), channel_id=1, source_target_pairs={{0,96},{16,112},{32,128},{48,144},{64,160},{80,176},{96,192},{112,... | collective-permute-start | bytes 786440 | tf_op jit(solution)/shard_map/ppermute | solution.py:425
  70.2 1.0 copy-start
  71.2 1.0 copy-start.2
  74.9 53.8 %collective-permute-start.7 = (f32[65,32,128]{2,1,0:T(8,128)S(1)}, f32[65,32,128]{2,1,0:T(8,128)S(1)}, u32[]{:S(2)}, u32[]{:S(2)}) collective-permute-start(f32[65,32,128]{2,1,0:T(8,128)S(1)} %get-tuple-element.59), channel_id=1, source_target_pairs={{0,16},{16,0},{32,48},{48,32},{64,80},{80,64},{96,112},{112,96},{1... | collective-permute-start | bytes 3194888 | tf_op jit(solution)/shard_map/ppermute | solution.py:444
  75.9 29.8 %collective-permute-start.21 = (f32[512,128]{1,0:T(8,128)}, f32[512,128]{1,0:T(8,128)S(1)}, u32[]{:S(2)}, u32[]{:S(2)}) collective-permute-start(f32[512,128]{1,0:T(8,128)} %get-tuple-element.76), channel_id=1, source_target_pairs={{0,128},{16,144},{32,160},{48,176},{64,192},{80,208},{96,224},{112... | collective-permute-start | bytes 786440 | tf_op jit(solution)/shard_map/ppermute | solution.py:425
  78.8 31.4 %collective-permute-start.22 = (f32[512,128]{1,0:T(8,128)}, f32[512,128]{1,0:T(8,128)S(1)}, u32[]{:S(2)}, u32[]{:S(2)}) collective-permute-start(f32[512,128]{1,0:T(8,128)} %get-tuple-element.77), channel_id=1, source_target_pairs={{0,160},{16,176},{32,192},{48,208},{64,224},{80,240},{96,0},{112,1... | collective-permute-start | bytes 786440 | tf_op jit(solution)/shard_map/ppermute | solution.py:425
  86.6 34.9 %collective-permute-start.23 = (f32[512,128]{1,0:T(8,128)}, f32[512,128]{1,0:T(8,128)S(1)}, u32[]{:S(2)}, u32[]{:S(2)}) collective-permute-start(f32[512,128]{1,0:T(8,128)} %get-tuple-element.78), channel_id=1, source_target_pairs={{0,192},{16,208},{32,224},{48,240},{64,0},{80,16},{96,32},{112,48}... | collective-permute-start | bytes 786440 | tf_op jit(solution)/shard_map/ppermute | solution.py:425
  103.2 22.1 %collective-permute-start.24 = (f32[512,128]{1,0:T(8,128)}, f32[512,128]{1,0:T(8,128)S(1)}, u32[]{:S(2)}, u32[]{:S(2)}) collective-permute-start(f32[512,128]{1,0:T(8,128)} %get-tuple-element.79), channel_id=1, source_target_pairs={{0,224},{16,240},{32,0},{48,16},{64,32},{80,48},{96,64},{112,80},{... | collective-permute-start | bytes 786440 | tf_op jit(solution)/shard_map/ppermute | solution.py:425
  125.4 1.0 copy-start.3
  127.7 15.0 %collective-permute-start.25 = (f32[64,32,128]{2,1,0:T(8,128)S(1)}, f32[64,32,128]{2,1,0:T(8,128)S(1)}, u32[]{:S(2)}, u32[]{:S(2)}) collective-permute-start(f32[64,32,128]{2,1,0:T(8,128)S(1)} %get-tuple-element.81), channel_id=1, source_target_pairs={{0,16},{16,0},{32,48},{48,32},{64,80},{80,64},{96,112},{112,96},{1... | collective-permute-start | bytes 3145736 | tf_op jit(solution)/shard_map/ppermute | solution.py:444
  142.6 14.5 %collective-permute-start.8 = (f32[64,32,128]{2,1,0:T(8,128)S(1)}, f32[64,32,128]{2,1,0:T(8,128)S(1)}, u32[]{:S(2)}, u32[]{:S(2)}) collective-permute-start(f32[64,32,128]{2,1,0:T(8,128)S(1)} %get-tuple-element.61), channel_id=1, source_target_pairs={{0,16},{16,0},{32,48},{48,32},{64,80},{80,64},{96,112},{112,96},{1... | collective-permute-start | bytes 3145736 | tf_op jit(solution)/shard_map/ppermute | solution.py:444
  156.6 12.6 %collective-permute-start.26 = (f32[64,32,128]{2,1,0:T(8,128)S(1)}, f32[64,32,128]{2,1,0:T(8,128)S(1)}, u32[]{:S(2)}, u32[]{:S(2)}) collective-permute-start(f32[64,32,128]{2,1,0:T(8,128)S(1)} %get-tuple-element.84), channel_id=1, source_target_pairs={{0,16},{16,0},{32,48},{48,32},{64,80},{80,64},{96,112},{112,96},{1... | collective-permute-start | bytes 3145736 | tf_op jit(solution)/shard_map/ppermute | solution.py:444
  158.5 15.9 %collective-permute-start.9 = (f32[512,128]{1,0:T(8,128)S(1)}, f32[512,128]{1,0:T(8,128)S(1)}, u32[]{:S(2)}, u32[]{:S(2)}) collective-permute-start(f32[512,128]{1,0:T(8,128)S(1)} %get-tuple-element.62), channel_id=1, source_target_pairs={{0,128},{16,144},{32,160},{48,176},{64,192},{80,208},{96,224},{112... | collective-permute-start | bytes 786440 | tf_op jit(solution)/shard_map/ppermute | solution.py:425
  161.2 30.1 %collective-permute-start.10 = (f32[512,128]{1,0:T(8,128)S(1)}, f32[512,128]{1,0:T(8,128)S(1)}, u32[]{:S(2)}, u32[]{:S(2)}) collective-permute-start(f32[512,128]{1,0:T(8,128)S(1)} %get-tuple-element.63), channel_id=1, source_target_pairs={{0,160},{16,176},{32,192},{48,208},{64,224},{80,240},{96,0},{112,1... | collective-permute-start | bytes 786440 | tf_op jit(solution)/shard_map/ppermute | solution.py:425
  165.4 27.9 %collective-permute-start.11 = (f32[512,128]{1,0:T(8,128)S(1)}, f32[512,128]{1,0:T(8,128)S(1)}, u32[]{:S(2)}, u32[]{:S(2)}) collective-permute-start(f32[512,128]{1,0:T(8,128)S(1)} %get-tuple-element.64), channel_id=1, source_target_pairs={{0,96},{16,112},{32,128},{48,144},{64,160},{80,176},{96,192},{112,... | collective-permute-start | bytes 786440 | tf_op jit(solution)/shard_map/ppermute | solution.py:425
  165.4 39.2 %collective-permute-start.12 = (f32[512,128]{1,0:T(8,128)S(1)}, f32[512,128]{1,0:T(8,128)S(1)}, u32[]{:S(2)}, u32[]{:S(2)}) collective-permute-start(f32[512,128]{1,0:T(8,128)S(1)} %get-tuple-element.65), channel_id=1, source_target_pairs={{0,192},{16,208},{32,224},{48,240},{64,0},{80,16},{96,32},{112,48}... | collective-permute-start | bytes 786440 | tf_op jit(solution)/shard_map/ppermute | solution.py:425
  169.2 35.4 %collective-permute-start.13 = (f32[512,128]{1,0:T(8,128)S(1)}, f32[512,128]{1,0:T(8,128)S(1)}, u32[]{:S(2)}, u32[]{:S(2)}) collective-permute-start(f32[512,128]{1,0:T(8,128)S(1)} %get-tuple-element.66), channel_id=1, source_target_pairs={{0,64},{16,80},{32,96},{48,112},{64,128},{80,144},{96,160},{112,17... | collective-permute-start | bytes 786440 | tf_op jit(solution)/shard_map/ppermute | solution.py:425
  174.4 34.7 %collective-permute-start.14 = (f32[512,128]{1,0:T(8,128)S(1)}, f32[512,128]{1,0:T(8,128)S(1)}, u32[]{:S(2)}, u32[]{:S(2)}) collective-permute-start(f32[512,128]{1,0:T(8,128)S(1)} %get-tuple-element.67), channel_id=1, source_target_pairs={{0,224},{16,240},{32,0},{48,16},{64,32},{80,48},{96,64},{112,80},{... | collective-permute-start | bytes 786440 | tf_op jit(solution)/shard_map/ppermute | solution.py:425
  191.3 18.9 %collective-permute-start.15 = (f32[512,128]{1,0:T(8,128)S(1)}, f32[512,128]{1,0:T(8,128)S(1)}, u32[]{:S(2)}, u32[]{:S(2)}) collective-permute-start(f32[512,128]{1,0:T(8,128)S(1)} %get-tuple-element.68), channel_id=1, source_target_pairs={{0,32},{16,48},{32,64},{48,80},{64,96},{80,112},{96,128},{112,144}... | collective-permute-start | bytes 786440 | tf_op jit(solution)/shard_map/ppermute | solution.py:425
  193.3 28.7 %collective-permute-start.27 = (f32[512,128]{1,0:T(8,128)S(1)}, f32[512,128]{1,0:T(8,128)S(1)}, u32[]{:S(2)}, u32[]{:S(2)}) collective-permute-start(f32[512,128]{1,0:T(8,128)S(1)} %get-tuple-element.85), channel_id=1, source_target_pairs={{0,128},{16,144},{32,160},{48,176},{64,192},{80,208},{96,224},{112... | collective-permute-start | bytes 786440 | tf_op jit(solution)/shard_map/ppermute | solution.py:425
  204.6 33.6 %collective-permute-start.28 = (f32[512,128]{1,0:T(8,128)S(1)}, f32[512,128]{1,0:T(8,128)S(1)}, u32[]{:S(2)}, u32[]{:S(2)}) collective-permute-start(f32[512,128]{1,0:T(8,128)S(1)} %get-tuple-element.87), channel_id=1, source_target_pairs={{0,96},{16,112},{32,128},{48,144},{64,160},{80,176},{96,192},{112,... | collective-permute-start | bytes 786440 | tf_op jit(solution)/shard_map/ppermute | solution.py:425
  204.6 35.9 %collective-permute-start.29 = (f32[512,128]{1,0:T(8,128)S(1)}, f32[512,128]{1,0:T(8,128)S(1)}, u32[]{:S(2)}, u32[]{:S(2)}) collective-permute-start(f32[512,128]{1,0:T(8,128)S(1)} %get-tuple-element.88), channel_id=1, source_target_pairs={{0,160},{16,176},{32,192},{48,208},{64,224},{80,240},{96,0},{112,1... | collective-permute-start | bytes 786440 | tf_op jit(solution)/shard_map/ppermute | solution.py:425
  209.1 40.4 %collective-permute-start.30 = (f32[512,128]{1,0:T(8,128)S(1)}, f32[512,128]{1,0:T(8,128)S(1)}, u32[]{:S(2)}, u32[]{:S(2)}) collective-permute-start(f32[512,128]{1,0:T(8,128)S(1)} %get-tuple-element.89), channel_id=1, source_target_pairs={{0,64},{16,80},{32,96},{48,112},{64,128},{80,144},{96,160},{112,17... | collective-permute-start | bytes 786440 | tf_op jit(solution)/shard_map/ppermute | solution.py:425
  210.2 44.9 %collective-permute-start.31 = (f32[512,128]{1,0:T(8,128)S(1)}, f32[512,128]{1,0:T(8,128)S(1)}, u32[]{:S(2)}, u32[]{:S(2)}) collective-permute-start(f32[512,128]{1,0:T(8,128)S(1)} %get-tuple-element.90), channel_id=1, source_target_pairs={{0,32},{16,48},{32,64},{48,80},{64,96},{80,112},{96,128},{112,144}... | collective-permute-start | bytes 786440 | tf_op jit(solution)/shard_map/ppermute | solution.py:425
  222.0 34.1 %collective-permute-start.32 = (f32[512,128]{1,0:T(8,128)S(1)}, f32[512,128]{1,0:T(8,128)S(1)}, u32[]{:S(2)}, u32[]{:S(2)}) collective-permute-start(f32[512,128]{1,0:T(8,128)S(1)} %get-tuple-element.91), channel_id=1, source_target_pairs={{0,192},{16,208},{32,224},{48,240},{64,0},{80,16},{96,32},{112,48}... | collective-permute-start | bytes 786440 | tf_op jit(solution)/shard_map/ppermute | solution.py:425
  238.2 17.9 %collective-permute-start.33 = (f32[512,128]{1,0:T(8,128)S(1)}, f32[512,128]{1,0:T(8,128)S(1)}, u32[]{:S(2)}, u32[]{:S(2)}) collective-permute-start(f32[512,128]{1,0:T(8,128)S(1)} %get-tuple-element.92), channel_id=1, source_target_pairs={{0,224},{16,240},{32,0},{48,16},{64,32},{80,48},{96,64},{112,80},{... | collective-permute-start | bytes 786440 | tf_op jit(solution)/shard_map/ppermute | solution.py:425

commit v3 on v2

--- a/solution.py
+++ b/solution.py
@@ -41,9 +41,83 @@
     return 8 * chip + jnp.where(chip >= 4, 64, 0)
 
 
+def stencil_tiles(chunk, win, m, here, before, behind, base, low, high, spread, mix, out):
+    row = lax.broadcasted_iota(jnp.int32, (8, WIDTH), 0)
+    lane = lax.broadcasted_iota(jnp.int32, (8, WIDTH), 1)
+    tiles = [win[m, v, pl.ds(here, 8), :] for v in range(VARS)]
+    for v in range(VARS):
+        t = tiles[v]
+        prev = pltpu.roll(win[m, v, pl.ds(before, 8), :], 1, 0)
+        nxt = pltpu.roll(win[m, v, pl.ds(behind, 8), :], 7, 0)
+        if chunk == 1:
+            prev = jnp.where(base == 0, pltpu.roll(low[m, v], 1, 0), prev)
+            nxt = jnp.where(base == LINES - 8, pltpu.roll(high[m, v], 7, 0), nxt)
+        up = jnp.where(row == 0, prev, pltpu.roll(t, 1, 0))
+        down = jnp.where(row == 7, nxt, pltpu.roll(t, 7, 0))
+        left = jnp.where(lane == 0, 0.0, pltpu.roll(t, 1, 1))
+        right = jnp.where(lane == WIDTH - 1, 0.0, pltpu.roll(t, WIDTH - 1, 1))
+        laplace = down + up + right + left - 4.0 * t
+        mixing = mix[v, 0] * tiles[0]
+        for w in range(1, VARS):
+            mixing = mixing + mix[v, w] * tiles[w]
+        res = t + spread[v] * laplace + mixing
+        for q in range(4):
+            at = m * 128 + (v * 4 + q) * 8
+            if not isinstance(m, int):
+                at = pl.multiple_of(at, 8)
+            out[pl.ds(at, 8), :] = res[:, q * 128 : (q + 1) * 128]
+
+
+def first_kernel(spread_in, mix_in, x, out, win, buf, spread, mix, in_sems, out_sems, scalar_sems):
+    chip = lax.axis_index("mem") // 2
+    start = pl.multiple_of(base_row(0, lax.rem(chip + FIRST, CHIPS)) - 8, 8)
+    copies = [
+        pltpu.make_async_copy(x.at[m, :, pl.ds(start, 24), :], win.at[m], in_sems.at[m]) for m in range(SHARE)
+    ]
+    scalars = [
+        pltpu.make_async_copy(spread_in, spread, scalar_sems.at[0]),
+        pltpu.make_async_copy(mix_in, mix, scalar_sems.at[1]),
+    ]
+    for copy in scalars + copies:
+        copy.start()
+    for copy in scalars:
+        copy.wait()
+    done = []
+    for m in range(SHARE):
+        copies[m].wait()
+        stencil_tiles(0, win, m, 8, 0, 16, None, None, None, spread, mix, buf)
+        rows = pl.ds(m * 128, 128)
+        copy = pltpu.make_async_copy(buf.at[rows, :], out.at[rows, :], out_sems.at[m])
+        copy.start()
+        done.append(copy)
+    for copy in done:
+        copy.wait()
+
+
+def first_stencil(spread, mix, x):
+    return pl.pallas_call(
+        first_kernel,
+        in_specs=[hbm()] * 3,
+        out_specs=hbm(),
+        out_shape=jax.ShapeDtypeStruct((BLOCK, 128), F32),
+        scratch_shapes=[
+            pltpu.VMEM((SHARE, VARS, 24, WIDTH), F32),
+            pltpu.VMEM((BLOCK, 128), F32),
+            pltpu.SMEM((VARS,), F32),
+            pltpu.SMEM((VARS, VARS), F32),
+            pltpu.SemaphoreType.DMA((SHARE,)),
+            pltpu.SemaphoreType.DMA((SHARE,)),
+            pltpu.SemaphoreType.DMA((2,)),
+        ],
+        compiler_params=params(),
+        cost_estimate=pl.CostEstimate(flops=2_500_000, bytes_accessed=MB, transcendentals=0),
+        name="stencil_a1",
+    )(spread, mix, x)
+
+
 def stencil_kernel(chunk, dists, part, *refs):
     low = high = obs_in = placed = None
-    if part == "first":
+    if part == "next":
         *obs_in, spread_in, mix_in, x = refs[:9]
         refs = refs[9:]
     elif part == "b":
@@ -53,8 +127,8 @@
         placed, spread_in, mix_in, x = refs[:4]
         refs = refs[4:]
     outs, refs = refs[: len(dists)], refs[len(dists) :]
-    if part == "first":
-        placed, *refs = refs
+    if part == "next":
+        placed, far, *refs = refs
     if part == "rest":
         first_out, last_out, *refs = refs
     win, spread, mix, sems, scalar_sems = refs
@@ -83,18 +157,19 @@
         ]
         for copy in edges:
             copy.start()
-    row = lax.broadcasted_iota(jnp.int32, (8, WIDTH), 0)
-    lane = lax.broadcasted_iota(jnp.int32, (8, WIDTH), 1)
-    if part == "first":
+    if part == "next":
         placed[...] = place_obs(*obs_in)
     if chunk == 0:
-        for k, d in enumerate(dists):
+        targets = [(d, outs[k].at[BLOCK : BLOCK + 8]) for k, d in enumerate(dists)]
+        if part == "next":
+            targets.append((FIRST, far))
+        for d, ref in targets:
             lanes = pl.multiple_of(lax.rem(chip + d, CHIPS) * 128, 128)
-            outs[k][BLOCK : BLOCK + 8, :] = placed[:, pl.ds(lanes, 128)]
+            ref[...] = placed[:, pl.ds(lanes, 128)]
     for copy in scalars:
         copy.wait()
     for k in range(len(dists)):
-        base, out = bases[k], outs[k]
+        base = bases[k]
         copies[k].wait()
         if chunk == 0:
             here, before, behind = 8, 0, 16
@@ -103,27 +178,8 @@
             before = pl.multiple_of(jnp.maximum(here - 8, 0), 8)
             behind = pl.multiple_of(jnp.minimum(here + 8, 16), 8)
 
-        def member(m, _, k=k, base=base, out=out, here=here, before=before, behind=behind):
-            tiles = [win[k, m, v, pl.ds(here, 8), :] for v in range(VARS)]
-            for v in range(VARS):
-                t = tiles[v]
-                prev = pltpu.roll(win[k, m, v, pl.ds(before, 8), :], 1, 0)
-                nxt = pltpu.roll(win[k, m, v, pl.ds(behind, 8), :], 7, 0)
-                if chunk == 1:
-                    prev = jnp.where(base == 0, pltpu.roll(low[m, v], 1, 0), prev)
-                    nxt = jnp.where(base == LINES - 8, pltpu.roll(high[m, v], 7, 0), nxt)
-                up = jnp.where(row == 0, prev, pltpu.roll(t, 1, 0))
-                down = jnp.where(row == 7, nxt, pltpu.roll(t, 7, 0))
-                left = jnp.where(lane == 0, 0.0, pltpu.roll(t, 1, 1))
-                right = jnp.where(lane == WIDTH - 1, 0.0, pltpu.roll(t, WIDTH - 1, 1))
-                laplace = down + up + right + left - 4.0 * t
-                mixing = mix[v, 0] * tiles[0]
-                for w in range(1, VARS):
-                    mixing = mixing + mix[v, w] * tiles[w]
-                res = t + spread[v] * laplace + mixing
-                for q in range(4):
-                    at = pl.multiple_of(m * 128 + (v * 4 + q) * 8, 8)
-                    out[pl.ds(at, 8), :] = res[:, q * 128 : (q + 1) * 128]
+        def member(m, _, k=k, base=base, here=here, before=before, behind=behind):
+            stencil_tiles(chunk, win.at[k], m, here, before, behind, base, low, high, spread, mix, outs[k])
             return 0
 
         lax.fori_loop(0, SHARE, member, 0)
@@ -139,8 +195,8 @@
     n = len(dists)
     rows = BLOCK + 8 if chunk == 0 else BLOCK
     more = []
-    if part == "first":
-        more = [jax.ShapeDtypeStruct((8, 2 * OBS), F32)]
+    if part == "next":
+        more = [jax.ShapeDtypeStruct((8, 2 * OBS), F32), jax.ShapeDtypeStruct((8, 128), F32)]
     if part == "rest":
         more = [jax.ShapeDtypeStruct((SHARE, VARS, 8, WIDTH), F32)] * 2
     res = pl.pallas_call(
@@ -218,7 +274,10 @@
 
 
 def gather_members_kernel(chunk, *refs):
-    blocks, (keep, send) = refs[:CHIPS], refs[CHIPS:]
+    blocks, refs = refs[:CHIPS], refs[CHIPS:]
+    if chunk == 0:
+        far, *refs = refs
+    keep, send = refs
     core = lax.axis_index("mem") % 2
     own = 4 * core
     for g in range(64):
@@ -233,7 +292,8 @@
                 first = whose * 64 + (q // 2) * CAP
                 packed = jnp.zeros((8, 128), F32)
                 for k in range(4):
-                    tile = blocks[(q % 2) * 4 + k][BLOCK : BLOCK + 8, :]
+                    d = (q % 2) * 4 + k
+                    tile = far[...] if d == FIRST else blocks[d][BLOCK : BLOCK + 8, :]
                     moved = pltpu.roll(tile, (k * CAP - first) & 127, 1)
                     packed = jnp.where(quarter == k, moved, packed)
                 out[64, pl.ds(q * 8, 8), :] = packed
@@ -243,7 +303,7 @@
     half = jax.ShapeDtypeStruct((65 if chunk == 0 else 64, HALF, 128), F32)
     return pl.pallas_call(
         functools.partial(gather_members_kernel, chunk),
-        in_specs=[vmem()] * CHIPS,
+        in_specs=[vmem()] * len(blocks),
         out_specs=[vmem()] * 2,
         out_shape=[half] * 2,
         compiler_params=params(16),
@@ -427,7 +487,8 @@
 
 ORDER = (4, 3, 5, 2, 6, 1, 7)
 ALL = ORDER + (0,)
-PIECES = ((4, 0, 5), (3, 6, 7), (2, 1))
+FIRST = ORDER[0]
+PIECES = ((4, 0, 5), (3, 6, 2), (1, 7))
 
 
 def exchange(blocks, dists, sign):
@@ -462,12 +523,13 @@
         assigned_subregion.reshape(1, OBS), taper_index, measured_entry, measured_data,
         inverse_error, taper_factors.reshape(1, -1),
     )
-    sent, (placed,) = stencil(0, ALL[:1], "first", obs, *physics)
+    sent = {FIRST: first_stencil(*physics)}
     got_a = exchange(sent, ALL[:1], 1)
-    sent, _ = stencil(0, ALL[1:3], "next", (placed,), *physics)
+    sent, (placed, far) = stencil(0, ALL[1:3], "next", obs, *physics)
     got_a |= exchange(sent, ALL[1:3], 1)
     sent, (first, last) = stencil(0, ALL[3:], "rest", (placed,), *physics)
     got_a |= exchange(sent, ALL[3:], 1)
+    far = hop(far, FIRST)
 
     count = lax.axis_size("dom")
     forward = [(i, i + 1) for i in range(count - 1)]
@@ -479,7 +541,8 @@
 
     back, slots = [], []
     for chunk, got in enumerate((got_a, got_b)):
-        keep, send = gather_members(chunk, [got[d] for d in range(CHIPS)])
+        blocks = [got[d] for d in range(CHIPS)] + ([far] if chunk == 0 else [])
+        keep, send = gather_members(chunk, blocks)
         came = swap(send)
         out_keep, out_send, *slots = analysis(chunk, keep, came, slots)
         returned = swap(out_send)

time: 260 us -> 264 us (1.015)
  waiting for transfers between devices: 119 us -> 127 us
    ppermute x28 -> x29, waiting for transfers between devices: 119 us -> 127 us  [hop(): return lax.ppermute(block, 'mem', [(i, (i + 2 * d) % n) for i in range(n)])]
    ppermute x28 -> x29, starting transfers between devices: 68.6 us -> 64.9 us  [hop(): return lax.ppermute(block, 'mem', [(i, (i + 2 * d) % n) for i in range(n)])]
    pallas_call x4 -> x3, Pallas kernels: 19.2 us -> 16.2 us  [stencil(): pl.pallas_call(functools.partial(stencil_kernel, chunk, dists, part), in_...]
  transfers between devices with their start and end apart: 34 -> 35, of which waited for: 17 -> 17; matrix products, arithmetic and copies ran while one was open for 0% -> 0% of each run, Pallas kernels for 19% -> 21%
where the time goes in v3:
time: 264 us; the launch traced here: 263 us
  waiting for transfers between devices  127 us (48%)
  starting transfers between devices  74 us (28%)
  Pallas kernels  57.1 us (22%)
  local copies, waits for them, and re-layouts  4.24 us (2%)
    ppermute x29, waiting for transfers between devices, hop(): return lax.ppermute(block, 'mem', [(i, (i + 2 * d) % n) for i in range(n)])  127 us
    ppermute x29, starting transfers between devices, hop(): return lax.ppermute(block, 'mem', [(i, (i + 2 * d) % n) for i in range(n)])  64.9 us
    pallas_call x2, Pallas kernels, analysis(): pl.pallas_call(functools.partial(analysis_kernel, chunk), in_specs=[vmem(...  28 us
    pallas_call x3, Pallas kernels, stencil(): pl.pallas_call(functools.partial(stencil_kernel, chunk, dists, part), in_...  16.2 us
  transfers between devices with their start and end apart: 35, of which 17 were waited for; matrix products, arithmetic and copies ran while one was open for 0% of the time, Pallas kernels for 21%

profile of v3, /device:TPU:29, one launch (start us, length us, event | category | flops | bytes accessed | tf_op | source)
XLA Modules:
  0.0 262.5 jit_solution(1139117037488582003)
XLA Ops:
  0.0 2.1 stencil_a1.1
  2.1 7.0 %collective-permute-start.3 = (f32[512,128]{1,0:T(8,128)}, f32[512,128]{1,0:T(8,128)}, u32[]{:S(2)}, u32[]{:S(2)}) collective-permute-start(f32[512,128]{1,0:T(8,128)} %stencil_a1.1), channel_id=1, source_target_pairs={{0,128},{16,144},{32,160},{48,176},{64,192},{80,208},{96,224},{112... | collective-permute-start | bytes 786440 | tf_op jit(solution)/shard_map/ppermute | solution.py:485
  9.1 3.7 %shard_map.91 = (f32[520,128]{1,0:T(8,128)}, f32[520,128]{1,0:T(8,128)}, f32[8,1024]{1,0:T(8,128)}, f32[8,128]{1,0:T(8,128)}) custom-call(s32[1,512]{1,0:T(1,128)} %bitcast.10, s32[1,512]{1,0:T(1,128)} %refs_1_.2, s32[1,512]{1,0:T(1,128)} %refs_2_.3, f32[1,512]{1,0:T(1,128)} %refs_3_.3, f32[1,512]{1,0:T(1,128)} %refs_4_.2, f32[1,64]{1,0:T(1,128)} %bitcast.11, ...), custom_call_target="tpu_custom_call" | custom-call | flops 5000000 | bytes 2097152 | tf_op jit(solution)/shard_map/pallas_call | solution.py:202
  12.8 5.4 %shard_map.92 = (f32[520,128]{1,0:T(8,128)}, f32[520,128]{1,0:T(8,128)}, f32[520,128]{1,0:T(8,128)}, f32[520,128]{1,0:T(8,128)}, f32[520,128]{1,0:T(8,128)}, /*i...) custom-call(f32[8,1024]{1,0:T(8,128)} %get-tuple-element.49.refs_0_, f32[4]{0:T(128)} %refs_2_.5, f32[4,4]{1,0:T(4,128)} %refs_3_.5, ...), custom_call_target="tpu_custom_call" | custom-call | flops 12500000 | bytes 5242880 | tf_op jit(solution)/shard_map/pallas_call | solution.py:202
  18.2 2.5 collective-permute-start.17
  20.7 1.7 collective-permute-start.2
  22.4 2.8 %collective-permute-start.18 = (f32[4,4,8,512]{3,2,1,0:T(8,128)}, f32[4,4,8,512]{3,2,1,0:T(8,128)S(1)}, u32[]{:S(2)}, u32[]{:S(2)}) collective-permute-start(f32[4,4,8,512]{3,2,1,0:T(8,128)} %get-tuple-element.71), channel_id=1, source_target_pairs={{1,0},{2,1},{3,2},{4,3},{5,4},{6,5},{7,6},{8,7},{9,8},{10,9},{11,1... | collective-permute-start | bytes 786440 | tf_op jit(solution)/shard_map/ppermute | solution.py:538
  25.2 1.2 collective-permute-start.7
  26.5 15.3 %collective-permute-done.7.refs_8_ = f32[8,128]{1,0:T(8,128)S(1)} collective-permute-done((f32[8,128]{1,0:T(8,128)}, f32[8,128]{1,0:T(8,128)S(1)}, u32[]{:S(2)}, u32[]{:S(2)}) %collective-permute-start.7) | collective-permute-done | bytes 4128 | tf_op jit(solution)/shard_map/ppermute | solution.py:485
  41.8 1.0 collective-permute-start
  42.8 2.5 collective-permute-start.1
  45.3 1.1 collective-permute-start.5
  46.4 0.7 copy-done.1
  47.1 2.2 collective-permute-start.6
  49.3 7.1 %shard_map.97 = (f32[512,128]{1,0:T(8,128)}, f32[512,128]{1,0:T(8,128)}, f32[512,128]{1,0:T(8,128)}, f32[512,128]{1,0:T(8,128)}, f32[512,128]{1,0:T(8,128)}, /*i...) custom-call(f32[4,4,8,512]{3,2,1,0:T(8,128)} %copy-done.6, f32[4,4,8,512]{3,2,1,0:T(8,128)} %copy-done.7, ...), custom_call_target="tpu_custom_call" | custom-call | flops 20000000 | bytes 8388608 | tf_op jit(solution)/shard_map/pallas_call | solution.py:202
  56.4 4.6 %collective-permute-done.4.refs_5_ = f32[520,128]{1,0:T(8,128)} collective-permute-done((f32[520,128]{1,0:T(8,128)}, f32[520,128]{1,0:T(8,128)}, u32[]{:S(2)}, u32[]{:S(2)}) %collective-permute-start.4) | collective-permute-done | bytes 266272 | tf_op jit(solution)/shard_map/ppermute | solution.py:485
  61.0 3.6 %collective-permute-start.20 = (f32[512,128]{1,0:T(8,128)}, f32[512,128]{1,0:T(8,128)S(1)}, u32[]{:S(2)}, u32[]{:S(2)}) collective-permute-start(f32[512,128]{1,0:T(8,128)} %get-tuple-element.74), channel_id=1, source_target_pairs={{0,64},{16,80},{32,96},{48,112},{64,128},{80,144},{96,160},{112,17... | collective-permute-start | bytes 786440 | tf_op jit(solution)/shard_map/ppermute | solution.py:485
  64.5 4.1 %collective-permute-done.5.refs_6_ = f32[520,128]{1,0:T(8,128)} collective-permute-done((f32[520,128]{1,0:T(8,128)}, f32[520,128]{1,0:T(8,128)}, u32[]{:S(2)}, u32[]{:S(2)}) %collective-permute-start.5) | collective-permute-done | bytes 266272 | tf_op jit(solution)/shard_map/ppermute | solution.py:485
  68.6 8.3 %collective-permute-done.6.refs_7_ = f32[520,128]{1,0:T(8,128)} collective-permute-done((f32[520,128]{1,0:T(8,128)}, f32[520,128]{1,0:T(8,128)}, u32[]{:S(2)}, u32[]{:S(2)}) %collective-permute-start.6) | collective-permute-done | bytes 266272 | tf_op jit(solution)/shard_map/ppermute | solution.py:485
  76.9 0.9 copy-done
  77.9 0.9 copy-done.2
  78.8 0.7 copy-done.5
  79.5 2.7 %shard_map.93 = (f32[65,32,128]{2,1,0:T(8,128)S(1)}, f32[65,32,128]{2,1,0:T(8,128)S(1)}) custom-call(f32[520,128]{1,0:T(8,128)S(1)} %copy-done, f32[520,128]{1,0:T(8,128)} %collective-permute-done.refs_1_, f32[520,128]{1,0:T(8,128)} %collective-permute-done.1.refs_2_, f32[520,128]{1,0:T(8,128)S(1)} %copy-done.2, f32[512,128]{1,0:T(8,128)} %collective-permute-done.3.refs_4_, ...), custom_call_target="tpu_custom_call" | custom-call | flops 20000000 | bytes 4194304 | tf_op jit(solution)/shard_map/pallas_call | solution.py:304
  82.2 2.2 collective-permute-start.8
  84.4 1.7 collective-permute-start.22
  86.1 1.9 collective-permute-start.23
  88.0 3.4 %collective-permute-start.24 = (f32[512,128]{1,0:T(8,128)}, f32[512,128]{1,0:T(8,128)S(1)}, u32[]{:S(2)}, u32[]{:S(2)}) collective-permute-start(f32[512,128]{1,0:T(8,128)} %get-tuple-element.78), channel_id=1, source_target_pairs={{0,192},{16,208},{32,224},{48,240},{64,0},{80,16},{96,32},{112,48}... | collective-permute-start | bytes 786440 | tf_op jit(solution)/shard_map/ppermute | solution.py:485
  91.4 4.6 %collective-permute-start.25 = (f32[512,128]{1,0:T(8,128)}, f32[512,128]{1,0:T(8,128)S(1)}, u32[]{:S(2)}, u32[]{:S(2)}) collective-permute-start(f32[512,128]{1,0:T(8,128)} %get-tuple-element.79), channel_id=1, source_target_pairs={{0,224},{16,240},{32,0},{48,16},{64,32},{80,48},{96,64},{112,80},{... | collective-permute-start | bytes 786440 | tf_op jit(solution)/shard_map/ppermute | solution.py:485
  96.0 10.4 %collective-permute-done.22.refs_4_ = f32[512,128]{1,0:T(8,128)S(1)} collective-permute-done((f32[512,128]{1,0:T(8,128)}, f32[512,128]{1,0:T(8,128)S(1)}, u32[]{:S(2)}, u32[]{:S(2)}) %collective-permute-start.22) | collective-permute-done | bytes 262176 | tf_op jit(solution)/shard_map/ppermute | solution.py:485
  106.4 11.0 %collective-permute-done.23.refs_5_ = f32[512,128]{1,0:T(8,128)S(1)} collective-permute-done((f32[512,128]{1,0:T(8,128)}, f32[512,128]{1,0:T(8,128)S(1)}, u32[]{:S(2)}, u32[]{:S(2)}) %collective-permute-start.23) | collective-permute-done | bytes 262176 | tf_op jit(solution)/shard_map/ppermute | solution.py:485
  117.5 11.3 %collective-permute-done.24.refs_6_ = f32[512,128]{1,0:T(8,128)S(1)} collective-permute-done((f32[512,128]{1,0:T(8,128)}, f32[512,128]{1,0:T(8,128)S(1)}, u32[]{:S(2)}, u32[]{:S(2)}) %collective-permute-start.24) | collective-permute-done | bytes 262176 | tf_op jit(solution)/shard_map/ppermute | solution.py:485
  128.8 2.7 %collective-permute-done.25.refs_7_ = f32[512,128]{1,0:T(8,128)S(1)} collective-permute-done((f32[512,128]{1,0:T(8,128)}, f32[512,128]{1,0:T(8,128)S(1)}, u32[]{:S(2)}, u32[]{:S(2)}) %collective-permute-start.25) | collective-permute-done | bytes 262176 | tf_op jit(solution)/shard_map/ppermute | solution.py:485
  131.5 0.9 copy-done.3
  132.5 1.4 shard_map.98
  133.9 1.0 collective-permute-start.26
  134.9 14.0 %shard_map.94 = (f32[64,32,128]{2,1,0:T(8,128)S(1)}, f32[64,32,128]{2,1,0:T(8,128)S(1)}, f32[8,512]{1,0:T(8,128)S(1)}) custom-call(f32[65,32,128]{2,1,0:T(8,128)S(1)} %get-tuple-element.58.keep, f32[65,32,128]{2,1,0:T(8,128)S(1)} %collective-permute-done.8.came), custom_call_target="tpu_custom_call" | custom-call | flops 100000000 | bytes 4194304 | tf_op jit(solution)/shard_map/pallas_call | solution.py:434
  148.9 0.0 collective-permute-start.9
  148.9 14.0 %shard_map.99 = (f32[64,32,128]{2,1,0:T(8,128)S(1)}, f32[64,32,128]{2,1,0:T(8,128)S(1)}) custom-call(f32[64,32,128]{2,1,0:T(8,128)S(1)} %get-tuple-element.80.keep, f32[64,32,128]{2,1,0:T(8,128)S(1)} %collective-permute-done.26.came, f32[8,512]{1,0:T(8,128)S(1)} %get-tuple-element.82.refs_0_), custom_call_target="tpu_custom_call" | custom-call | flops 100000000 | bytes 4194304 | tf_op jit(solution)/shard_map/pallas_call | solution.py:434
  162.9 0.5 collective-permute-start.27
  163.4 1.4 shard_map.95
  164.8 3.9 %collective-permute-start.10 = (f32[512,128]{1,0:T(8,128)S(1)}, f32[512,128]{1,0:T(8,128)S(1)}, u32[]{:S(2)}, u32[]{:S(2)}) collective-permute-start(f32[512,128]{1,0:T(8,128)S(1)} %get-tuple-element.62), channel_id=1, source_target_pairs={{0,128},{16,144},{32,160},{48,176},{64,192},{80,208},{96,224},{112... | collective-permute-start | bytes 786440 | tf_op jit(solution)/shard_map/ppermute | solution.py:485
  168.6 3.8 %collective-permute-start.11 = (f32[512,128]{1,0:T(8,128)S(1)}, f32[512,128]{1,0:T(8,128)S(1)}, u32[]{:S(2)}, u32[]{:S(2)}) collective-permute-start(f32[512,128]{1,0:T(8,128)S(1)} %get-tuple-element.63), channel_id=1, source_target_pairs={{0,160},{16,176},{32,192},{48,208},{64,224},{80,240},{96,0},{112,1... | collective-permute-start | bytes 786440 | tf_op jit(solution)/shard_map/ppermute | solution.py:485
  172.5 3.9 %collective-permute-start.13 = (f32[512,128]{1,0:T(8,128)S(1)}, f32[512,128]{1,0:T(8,128)S(1)}, u32[]{:S(2)}, u32[]{:S(2)}) collective-permute-start(f32[512,128]{1,0:T(8,128)S(1)} %get-tuple-element.65), channel_id=1, source_target_pairs={{0,192},{16,208},{32,224},{48,240},{64,0},{80,16},{96,32},{112,48}... | collective-permute-start | bytes 786440 | tf_op jit(solution)/shard_map/ppermute | solution.py:485
  176.4 2.0 collective-permute-done.10.refs_0_
  178.4 2.7 %collective-permute-start.15 = (f32[512,128]{1,0:T(8,128)S(1)}, f32[512,128]{1,0:T(8,128)S(1)}, u32[]{:S(2)}, u32[]{:S(2)}) collective-permute-start(f32[512,128]{1,0:T(8,128)S(1)} %get-tuple-element.67), channel_id=1, source_target_pairs={{0,224},{16,240},{32,0},{48,16},{64,32},{80,48},{96,64},{112,80},{... | collective-permute-start | bytes 786440 | tf_op jit(solution)/shard_map/ppermute | solution.py:485
  181.1 15.8 %collective-permute-done.11.refs_1_ = f32[512,128]{1,0:T(8,128)S(1)} collective-permute-done((f32[512,128]{1,0:T(8,128)S(1)}, f32[512,128]{1,0:T(8,128)S(1)}, u32[]{:S(2)}, u32[]{:S(2)}) %collective-permute-start.11) | collective-permute-done | bytes 262176 | tf_op jit(solution)/shard_map/ppermute | solution.py:485
  196.9 6.6 %collective-permute-start.16 = (f32[512,128]{1,0:T(8,128)S(1)}, f32[512,128]{1,0:T(8,128)S(1)}, u32[]{:S(2)}, u32[]{:S(2)}) collective-permute-start(f32[512,128]{1,0:T(8,128)S(1)} %get-tuple-element.68), channel_id=1, source_target_pairs={{0,32},{16,48},{32,64},{48,80},{64,96},{80,112},{96,128},{112,144}... | collective-permute-start | bytes 786440 | tf_op jit(solution)/shard_map/ppermute | solution.py:485
  203.6 1.4 shard_map.100
  204.9 0.1 collective-permute-start.28
  205.0 6.1 %collective-permute-done.13.refs_3_ = f32[512,128]{1,0:T(8,128)S(1)} collective-permute-done((f32[512,128]{1,0:T(8,128)S(1)}, f32[512,128]{1,0:T(8,128)S(1)}, u32[]{:S(2)}, u32[]{:S(2)}) %collective-permute-start.13) | collective-permute-done | bytes 262176 | tf_op jit(solution)/shard_map/ppermute | solution.py:485
  211.1 4.5 %collective-permute-start.30 = (f32[512,128]{1,0:T(8,128)S(1)}, f32[512,128]{1,0:T(8,128)S(1)}, u32[]{:S(2)}, u32[]{:S(2)}) collective-permute-start(f32[512,128]{1,0:T(8,128)S(1)} %get-tuple-element.88), channel_id=1, source_target_pairs={{0,160},{16,176},{32,192},{48,208},{64,224},{80,240},{96,0},{112,1... | collective-permute-start | bytes 786440 | tf_op jit(solution)/shard_map/ppermute | solution.py:485
  215.6 3.0 %collective-permute-start.31 = (f32[512,128]{1,0:T(8,128)S(1)}, f32[512,128]{1,0:T(8,128)S(1)}, u32[]{:S(2)}, u32[]{:S(2)}) collective-permute-start(f32[512,128]{1,0:T(8,128)S(1)} %get-tuple-element.89), channel_id=1, source_target_pairs={{0,64},{16,80},{32,96},{48,112},{64,128},{80,144},{96,160},{112,17... | collective-permute-start | bytes 786440 | tf_op jit(solution)/shard_map/ppermute | solution.py:485
  218.6 0.6 collective-permute-start.32
  219.2 3.0 %collective-permute-done.28.refs_1_ = f32[512,128]{1,0:T(8,128)S(1)} collective-permute-done((f32[512,128]{1,0:T(8,128)S(1)}, f32[512,128]{1,0:T(8,128)S(1)}, u32[]{:S(2)}, u32[]{:S(2)}) %collective-permute-start.28) | collective-permute-done | bytes 262176 | tf_op jit(solution)/shard_map/ppermute | solution.py:485
  222.2 3.9 %collective-permute-start.33 = (f32[512,128]{1,0:T(8,128)S(1)}, f32[512,128]{1,0:T(8,128)S(1)}, u32[]{:S(2)}, u32[]{:S(2)}) collective-permute-start(f32[512,128]{1,0:T(8,128)S(1)} %get-tuple-element.91), channel_id=1, source_target_pairs={{0,224},{16,240},{32,0},{48,16},{64,32},{80,48},{96,64},{112,80},{... | collective-permute-start | bytes 786440 | tf_op jit(solution)/shard_map/ppermute | solution.py:485
  226.1 20.6 %collective-permute-done.29.refs_3_ = f32[512,128]{1,0:T(8,128)S(1)} collective-permute-done((f32[512,128]{1,0:T(8,128)S(1)}, f32[512,128]{1,0:T(8,128)S(1)}, u32[]{:S(2)}, u32[]{:S(2)}) %collective-permute-start.29) | collective-permute-done | bytes 262176 | tf_op jit(solution)/shard_map/ppermute | solution.py:485
  246.7 1.4 shard_map.96.refs_0_
  248.1 0.9 shard_map.101.refs_0_
  249.1 6.8 %collective-permute-done.31.refs_2_ = f32[512,128]{1,0:T(8,128)S(1)} collective-permute-done((f32[512,128]{1,0:T(8,128)S(1)}, f32[512,128]{1,0:T(8,128)S(1)}, u32[]{:S(2)}, u32[]{:S(2)}) %collective-permute-start.31) | collective-permute-done | bytes 262176 | tf_op jit(solution)/shard_map/ppermute | solution.py:485
  255.9 0.3 collective-permute-done.32.refs_3_
  256.2 0.9 shard_map.102.refs_0_
  257.1 2.9 %collective-permute-done.33.refs_1_ = f32[512,128]{1,0:T(8,128)S(1)} collective-permute-done((f32[512,128]{1,0:T(8,128)S(1)}, f32[512,128]{1,0:T(8,128)S(1)}, u32[]{:S(2)}, u32[]{:S(2)}) %collective-permute-start.33) | collective-permute-done | bytes 262176 | tf_op jit(solution)/shard_map/ppermute | solution.py:485
  260.0 1.5 collective-permute-done.34.refs_2_
  261.5 0.8 shard_map.103
  (36 shorter events, 0.1 us)
Async XLA Ops:
  2.1 39.7 %collective-permute-start.3 = (f32[512,128]{1,0:T(8,128)}, f32[512,128]{1,0:T(8,128)}, u32[]{:S(2)}, u32[]{:S(2)}) collective-permute-start(f32[512,128]{1,0:T(8,128)} %stencil_a1.1), channel_id=1, source_target_pairs={{0,128},{16,144},{32,160},{48,176},{64,192},{80,208},{96,224},{112... | collective-permute-start | bytes 786440 | tf_op jit(solution)/shard_map/ppermute | solution.py:485
  18.2 24.6 %collective-permute-start.17 = (f32[4,4,8,512]{3,2,1,0:T(8,128)}, f32[4,4,8,512]{3,2,1,0:T(8,128)S(1)}, u32[]{:S(2)}, u32[]{:S(2)}) collective-permute-start(f32[4,4,8,512]{3,2,1,0:T(8,128)} %get-tuple-element.70), channel_id=1, source_target_pairs={{0,1},{1,2},{2,3},{3,4},{4,5},{5,6},{6,7},{7,8},{8,9},{9,10},{10,1... | collective-permute-start | bytes 786440 | tf_op jit(solution)/shard_map/ppermute | solution.py:537
  20.7 25.7 %collective-permute-start.2 = (f32[520,128]{1,0:T(8,128)}, f32[520,128]{1,0:T(8,128)S(1)}, u32[]{:S(2)}, u32[]{:S(2)}) collective-permute-start(f32[520,128]{1,0:T(8,128)} %get-tuple-element.53), channel_id=1, source_target_pairs={{0,96},{16,112},{32,128},{48,144},{64,160},{80,176},{96,192},{112,... | collective-permute-start | bytes 798728 | tf_op jit(solution)/shard_map/ppermute | solution.py:485
  22.4 22.9 %collective-permute-start.18 = (f32[4,4,8,512]{3,2,1,0:T(8,128)}, f32[4,4,8,512]{3,2,1,0:T(8,128)S(1)}, u32[]{:S(2)}, u32[]{:S(2)}) collective-permute-start(f32[4,4,8,512]{3,2,1,0:T(8,128)} %get-tuple-element.71), channel_id=1, source_target_pairs={{1,0},{2,1},{3,2},{4,3},{5,4},{6,5},{7,6},{8,7},{9,8},{10,9},{11,1... | collective-permute-start | bytes 786440 | tf_op jit(solution)/shard_map/ppermute | solution.py:538
  25.2 16.6 %collective-permute-start.7 = (f32[8,128]{1,0:T(8,128)}, f32[8,128]{1,0:T(8,128)S(1)}, u32[]{:S(2)}, u32[]{:S(2)}) collective-permute-start(f32[8,128]{1,0:T(8,128)} %get-tuple-element.57), channel_id=1, source_target_pairs={{0,128},{16,144},{32,160},{48,176},{64,192},{80,208},{96,224},{112... | collective-permute-start | bytes 12296 | tf_op jit(solution)/shard_map/ppermute | solution.py:485
  41.8 4.6 %copy-start.4 = (f32[8,128]{1,0:T(8,128)}, f32[8,128]{1,0:T(8,128)S(1)}, u32[]{:S(2)}) copy-start(f32[8,128]{1,0:T(8,128)S(1)} %collective-permute-done.7.refs_8_) | copy-start | bytes 12292
  41.8 19.2 %collective-permute-start.4 = (f32[520,128]{1,0:T(8,128)}, f32[520,128]{1,0:T(8,128)}, u32[]{:S(2)}, u32[]{:S(2)}) collective-permute-start(f32[520,128]{1,0:T(8,128)} %get-tuple-element.54), channel_id=1, source_target_pairs={{0,160},{16,176},{32,192},{48,208},{64,224},{80,240},{96,0},{112,1... | collective-permute-start | bytes 798728 | tf_op jit(solution)/shard_map/ppermute | solution.py:485
  41.8 19.2 %collective-permute-start = (f32[520,128]{1,0:T(8,128)}, f32[520,128]{1,0:T(8,128)}, u32[]{:S(2)}, u32[]{:S(2)}) collective-permute-start(f32[520,128]{1,0:T(8,128)} %get-tuple-element.51), channel_id=1, source_target_pairs={{0,32},{16,48},{32,64},{48,80},{64,96},{80,112},{96,128},{112,144}... | collective-permute-start | bytes 798728 | tf_op jit(solution)/shard_map/ppermute | solution.py:485
  42.8 4.3 %copy-start.6 = (f32[4,4,8,512]{3,2,1,0:T(8,128)}, f32[4,4,8,512]{3,2,1,0:T(8,128)S(1)}, u32[]{:S(2)}) copy-start(f32[4,4,8,512]{3,2,1,0:T(8,128)S(1)} %collective-permute-done.17.refs_0_) | copy-start | bytes 786436
  42.8 21.7 %collective-permute-start.1 = (f32[520,128]{1,0:T(8,128)}, f32[520,128]{1,0:T(8,128)}, u32[]{:S(2)}, u32[]{:S(2)}) collective-permute-start(f32[520,128]{1,0:T(8,128)} %get-tuple-element.52), channel_id=1, source_target_pairs={{0,64},{16,80},{32,96},{48,112},{64,128},{80,144},{96,160},{112,17... | collective-permute-start | bytes 798728 | tf_op jit(solution)/shard_map/ppermute | solution.py:485
  45.3 1.8 copy-start.7
  45.3 23.3 %collective-permute-start.5 = (f32[520,128]{1,0:T(8,128)}, f32[520,128]{1,0:T(8,128)}, u32[]{:S(2)}, u32[]{:S(2)}) collective-permute-start(f32[520,128]{1,0:T(8,128)} %get-tuple-element.55), channel_id=1, source_target_pairs={{0,192},{16,208},{32,224},{48,240},{64,0},{80,16},{96,32},{112,48}... | collective-permute-start | bytes 798728 | tf_op jit(solution)/shard_map/ppermute | solution.py:485
  46.4 0.7 copy-start.1
  47.1 29.8 %collective-permute-start.6 = (f32[520,128]{1,0:T(8,128)}, f32[520,128]{1,0:T(8,128)}, u32[]{:S(2)}, u32[]{:S(2)}) collective-permute-start(f32[520,128]{1,0:T(8,128)} %get-tuple-element.56), channel_id=1, source_target_pairs={{0,224},{16,240},{32,0},{48,16},{64,32},{80,48},{96,64},{112,80},{... | collective-permute-start | bytes 798728 | tf_op jit(solution)/shard_map/ppermute | solution.py:485
  61.0 25.2 %collective-permute-start.19 = (f32[512,128]{1,0:T(8,128)}, f32[512,128]{1,0:T(8,128)S(1)}, u32[]{:S(2)}, u32[]{:S(2)}) collective-permute-start(f32[512,128]{1,0:T(8,128)} %get-tuple-element.73), channel_id=1, source_target_pairs={{0,32},{16,48},{32,64},{48,80},{64,96},{80,112},{96,128},{112,144}... | collective-permute-start | bytes 786440 | tf_op jit(solution)/shard_map/ppermute | solution.py:485
  61.0 27.1 %collective-permute-start.20 = (f32[512,128]{1,0:T(8,128)}, f32[512,128]{1,0:T(8,128)S(1)}, u32[]{:S(2)}, u32[]{:S(2)}) collective-permute-start(f32[512,128]{1,0:T(8,128)} %get-tuple-element.74), channel_id=1, source_target_pairs={{0,64},{16,80},{32,96},{48,112},{64,128},{80,144},{96,160},{112,17... | collective-permute-start | bytes 786440 | tf_op jit(solution)/shard_map/ppermute | solution.py:485
  64.5 26.9 %collective-permute-start.21 = (f32[512,128]{1,0:T(8,128)}, f32[512,128]{1,0:T(8,128)S(1)}, u32[]{:S(2)}, u32[]{:S(2)}) collective-permute-start(f32[512,128]{1,0:T(8,128)} %get-tuple-element.75), channel_id=1, source_target_pairs={{0,96},{16,112},{32,128},{48,144},{64,160},{80,176},{96,192},{112,... | collective-permute-start | bytes 786440 | tf_op jit(solution)/shard_map/ppermute | solution.py:485
  76.9 1.0 copy-start
  77.9 1.0 copy-start.2
  78.8 0.7 copy-start.5
  82.2 52.7 %collective-permute-start.8 = (f32[65,32,128]{2,1,0:T(8,128)S(1)}, f32[65,32,128]{2,1,0:T(8,128)S(1)}, u32[]{:S(2)}, u32[]{:S(2)}) collective-permute-start(f32[65,32,128]{2,1,0:T(8,128)S(1)} %get-tuple-element.59), channel_id=1, source_target_pairs={{0,16},{16,0},{32,48},{48,32},{64,80},{80,64},{96,112},{112,96},{1... | collective-permute-start | bytes 3194888 | tf_op jit(solution)/shard_map/ppermute | solution.py:505
  84.4 22.0 %collective-permute-start.22 = (f32[512,128]{1,0:T(8,128)}, f32[512,128]{1,0:T(8,128)S(1)}, u32[]{:S(2)}, u32[]{:S(2)}) collective-permute-start(f32[512,128]{1,0:T(8,128)} %get-tuple-element.76), channel_id=1, source_target_pairs={{0,128},{16,144},{32,160},{48,176},{64,192},{80,208},{96,224},{112... | collective-permute-start | bytes 786440 | tf_op jit(solution)/shard_map/ppermute | solution.py:485
  86.1 31.3 %collective-permute-start.23 = (f32[512,128]{1,0:T(8,128)}, f32[512,128]{1,0:T(8,128)S(1)}, u32[]{:S(2)}, u32[]{:S(2)}) collective-permute-start(f32[512,128]{1,0:T(8,128)} %get-tuple-element.77), channel_id=1, source_target_pairs={{0,160},{16,176},{32,192},{48,208},{64,224},{80,240},{96,0},{112,1... | collective-permute-start | bytes 786440 | tf_op jit(solution)/shard_map/ppermute | solution.py:485
  88.0 40.8 %collective-permute-start.24 = (f32[512,128]{1,0:T(8,128)}, f32[512,128]{1,0:T(8,128)S(1)}, u32[]{:S(2)}, u32[]{:S(2)}) collective-permute-start(f32[512,128]{1,0:T(8,128)} %get-tuple-element.78), channel_id=1, source_target_pairs={{0,192},{16,208},{32,224},{48,240},{64,0},{80,16},{96,32},{112,48}... | collective-permute-start | bytes 786440 | tf_op jit(solution)/shard_map/ppermute | solution.py:485
  91.4 40.1 %collective-permute-start.25 = (f32[512,128]{1,0:T(8,128)}, f32[512,128]{1,0:T(8,128)S(1)}, u32[]{:S(2)}, u32[]{:S(2)}) collective-permute-start(f32[512,128]{1,0:T(8,128)} %get-tuple-element.79), channel_id=1, source_target_pairs={{0,224},{16,240},{32,0},{48,16},{64,32},{80,48},{96,64},{112,80},{... | collective-permute-start | bytes 786440 | tf_op jit(solution)/shard_map/ppermute | solution.py:485
  131.5 1.0 copy-start.3
  133.9 15.1 %collective-permute-start.26 = (f32[64,32,128]{2,1,0:T(8,128)S(1)}, f32[64,32,128]{2,1,0:T(8,128)S(1)}, u32[]{:S(2)}, u32[]{:S(2)}) collective-permute-start(f32[64,32,128]{2,1,0:T(8,128)S(1)} %get-tuple-element.81), channel_id=1, source_target_pairs={{0,16},{16,0},{32,48},{48,32},{64,80},{80,64},{96,112},{112,96},{1... | collective-permute-start | bytes 3145736 | tf_op jit(solution)/shard_map/ppermute | solution.py:505
  148.9 14.5 %collective-permute-start.9 = (f32[64,32,128]{2,1,0:T(8,128)S(1)}, f32[64,32,128]{2,1,0:T(8,128)S(1)}, u32[]{:S(2)}, u32[]{:S(2)}) collective-permute-start(f32[64,32,128]{2,1,0:T(8,128)S(1)} %get-tuple-element.61), channel_id=1, source_target_pairs={{0,16},{16,0},{32,48},{48,32},{64,80},{80,64},{96,112},{112,96},{1... | collective-permute-start | bytes 3145736 | tf_op jit(solution)/shard_map/ppermute | solution.py:505
  162.9 13.5 %collective-permute-start.27 = (f32[64,32,128]{2,1,0:T(8,128)S(1)}, f32[64,32,128]{2,1,0:T(8,128)S(1)}, u32[]{:S(2)}, u32[]{:S(2)}) collective-permute-start(f32[64,32,128]{2,1,0:T(8,128)S(1)} %get-tuple-element.84), channel_id=1, source_target_pairs={{0,16},{16,0},{32,48},{48,32},{64,80},{80,64},{96,112},{112,96},{1... | collective-permute-start | bytes 3145736 | tf_op jit(solution)/shard_map/ppermute | solution.py:505
  164.8 13.6 %collective-permute-start.10 = (f32[512,128]{1,0:T(8,128)S(1)}, f32[512,128]{1,0:T(8,128)S(1)}, u32[]{:S(2)}, u32[]{:S(2)}) collective-permute-start(f32[512,128]{1,0:T(8,128)S(1)} %get-tuple-element.62), channel_id=1, source_target_pairs={{0,128},{16,144},{32,160},{48,176},{64,192},{80,208},{96,224},{112... | collective-permute-start | bytes 786440 | tf_op jit(solution)/shard_map/ppermute | solution.py:485
  168.6 28.3 %collective-permute-start.11 = (f32[512,128]{1,0:T(8,128)S(1)}, f32[512,128]{1,0:T(8,128)S(1)}, u32[]{:S(2)}, u32[]{:S(2)}) collective-permute-start(f32[512,128]{1,0:T(8,128)S(1)} %get-tuple-element.63), channel_id=1, source_target_pairs={{0,160},{16,176},{32,192},{48,208},{64,224},{80,240},{96,0},{112,1... | collective-permute-start | bytes 786440 | tf_op jit(solution)/shard_map/ppermute | solution.py:485
  172.4 32.5 %collective-permute-start.12 = (f32[512,128]{1,0:T(8,128)S(1)}, f32[512,128]{1,0:T(8,128)S(1)}, u32[]{:S(2)}, u32[]{:S(2)}) collective-permute-start(f32[512,128]{1,0:T(8,128)S(1)} %get-tuple-element.64), channel_id=1, source_target_pairs={{0,96},{16,112},{32,128},{48,144},{64,160},{80,176},{96,192},{112,... | collective-permute-start | bytes 786440 | tf_op jit(solution)/shard_map/ppermute | solution.py:485
  172.5 38.7 %collective-permute-start.13 = (f32[512,128]{1,0:T(8,128)S(1)}, f32[512,128]{1,0:T(8,128)S(1)}, u32[]{:S(2)}, u32[]{:S(2)}) collective-permute-start(f32[512,128]{1,0:T(8,128)S(1)} %get-tuple-element.65), channel_id=1, source_target_pairs={{0,192},{16,208},{32,224},{48,240},{64,0},{80,16},{96,32},{112,48}... | collective-permute-start | bytes 786440 | tf_op jit(solution)/shard_map/ppermute | solution.py:485
  176.4 34.7 %collective-permute-start.14 = (f32[512,128]{1,0:T(8,128)S(1)}, f32[512,128]{1,0:T(8,128)S(1)}, u32[]{:S(2)}, u32[]{:S(2)}) collective-permute-start(f32[512,128]{1,0:T(8,128)S(1)} %get-tuple-element.66), channel_id=1, source_target_pairs={{0,64},{16,80},{32,96},{48,112},{64,128},{80,144},{96,160},{112,17... | collective-permute-start | bytes 786440 | tf_op jit(solution)/shard_map/ppermute | solution.py:485
  178.4 37.2 %collective-permute-start.15 = (f32[512,128]{1,0:T(8,128)S(1)}, f32[512,128]{1,0:T(8,128)S(1)}, u32[]{:S(2)}, u32[]{:S(2)}) collective-permute-start(f32[512,128]{1,0:T(8,128)S(1)} %get-tuple-element.67), channel_id=1, source_target_pairs={{0,224},{16,240},{32,0},{48,16},{64,32},{80,48},{96,64},{112,80},{... | collective-permute-start | bytes 786440 | tf_op jit(solution)/shard_map/ppermute | solution.py:485
  196.9 21.7 %collective-permute-start.16 = (f32[512,128]{1,0:T(8,128)S(1)}, f32[512,128]{1,0:T(8,128)S(1)}, u32[]{:S(2)}, u32[]{:S(2)}) collective-permute-start(f32[512,128]{1,0:T(8,128)S(1)} %get-tuple-element.68), channel_id=1, source_target_pairs={{0,32},{16,48},{32,64},{48,80},{64,96},{80,112},{96,128},{112,144}... | collective-permute-start | bytes 786440 | tf_op jit(solution)/shard_map/ppermute | solution.py:485
  204.9 17.3 %collective-permute-start.28 = (f32[512,128]{1,0:T(8,128)S(1)}, f32[512,128]{1,0:T(8,128)S(1)}, u32[]{:S(2)}, u32[]{:S(2)}) collective-permute-start(f32[512,128]{1,0:T(8,128)S(1)} %get-tuple-element.85), channel_id=1, source_target_pairs={{0,128},{16,144},{32,160},{48,176},{64,192},{80,208},{96,224},{112... | collective-permute-start | bytes 786440 | tf_op jit(solution)/shard_map/ppermute | solution.py:485
  211.1 35.6 %collective-permute-start.29 = (f32[512,128]{1,0:T(8,128)S(1)}, f32[512,128]{1,0:T(8,128)S(1)}, u32[]{:S(2)}, u32[]{:S(2)}) collective-permute-start(f32[512,128]{1,0:T(8,128)S(1)} %get-tuple-element.87), channel_id=1, source_target_pairs={{0,96},{16,112},{32,128},{48,144},{64,160},{80,176},{96,192},{112,... | collective-permute-start | bytes 786440 | tf_op jit(solution)/shard_map/ppermute | solution.py:485
  211.1 38.0 %collective-permute-start.30 = (f32[512,128]{1,0:T(8,128)S(1)}, f32[512,128]{1,0:T(8,128)S(1)}, u32[]{:S(2)}, u32[]{:S(2)}) collective-permute-start(f32[512,128]{1,0:T(8,128)S(1)} %get-tuple-element.88), channel_id=1, source_target_pairs={{0,160},{16,176},{32,192},{48,208},{64,224},{80,240},{96,0},{112,1... | collective-permute-start | bytes 786440 | tf_op jit(solution)/shard_map/ppermute | solution.py:485
  215.6 40.3 %collective-permute-start.31 = (f32[512,128]{1,0:T(8,128)S(1)}, f32[512,128]{1,0:T(8,128)S(1)}, u32[]{:S(2)}, u32[]{:S(2)}) collective-permute-start(f32[512,128]{1,0:T(8,128)S(1)} %get-tuple-element.89), channel_id=1, source_target_pairs={{0,64},{16,80},{32,96},{48,112},{64,128},{80,144},{96,160},{112,17... | collective-permute-start | bytes 786440 | tf_op jit(solution)/shard_map/ppermute | solution.py:485
  218.6 37.6 %collective-permute-start.32 = (f32[512,128]{1,0:T(8,128)S(1)}, f32[512,128]{1,0:T(8,128)S(1)}, u32[]{:S(2)}, u32[]{:S(2)}) collective-permute-start(f32[512,128]{1,0:T(8,128)S(1)} %get-tuple-element.90), channel_id=1, source_target_pairs={{0,192},{16,208},{32,224},{48,240},{64,0},{80,16},{96,32},{112,48}... | collective-permute-start | bytes 786440 | tf_op jit(solution)/shard_map/ppermute | solution.py:485
  222.2 37.8 %collective-permute-start.33 = (f32[512,128]{1,0:T(8,128)S(1)}, f32[512,128]{1,0:T(8,128)S(1)}, u32[]{:S(2)}, u32[]{:S(2)}) collective-permute-start(f32[512,128]{1,0:T(8,128)S(1)} %get-tuple-element.91), channel_id=1, source_target_pairs={{0,224},{16,240},{32,0},{48,16},{64,32},{80,48},{96,64},{112,80},{... | collective-permute-start | bytes 786440 | tf_op jit(solution)/shard_map/ppermute | solution.py:485
  246.7 14.8 %collective-permute-start.34 = (f32[512,128]{1,0:T(8,128)S(1)}, f32[512,128]{1,0:T(8,128)S(1)}, u32[]{:S(2)}, u32[]{:S(2)}) collective-permute-start(f32[512,128]{1,0:T(8,128)S(1)} %get-tuple-element.92), channel_id=1, source_target_pairs={{0,32},{16,48},{32,64},{48,80},{64,96},{80,112},{96,128},{112,144}... | collective-permute-start | bytes 786440 | tf_op jit(solution)/shard_map/ppermute | solution.py:485

commit v4 on v3

--- a/solution.py
+++ b/solution.py
@@ -68,7 +68,7 @@
             out[pl.ds(at, 8), :] = res[:, q * 128 : (q + 1) * 128]
 
 
-def first_kernel(spread_in, mix_in, x, out, win, buf, spread, mix, in_sems, out_sems, scalar_sems):
+def first_kernel(spread_in, mix_in, x, out, win, spread, mix, in_sems, scalar_sems):
     chip = lax.axis_index("mem") // 2
     start = pl.multiple_of(base_row(0, lax.rem(chip + FIRST, CHIPS)) - 8, 8)
     copies = [
@@ -82,34 +82,25 @@
         copy.start()
     for copy in scalars:
         copy.wait()
-    done = []
     for m in range(SHARE):
         copies[m].wait()
-        stencil_tiles(0, win, m, 8, 0, 16, None, None, None, spread, mix, buf)
-        rows = pl.ds(m * 128, 128)
-        copy = pltpu.make_async_copy(buf.at[rows, :], out.at[rows, :], out_sems.at[m])
-        copy.start()
-        done.append(copy)
-    for copy in done:
-        copy.wait()
+        stencil_tiles(0, win, m, 8, 0, 16, None, None, None, spread, mix, out)
 
 
 def first_stencil(spread, mix, x):
     return pl.pallas_call(
         first_kernel,
         in_specs=[hbm()] * 3,
-        out_specs=hbm(),
+        out_specs=vmem(),
         out_shape=jax.ShapeDtypeStruct((BLOCK, 128), F32),
         scratch_shapes=[
             pltpu.VMEM((SHARE, VARS, 24, WIDTH), F32),
-            pltpu.VMEM((BLOCK, 128), F32),
             pltpu.SMEM((VARS,), F32),
             pltpu.SMEM((VARS, VARS), F32),
             pltpu.SemaphoreType.DMA((SHARE,)),
-            pltpu.SemaphoreType.DMA((SHARE,)),
             pltpu.SemaphoreType.DMA((2,)),
         ],
-        compiler_params=params(),
+        compiler_params=params(8),
         cost_estimate=pl.CostEstimate(flops=2_500_000, bytes_accessed=MB, transcendentals=0),
         name="stencil_a1",
     )(spread, mix, x)
@@ -211,7 +202,7 @@
             pltpu.SemaphoreType.DMA((n + 2,)),
             pltpu.SemaphoreType.DMA((2,)),
         ],
-        compiler_params=params(),
+        compiler_params=params(24),
         cost_estimate=pl.CostEstimate(flops=2_500_000 * n, bytes_accessed=n * MB, transcendentals=0),
     )(*extra, spread, mix, x)
     return dict(zip(dists, res[:n])), res[n:]
@@ -516,7 +507,9 @@
     taper_index,
     taper_factors,
 ):
-    x = prior_ensemble
+    x, spreading_factor, tendency_matrix = [
+        pltpu.with_memory_space_constraint(a, pltpu.HBM) for a in (prior_ensemble, spreading_factor, tendency_matrix)
+    ]
     physics = (spreading_factor, tendency_matrix, x)
 
     obs = (

time: 264 us -> 255 us (0.966)
  Pallas kernels: 57.1 us -> 49.6 us
  local copies, waits for them, and re-layouts: 4.24 us -> 0.02 us
  starting transfers between devices: 74 us -> 77 us
    pallas_call x3, Pallas kernels: 16.2 us -> 10.6 us  [stencil(): pl.pallas_call(functools.partial(stencil_kernel, chunk, dists, part), in_...]
    unnamed x16 -> x12, local copies, waits for them, and re-layouts: 4.24 us -> 0.02 us
  transfers between devices with their start and end apart: 35 -> 35, of which waited for: 17 -> 19; matrix products, arithmetic and copies ran while one was open for 0% -> 0% of each run, Pallas kernels for 21% -> 19%
where the time goes in v4:
time: 255 us; the launch traced here: 252 us
  waiting for transfers between devices  125 us (49%)
  starting transfers between devices  77 us (30%)
  Pallas kernels  49.6 us (19%)
    ppermute x29, waiting for transfers between devices, hop(): return lax.ppermute(block, 'mem', [(i, (i + 2 * d) % n) for i in range(n)])  125 us
    ppermute x29, starting transfers between devices, hop(): return lax.ppermute(block, 'mem', [(i, (i + 2 * d) % n) for i in range(n)])  66.5 us
    pallas_call x2, Pallas kernels, analysis(): pl.pallas_call(functools.partial(analysis_kernel, chunk), in_specs=[vmem(...  27.9 us
    pallas_call x3, Pallas kernels, stencil(): pl.pallas_call(functools.partial(stencil_kernel, chunk, dists, part), in_...  10.6 us
    ppermute x4, starting transfers between devices, swap(): return lax.ppermute(x, 'mem', [(i, i ^ 1) for i in range(2 * CHIPS)])  5.23 us
  transfers between devices with their start and end apart: 35, of which 19 were waited for; matrix products, arithmetic and copies ran while one was open for 0% of the time, Pallas kernels for 19%

profile of v4, /device:TPU:29, one launch (start us, length us, event | category | flops | bytes accessed | tf_op | source)
XLA Modules:
  0.0 251.6 jit_solution(18329831613694849375)
XLA Ops:
  0.0 1.5 stencil_a1.1
  1.5 7.0 %collective-permute-start.3 = (f32[512,128]{1,0:T(8,128)S(1)}, f32[512,128]{1,0:T(8,128)S(1)}, u32[]{:S(2)}, u32[]{:S(2)}) collective-permute-start(f32[512,128]{1,0:T(8,128)S(1)} %stencil_a1.1), channel_id=1, source_target_pairs={{0,128},{16,144},{32,160},{48,176},{64,192},{80,208},{96,224},{112... | collective-permute-start | bytes 786440 | tf_op jit(solution)/shard_map/ppermute | solution.py:476
  8.6 2.3 shard_map.91
  10.9 3.5 %shard_map.92 = (f32[520,128]{1,0:T(8,128)S(1)}, f32[520,128]{1,0:T(8,128)S(1)}, f32[520,128]{1,0:T(8,128)S(1)}, f32[520,128]{1,0:T(8,128)S(1)}, f32[520,128]{1,...) custom-call(f32[8,1024]{1,0:T(8,128)S(1)} %get-tuple-element.49.refs_0_, f32[4]{0:T(128)} %refs_2_.5, ...), custom_call_target="tpu_custom_call" | custom-call | flops 12500000 | bytes 5242880 | tf_op jit(solution)/shard_map/pallas_call | solution.py:193
  14.3 2.5 collective-permute-start.17
  16.8 1.7 collective-permute-start.2
  18.5 2.8 %collective-permute-start.18 = (f32[4,4,8,512]{3,2,1,0:T(8,128)S(1)}, f32[4,4,8,512]{3,2,1,0:T(8,128)S(1)}, u32[]{:S(2)}, u32[]{:S(2)}) collective-permute-start(f32[4,4,8,512]{3,2,1,0:T(8,128)S(1)} %get-tuple-element.71), channel_id=1, source_target_pairs={{1,0},{2,1},{3,2},{4,3},{5,4},{6,5},{7,6},{8,7},{9,8},{10,9},{11,1... | collective-permute-start | bytes 786440 | tf_op jit(solution)/shard_map/ppermute | solution.py:531
  21.3 1.2 collective-permute-start.7
  22.6 12.0 %collective-permute-done.7.refs_8_ = f32[8,128]{1,0:T(8,128)S(1)} collective-permute-done((f32[8,128]{1,0:T(8,128)S(1)}, f32[8,128]{1,0:T(8,128)S(1)}, u32[]{:S(2)}, u32[]{:S(2)}) %collective-permute-start.7) | collective-permute-done | bytes 4128 | tf_op jit(solution)/shard_map/ppermute | solution.py:476
  34.6 0.0 collective-permute-start.4
  34.6 0.0 collective-permute-done.3.refs_4_
  34.6 3.5 %collective-permute-start = (f32[520,128]{1,0:T(8,128)S(1)}, f32[520,128]{1,0:T(8,128)S(1)}, u32[]{:S(2)}, u32[]{:S(2)}) collective-permute-start(f32[520,128]{1,0:T(8,128)S(1)} %get-tuple-element.51), channel_id=1, source_target_pairs={{0,32},{16,48},{32,64},{48,80},{64,96},{80,112},{96,128},{112,144}... | collective-permute-start | bytes 798728 | tf_op jit(solution)/shard_map/ppermute | solution.py:476
  38.1 0.0 collective-permute-start.1
  38.1 3.8 %collective-permute-start.5 = (f32[520,128]{1,0:T(8,128)S(1)}, f32[520,128]{1,0:T(8,128)S(1)}, u32[]{:S(2)}, u32[]{:S(2)}) collective-permute-start(f32[520,128]{1,0:T(8,128)S(1)} %get-tuple-element.55), channel_id=1, source_target_pairs={{0,192},{16,208},{32,224},{48,240},{64,0},{80,16},{96,32},{112,48}... | collective-permute-start | bytes 798728 | tf_op jit(solution)/shard_map/ppermute | solution.py:476
  41.9 1.2 collective-permute-start.6
  43.1 4.8 %shard_map.97 = (f32[512,128]{1,0:T(8,128)S(1)}, f32[512,128]{1,0:T(8,128)S(1)}, f32[512,128]{1,0:T(8,128)S(1)}, f32[512,128]{1,0:T(8,128)S(1)}, f32[512,128]{1,...) custom-call(f32[4,4,8,512]{3,2,1,0:T(8,128)S(1)} %collective-permute-done.17.refs_0_, ...), custom_call_target="tpu_custom_call" | custom-call | flops 20000000 | bytes 8388608 | tf_op jit(solution)/shard_map/pallas_call | solution.py:193
  47.9 4.0 %collective-permute-start.19 = (f32[512,128]{1,0:T(8,128)S(1)}, f32[512,128]{1,0:T(8,128)S(1)}, u32[]{:S(2)}, u32[]{:S(2)}) collective-permute-start(f32[512,128]{1,0:T(8,128)S(1)} %get-tuple-element.73), channel_id=1, source_target_pairs={{0,32},{16,48},{32,64},{48,80},{64,96},{80,112},{96,128},{112,144}... | collective-permute-start | bytes 786440 | tf_op jit(solution)/shard_map/ppermute | solution.py:476
  51.9 3.5 %collective-permute-done.1.refs_2_ = f32[520,128]{1,0:T(8,128)S(1)} collective-permute-done((f32[520,128]{1,0:T(8,128)S(1)}, f32[520,128]{1,0:T(8,128)S(1)}, u32[]{:S(2)}, u32[]{:S(2)}) %collective-permute-start.1) | collective-permute-done | bytes 266272 | tf_op jit(solution)/shard_map/ppermute | solution.py:476
  55.4 0.9 collective-permute-start.21
  56.3 2.3 collective-permute-done.5.refs_6_
  58.6 8.9 %collective-permute-done.6.refs_7_ = f32[520,128]{1,0:T(8,128)S(1)} collective-permute-done((f32[520,128]{1,0:T(8,128)S(1)}, f32[520,128]{1,0:T(8,128)S(1)}, u32[]{:S(2)}, u32[]{:S(2)}) %collective-permute-start.6) | collective-permute-done | bytes 266272 | tf_op jit(solution)/shard_map/ppermute | solution.py:476
  67.5 1.4 shard_map.93
  68.9 3.6 %collective-permute-start.8 = (f32[65,32,128]{2,1,0:T(8,128)S(1)}, f32[65,32,128]{2,1,0:T(8,128)S(1)}, u32[]{:S(2)}, u32[]{:S(2)}) collective-permute-start(f32[65,32,128]{2,1,0:T(8,128)S(1)} %get-tuple-element.59), channel_id=1, source_target_pairs={{0,16},{16,0},{32,48},{48,32},{64,80},{80,64},{96,112},{112,96},{1... | collective-permute-start | bytes 3194888 | tf_op jit(solution)/shard_map/ppermute | solution.py:496
  72.5 3.4 %collective-permute-start.22 = (f32[512,128]{1,0:T(8,128)S(1)}, f32[512,128]{1,0:T(8,128)S(1)}, u32[]{:S(2)}, u32[]{:S(2)}) collective-permute-start(f32[512,128]{1,0:T(8,128)S(1)} %get-tuple-element.76), channel_id=1, source_target_pairs={{0,128},{16,144},{32,160},{48,176},{64,192},{80,208},{96,224},{112... | collective-permute-start | bytes 786440 | tf_op jit(solution)/shard_map/ppermute | solution.py:476
  76.0 1.8 collective-permute-start.23
  77.8 2.2 collective-permute-start.24
  80.0 4.2 %collective-permute-done.21.refs_3_ = f32[512,128]{1,0:T(8,128)S(1)} collective-permute-done((f32[512,128]{1,0:T(8,128)S(1)}, f32[512,128]{1,0:T(8,128)S(1)}, u32[]{:S(2)}, u32[]{:S(2)}) %collective-permute-start.21) | collective-permute-done | bytes 262176 | tf_op jit(solution)/shard_map/ppermute | solution.py:476
  84.2 5.1 %collective-permute-done.22.refs_4_ = f32[512,128]{1,0:T(8,128)S(1)} collective-permute-done((f32[512,128]{1,0:T(8,128)S(1)}, f32[512,128]{1,0:T(8,128)S(1)}, u32[]{:S(2)}, u32[]{:S(2)}) %collective-permute-start.22) | collective-permute-done | bytes 262176 | tf_op jit(solution)/shard_map/ppermute | solution.py:476
  89.4 14.9 %collective-permute-done.23.refs_5_ = f32[512,128]{1,0:T(8,128)S(1)} collective-permute-done((f32[512,128]{1,0:T(8,128)S(1)}, f32[512,128]{1,0:T(8,128)S(1)}, u32[]{:S(2)}, u32[]{:S(2)}) %collective-permute-start.23) | collective-permute-done | bytes 262176 | tf_op jit(solution)/shard_map/ppermute | solution.py:476
  104.3 13.9 %collective-permute-done.24.refs_6_ = f32[512,128]{1,0:T(8,128)S(1)} collective-permute-done((f32[512,128]{1,0:T(8,128)S(1)}, f32[512,128]{1,0:T(8,128)S(1)}, u32[]{:S(2)}, u32[]{:S(2)}) %collective-permute-start.24) | collective-permute-done | bytes 262176 | tf_op jit(solution)/shard_map/ppermute | solution.py:476
  118.1 4.2 %collective-permute-done.25.refs_7_ = f32[512,128]{1,0:T(8,128)S(1)} collective-permute-done((f32[512,128]{1,0:T(8,128)S(1)}, f32[512,128]{1,0:T(8,128)S(1)}, u32[]{:S(2)}, u32[]{:S(2)}) %collective-permute-start.25) | collective-permute-done | bytes 262176 | tf_op jit(solution)/shard_map/ppermute | solution.py:476
  122.4 1.4 shard_map.98
  123.7 1.0 collective-permute-start.26
  124.8 14.0 %shard_map.94 = (f32[64,32,128]{2,1,0:T(8,128)S(1)}, f32[64,32,128]{2,1,0:T(8,128)S(1)}, f32[8,512]{1,0:T(8,128)S(1)}) custom-call(f32[65,32,128]{2,1,0:T(8,128)S(1)} %get-tuple-element.58.keep, f32[65,32,128]{2,1,0:T(8,128)S(1)} %collective-permute-done.8.came), custom_call_target="tpu_custom_call" | custom-call | flops 100000000 | bytes 4194304 | tf_op jit(solution)/shard_map/pallas_call | solution.py:425
  138.8 0.0 collective-permute-start.9
  138.8 14.0 %shard_map.99 = (f32[64,32,128]{2,1,0:T(8,128)S(1)}, f32[64,32,128]{2,1,0:T(8,128)S(1)}) custom-call(f32[64,32,128]{2,1,0:T(8,128)S(1)} %get-tuple-element.80.keep, f32[64,32,128]{2,1,0:T(8,128)S(1)} %collective-permute-done.26.came, f32[8,512]{1,0:T(8,128)S(1)} %get-tuple-element.82.refs_0_), custom_call_target="tpu_custom_call" | custom-call | flops 100000000 | bytes 4194304 | tf_op jit(solution)/shard_map/pallas_call | solution.py:425
  152.8 0.5 collective-permute-start.27
  153.3 1.4 shard_map.95
  154.6 2.6 %collective-permute-start.10 = (f32[512,128]{1,0:T(8,128)S(1)}, f32[512,128]{1,0:T(8,128)S(1)}, u32[]{:S(2)}, u32[]{:S(2)}) collective-permute-start(f32[512,128]{1,0:T(8,128)S(1)} %get-tuple-element.62), channel_id=1, source_target_pairs={{0,128},{16,144},{32,160},{48,176},{64,192},{80,208},{96,224},{112... | collective-permute-start | bytes 786440 | tf_op jit(solution)/shard_map/ppermute | solution.py:476
  157.2 3.2 %collective-permute-start.11 = (f32[512,128]{1,0:T(8,128)S(1)}, f32[512,128]{1,0:T(8,128)S(1)}, u32[]{:S(2)}, u32[]{:S(2)}) collective-permute-start(f32[512,128]{1,0:T(8,128)S(1)} %get-tuple-element.63), channel_id=1, source_target_pairs={{0,160},{16,176},{32,192},{48,208},{64,224},{80,240},{96,0},{112,1... | collective-permute-start | bytes 786440 | tf_op jit(solution)/shard_map/ppermute | solution.py:476
  160.4 0.1 collective-permute-start.12
  160.5 3.5 %collective-permute-start.13 = (f32[512,128]{1,0:T(8,128)S(1)}, f32[512,128]{1,0:T(8,128)S(1)}, u32[]{:S(2)}, u32[]{:S(2)}) collective-permute-start(f32[512,128]{1,0:T(8,128)S(1)} %get-tuple-element.65), channel_id=1, source_target_pairs={{0,192},{16,208},{32,224},{48,240},{64,0},{80,16},{96,32},{112,48}... | collective-permute-start | bytes 786440 | tf_op jit(solution)/shard_map/ppermute | solution.py:476
  164.0 5.2 %collective-permute-done.10.refs_0_ = f32[512,128]{1,0:T(8,128)S(1)} collective-permute-done((f32[512,128]{1,0:T(8,128)S(1)}, f32[512,128]{1,0:T(8,128)S(1)}, u32[]{:S(2)}, u32[]{:S(2)}) %collective-permute-start.10) | collective-permute-done | bytes 262176 | tf_op jit(solution)/shard_map/ppermute | solution.py:476
  169.2 5.8 %collective-permute-start.15 = (f32[512,128]{1,0:T(8,128)S(1)}, f32[512,128]{1,0:T(8,128)S(1)}, u32[]{:S(2)}, u32[]{:S(2)}) collective-permute-start(f32[512,128]{1,0:T(8,128)S(1)} %get-tuple-element.67), channel_id=1, source_target_pairs={{0,224},{16,240},{32,0},{48,16},{64,32},{80,48},{96,64},{112,80},{... | collective-permute-start | bytes 786440 | tf_op jit(solution)/shard_map/ppermute | solution.py:476
  175.0 13.1 %collective-permute-done.11.refs_1_ = f32[512,128]{1,0:T(8,128)S(1)} collective-permute-done((f32[512,128]{1,0:T(8,128)S(1)}, f32[512,128]{1,0:T(8,128)S(1)}, u32[]{:S(2)}, u32[]{:S(2)}) %collective-permute-start.11) | collective-permute-done | bytes 262176 | tf_op jit(solution)/shard_map/ppermute | solution.py:476
  188.1 3.4 %collective-permute-start.16 = (f32[512,128]{1,0:T(8,128)S(1)}, f32[512,128]{1,0:T(8,128)S(1)}, u32[]{:S(2)}, u32[]{:S(2)}) collective-permute-start(f32[512,128]{1,0:T(8,128)S(1)} %get-tuple-element.68), channel_id=1, source_target_pairs={{0,32},{16,48},{32,64},{48,80},{64,96},{80,112},{96,128},{112,144}... | collective-permute-start | bytes 786440 | tf_op jit(solution)/shard_map/ppermute | solution.py:476
  191.5 1.4 shard_map.100
  192.9 3.1 %collective-permute-start.28 = (f32[512,128]{1,0:T(8,128)S(1)}, f32[512,128]{1,0:T(8,128)S(1)}, u32[]{:S(2)}, u32[]{:S(2)}) collective-permute-start(f32[512,128]{1,0:T(8,128)S(1)} %get-tuple-element.85), channel_id=1, source_target_pairs={{0,128},{16,144},{32,160},{48,176},{64,192},{80,208},{96,224},{112... | collective-permute-start | bytes 786440 | tf_op jit(solution)/shard_map/ppermute | solution.py:476
  196.0 4.8 %collective-permute-done.13.refs_3_ = f32[512,128]{1,0:T(8,128)S(1)} collective-permute-done((f32[512,128]{1,0:T(8,128)S(1)}, f32[512,128]{1,0:T(8,128)S(1)}, u32[]{:S(2)}, u32[]{:S(2)}) %collective-permute-start.13) | collective-permute-done | bytes 262176 | tf_op jit(solution)/shard_map/ppermute | solution.py:476
  200.8 4.5 %collective-permute-start.30 = (f32[512,128]{1,0:T(8,128)S(1)}, f32[512,128]{1,0:T(8,128)S(1)}, u32[]{:S(2)}, u32[]{:S(2)}) collective-permute-start(f32[512,128]{1,0:T(8,128)S(1)} %get-tuple-element.88), channel_id=1, source_target_pairs={{0,160},{16,176},{32,192},{48,208},{64,224},{80,240},{96,0},{112,1... | collective-permute-start | bytes 786440 | tf_op jit(solution)/shard_map/ppermute | solution.py:476
  205.3 1.2 collective-permute-start.31
  206.5 0.7 collective-permute-done.16.refs_6_
  207.3 1.6 collective-permute-start.32
  208.9 4.8 %collective-permute-done.28.refs_1_ = f32[512,128]{1,0:T(8,128)S(1)} collective-permute-done((f32[512,128]{1,0:T(8,128)S(1)}, f32[512,128]{1,0:T(8,128)S(1)}, u32[]{:S(2)}, u32[]{:S(2)}) %collective-permute-start.28) | collective-permute-done | bytes 262176 | tf_op jit(solution)/shard_map/ppermute | solution.py:476
  213.7 6.7 %collective-permute-start.33 = (f32[512,128]{1,0:T(8,128)S(1)}, f32[512,128]{1,0:T(8,128)S(1)}, u32[]{:S(2)}, u32[]{:S(2)}) collective-permute-start(f32[512,128]{1,0:T(8,128)S(1)} %get-tuple-element.91), channel_id=1, source_target_pairs={{0,224},{16,240},{32,0},{48,16},{64,32},{80,48},{96,64},{112,80},{... | collective-permute-start | bytes 786440 | tf_op jit(solution)/shard_map/ppermute | solution.py:476
  220.4 15.1 %collective-permute-done.29.refs_3_ = f32[512,128]{1,0:T(8,128)S(1)} collective-permute-done((f32[512,128]{1,0:T(8,128)S(1)}, f32[512,128]{1,0:T(8,128)S(1)}, u32[]{:S(2)}, u32[]{:S(2)}) %collective-permute-start.29) | collective-permute-done | bytes 262176 | tf_op jit(solution)/shard_map/ppermute | solution.py:476
  235.5 1.4 shard_map.96.refs_0_
  236.9 0.9 shard_map.101.refs_0_
  237.9 1.0 collective-permute-done.31.refs_2_
  238.8 6.9 %collective-permute-done.32.refs_3_ = f32[512,128]{1,0:T(8,128)S(1)} collective-permute-done((f32[512,128]{1,0:T(8,128)S(1)}, f32[512,128]{1,0:T(8,128)S(1)}, u32[]{:S(2)}, u32[]{:S(2)}) %collective-permute-start.32) | collective-permute-done | bytes 262176 | tf_op jit(solution)/shard_map/ppermute | solution.py:476
  245.8 0.9 shard_map.102.refs_0_
  246.7 2.7 %collective-permute-done.33.refs_1_ = f32[512,128]{1,0:T(8,128)S(1)} collective-permute-done((f32[512,128]{1,0:T(8,128)S(1)}, f32[512,128]{1,0:T(8,128)S(1)}, u32[]{:S(2)}, u32[]{:S(2)}) %collective-permute-start.33) | collective-permute-done | bytes 262176 | tf_op jit(solution)/shard_map/ppermute | solution.py:476
  249.4 1.2 collective-permute-done.34.refs_2_
  250.6 0.8 shard_map.103
  (32 shorter events, 0.1 us)
Async XLA Ops:
  0.0 8.5 %copy-start.5 = (f32[64]{0:T(128)S(1)}, f32[64]{0:T(128)}, u32[]{:S(2)}) copy-start(f32[64]{0:T(128)} %param.17) | copy-start | bytes 772
  0.0 8.5 %copy-start.1 = (s32[1,512]{1,0:T(1,128)S(1)}, s32[1,512]{1,0:T(1,128)}, u32[]{:S(2)}) copy-start(s32[1,512]{1,0:T(1,128)} %refs_1_.2) | copy-start | bytes 6148
  0.0 8.5 %copy-start.2 = (s32[1,512]{1,0:T(1,128)S(1)}, s32[1,512]{1,0:T(1,128)}, u32[]{:S(2)}) copy-start(s32[1,512]{1,0:T(1,128)} %refs_2_.3) | copy-start | bytes 6148
  0.0 8.5 %copy-start = (s32[1,512,1]{1,2,0:T(1,128)S(1)}, s32[1,512,1]{1,2,0:T(1,128)}, u32[]{:S(2)}) copy-start(s32[1,512,1]{1,2,0:T(1,128)} %param.14) | copy-start | bytes 6148
  0.0 8.5 %copy-start.4 = (f32[1,512]{1,0:T(1,128)S(1)}, f32[1,512]{1,0:T(1,128)}, u32[]{:S(2)}) copy-start(f32[1,512]{1,0:T(1,128)} %refs_4_.2) | copy-start | bytes 6148
  0.0 8.5 %copy-start.3 = (f32[1,512]{1,0:T(1,128)S(1)}, f32[1,512]{1,0:T(1,128)}, u32[]{:S(2)}) copy-start(f32[1,512]{1,0:T(1,128)} %refs_3_.3) | copy-start | bytes 6148
  1.5 33.0 %collective-permute-start.3 = (f32[512,128]{1,0:T(8,128)S(1)}, f32[512,128]{1,0:T(8,128)S(1)}, u32[]{:S(2)}, u32[]{:S(2)}) collective-permute-start(f32[512,128]{1,0:T(8,128)S(1)} %stencil_a1.1), channel_id=1, source_target_pairs={{0,128},{16,144},{32,160},{48,176},{64,192},{80,208},{96,224},{112... | collective-permute-start | bytes 786440 | tf_op jit(solution)/shard_map/ppermute | solution.py:476
  14.3 23.7 %collective-permute-start.17 = (f32[4,4,8,512]{3,2,1,0:T(8,128)S(1)}, f32[4,4,8,512]{3,2,1,0:T(8,128)S(1)}, u32[]{:S(2)}, u32[]{:S(2)}) collective-permute-start(f32[4,4,8,512]{3,2,1,0:T(8,128)S(1)} %get-tuple-element.70), channel_id=1, source_target_pairs={{0,1},{1,2},{2,3},{3,4},{4,5},{5,6},{6,7},{7,8},{8,9},{9,10},{10,1... | collective-permute-start | bytes 786440 | tf_op jit(solution)/shard_map/ppermute | solution.py:530
  16.8 25.1 %collective-permute-start.2 = (f32[520,128]{1,0:T(8,128)S(1)}, f32[520,128]{1,0:T(8,128)S(1)}, u32[]{:S(2)}, u32[]{:S(2)}) collective-permute-start(f32[520,128]{1,0:T(8,128)S(1)} %get-tuple-element.53), channel_id=1, source_target_pairs={{0,96},{16,112},{32,128},{48,144},{64,160},{80,176},{96,192},{112,... | collective-permute-start | bytes 798728 | tf_op jit(solution)/shard_map/ppermute | solution.py:476
  18.5 19.6 %collective-permute-start.18 = (f32[4,4,8,512]{3,2,1,0:T(8,128)S(1)}, f32[4,4,8,512]{3,2,1,0:T(8,128)S(1)}, u32[]{:S(2)}, u32[]{:S(2)}) collective-permute-start(f32[4,4,8,512]{3,2,1,0:T(8,128)S(1)} %get-tuple-element.71), channel_id=1, source_target_pairs={{1,0},{2,1},{3,2},{4,3},{5,4},{6,5},{7,6},{8,7},{9,8},{10,9},{11,1... | collective-permute-start | bytes 786440 | tf_op jit(solution)/shard_map/ppermute | solution.py:531
  21.3 13.2 %collective-permute-start.7 = (f32[8,128]{1,0:T(8,128)S(1)}, f32[8,128]{1,0:T(8,128)S(1)}, u32[]{:S(2)}, u32[]{:S(2)}) collective-permute-start(f32[8,128]{1,0:T(8,128)S(1)} %get-tuple-element.57), channel_id=1, source_target_pairs={{0,128},{16,144},{32,160},{48,176},{64,192},{80,208},{96,224},{112... | collective-permute-start | bytes 12296 | tf_op jit(solution)/shard_map/ppermute | solution.py:476
  34.6 13.4 %collective-permute-start.4 = (f32[520,128]{1,0:T(8,128)S(1)}, f32[520,128]{1,0:T(8,128)S(1)}, u32[]{:S(2)}, u32[]{:S(2)}) collective-permute-start(f32[520,128]{1,0:T(8,128)S(1)} %get-tuple-element.54), channel_id=1, source_target_pairs={{0,160},{16,176},{32,192},{48,208},{64,224},{80,240},{96,0},{112,1... | collective-permute-start | bytes 798728 | tf_op jit(solution)/shard_map/ppermute | solution.py:476
  34.6 17.3 %collective-permute-start = (f32[520,128]{1,0:T(8,128)S(1)}, f32[520,128]{1,0:T(8,128)S(1)}, u32[]{:S(2)}, u32[]{:S(2)}) collective-permute-start(f32[520,128]{1,0:T(8,128)S(1)} %get-tuple-element.51), channel_id=1, source_target_pairs={{0,32},{16,48},{32,64},{48,80},{64,96},{80,112},{96,128},{112,144}... | collective-permute-start | bytes 798728 | tf_op jit(solution)/shard_map/ppermute | solution.py:476
  38.1 17.3 %collective-permute-start.1 = (f32[520,128]{1,0:T(8,128)S(1)}, f32[520,128]{1,0:T(8,128)S(1)}, u32[]{:S(2)}, u32[]{:S(2)}) collective-permute-start(f32[520,128]{1,0:T(8,128)S(1)} %get-tuple-element.52), channel_id=1, source_target_pairs={{0,64},{16,80},{32,96},{48,112},{64,128},{80,144},{96,160},{112,17... | collective-permute-start | bytes 798728 | tf_op jit(solution)/shard_map/ppermute | solution.py:476
  38.1 20.5 %collective-permute-start.5 = (f32[520,128]{1,0:T(8,128)S(1)}, f32[520,128]{1,0:T(8,128)S(1)}, u32[]{:S(2)}, u32[]{:S(2)}) collective-permute-start(f32[520,128]{1,0:T(8,128)S(1)} %get-tuple-element.55), channel_id=1, source_target_pairs={{0,192},{16,208},{32,224},{48,240},{64,0},{80,16},{96,32},{112,48}... | collective-permute-start | bytes 798728 | tf_op jit(solution)/shard_map/ppermute | solution.py:476
  41.9 25.6 %collective-permute-start.6 = (f32[520,128]{1,0:T(8,128)S(1)}, f32[520,128]{1,0:T(8,128)S(1)}, u32[]{:S(2)}, u32[]{:S(2)}) collective-permute-start(f32[520,128]{1,0:T(8,128)S(1)} %get-tuple-element.56), channel_id=1, source_target_pairs={{0,224},{16,240},{32,0},{48,16},{64,32},{80,48},{96,64},{112,80},{... | collective-permute-start | bytes 798728 | tf_op jit(solution)/shard_map/ppermute | solution.py:476
  47.9 28.1 %collective-permute-start.19 = (f32[512,128]{1,0:T(8,128)S(1)}, f32[512,128]{1,0:T(8,128)S(1)}, u32[]{:S(2)}, u32[]{:S(2)}) collective-permute-start(f32[512,128]{1,0:T(8,128)S(1)} %get-tuple-element.73), channel_id=1, source_target_pairs={{0,32},{16,48},{32,64},{48,80},{64,96},{80,112},{96,128},{112,144}... | collective-permute-start | bytes 786440 | tf_op jit(solution)/shard_map/ppermute | solution.py:476
  51.9 25.9 %collective-permute-start.20 = (f32[512,128]{1,0:T(8,128)S(1)}, f32[512,128]{1,0:T(8,128)S(1)}, u32[]{:S(2)}, u32[]{:S(2)}) collective-permute-start(f32[512,128]{1,0:T(8,128)S(1)} %get-tuple-element.74), channel_id=1, source_target_pairs={{0,64},{16,80},{32,96},{48,112},{64,128},{80,144},{96,160},{112,17... | collective-permute-start | bytes 786440 | tf_op jit(solution)/shard_map/ppermute | solution.py:476
  55.4 28.8 %collective-permute-start.21 = (f32[512,128]{1,0:T(8,128)S(1)}, f32[512,128]{1,0:T(8,128)S(1)}, u32[]{:S(2)}, u32[]{:S(2)}) collective-permute-start(f32[512,128]{1,0:T(8,128)S(1)} %get-tuple-element.75), channel_id=1, source_target_pairs={{0,96},{16,112},{32,128},{48,144},{64,160},{80,176},{96,192},{112,... | collective-permute-start | bytes 786440 | tf_op jit(solution)/shard_map/ppermute | solution.py:476
  68.9 55.9 %collective-permute-start.8 = (f32[65,32,128]{2,1,0:T(8,128)S(1)}, f32[65,32,128]{2,1,0:T(8,128)S(1)}, u32[]{:S(2)}, u32[]{:S(2)}) collective-permute-start(f32[65,32,128]{2,1,0:T(8,128)S(1)} %get-tuple-element.59), channel_id=1, source_target_pairs={{0,16},{16,0},{32,48},{48,32},{64,80},{80,64},{96,112},{112,96},{1... | collective-permute-start | bytes 3194888 | tf_op jit(solution)/shard_map/ppermute | solution.py:496
  72.5 16.8 %collective-permute-start.22 = (f32[512,128]{1,0:T(8,128)S(1)}, f32[512,128]{1,0:T(8,128)S(1)}, u32[]{:S(2)}, u32[]{:S(2)}) collective-permute-start(f32[512,128]{1,0:T(8,128)S(1)} %get-tuple-element.76), channel_id=1, source_target_pairs={{0,128},{16,144},{32,160},{48,176},{64,192},{80,208},{96,224},{112... | collective-permute-start | bytes 786440 | tf_op jit(solution)/shard_map/ppermute | solution.py:476
  76.0 28.3 %collective-permute-start.23 = (f32[512,128]{1,0:T(8,128)S(1)}, f32[512,128]{1,0:T(8,128)S(1)}, u32[]{:S(2)}, u32[]{:S(2)}) collective-permute-start(f32[512,128]{1,0:T(8,128)S(1)} %get-tuple-element.77), channel_id=1, source_target_pairs={{0,160},{16,176},{32,192},{48,208},{64,224},{80,240},{96,0},{112,1... | collective-permute-start | bytes 786440 | tf_op jit(solution)/shard_map/ppermute | solution.py:476
  77.8 40.3 %collective-permute-start.24 = (f32[512,128]{1,0:T(8,128)S(1)}, f32[512,128]{1,0:T(8,128)S(1)}, u32[]{:S(2)}, u32[]{:S(2)}) collective-permute-start(f32[512,128]{1,0:T(8,128)S(1)} %get-tuple-element.78), channel_id=1, source_target_pairs={{0,192},{16,208},{32,224},{48,240},{64,0},{80,16},{96,32},{112,48}... | collective-permute-start | bytes 786440 | tf_op jit(solution)/shard_map/ppermute | solution.py:476
  84.2 38.1 %collective-permute-start.25 = (f32[512,128]{1,0:T(8,128)S(1)}, f32[512,128]{1,0:T(8,128)S(1)}, u32[]{:S(2)}, u32[]{:S(2)}) collective-permute-start(f32[512,128]{1,0:T(8,128)S(1)} %get-tuple-element.79), channel_id=1, source_target_pairs={{0,224},{16,240},{32,0},{48,16},{64,32},{80,48},{96,64},{112,80},{... | collective-permute-start | bytes 786440 | tf_op jit(solution)/shard_map/ppermute | solution.py:476
  123.7 15.1 %collective-permute-start.26 = (f32[64,32,128]{2,1,0:T(8,128)S(1)}, f32[64,32,128]{2,1,0:T(8,128)S(1)}, u32[]{:S(2)}, u32[]{:S(2)}) collective-permute-start(f32[64,32,128]{2,1,0:T(8,128)S(1)} %get-tuple-element.81), channel_id=1, source_target_pairs={{0,16},{16,0},{32,48},{48,32},{64,80},{80,64},{96,112},{112,96},{1... | collective-permute-start | bytes 3145736 | tf_op jit(solution)/shard_map/ppermute | solution.py:496
  138.8 14.5 %collective-permute-start.9 = (f32[64,32,128]{2,1,0:T(8,128)S(1)}, f32[64,32,128]{2,1,0:T(8,128)S(1)}, u32[]{:S(2)}, u32[]{:S(2)}) collective-permute-start(f32[64,32,128]{2,1,0:T(8,128)S(1)} %get-tuple-element.61), channel_id=1, source_target_pairs={{0,16},{16,0},{32,48},{48,32},{64,80},{80,64},{96,112},{112,96},{1... | collective-permute-start | bytes 3145736 | tf_op jit(solution)/shard_map/ppermute | solution.py:496
  152.8 11.2 %collective-permute-start.27 = (f32[64,32,128]{2,1,0:T(8,128)S(1)}, f32[64,32,128]{2,1,0:T(8,128)S(1)}, u32[]{:S(2)}, u32[]{:S(2)}) collective-permute-start(f32[64,32,128]{2,1,0:T(8,128)S(1)} %get-tuple-element.84), channel_id=1, source_target_pairs={{0,16},{16,0},{32,48},{48,32},{64,80},{80,64},{96,112},{112,96},{1... | collective-permute-start | bytes 3145736 | tf_op jit(solution)/shard_map/ppermute | solution.py:496
  154.6 14.6 %collective-permute-start.10 = (f32[512,128]{1,0:T(8,128)S(1)}, f32[512,128]{1,0:T(8,128)S(1)}, u32[]{:S(2)}, u32[]{:S(2)}) collective-permute-start(f32[512,128]{1,0:T(8,128)S(1)} %get-tuple-element.62), channel_id=1, source_target_pairs={{0,128},{16,144},{32,160},{48,176},{64,192},{80,208},{96,224},{112... | collective-permute-start | bytes 786440 | tf_op jit(solution)/shard_map/ppermute | solution.py:476
  157.2 30.9 %collective-permute-start.11 = (f32[512,128]{1,0:T(8,128)S(1)}, f32[512,128]{1,0:T(8,128)S(1)}, u32[]{:S(2)}, u32[]{:S(2)}) collective-permute-start(f32[512,128]{1,0:T(8,128)S(1)} %get-tuple-element.63), channel_id=1, source_target_pairs={{0,160},{16,176},{32,192},{48,208},{64,224},{80,240},{96,0},{112,1... | collective-permute-start | bytes 786440 | tf_op jit(solution)/shard_map/ppermute | solution.py:476
  160.4 32.5 %collective-permute-start.12 = (f32[512,128]{1,0:T(8,128)S(1)}, f32[512,128]{1,0:T(8,128)S(1)}, u32[]{:S(2)}, u32[]{:S(2)}) collective-permute-start(f32[512,128]{1,0:T(8,128)S(1)} %get-tuple-element.64), channel_id=1, source_target_pairs={{0,96},{16,112},{32,128},{48,144},{64,160},{80,176},{96,192},{112,... | collective-permute-start | bytes 786440 | tf_op jit(solution)/shard_map/ppermute | solution.py:476
  160.5 40.3 %collective-permute-start.13 = (f32[512,128]{1,0:T(8,128)S(1)}, f32[512,128]{1,0:T(8,128)S(1)}, u32[]{:S(2)}, u32[]{:S(2)}) collective-permute-start(f32[512,128]{1,0:T(8,128)S(1)} %get-tuple-element.65), channel_id=1, source_target_pairs={{0,192},{16,208},{32,224},{48,240},{64,0},{80,16},{96,32},{112,48}... | collective-permute-start | bytes 786440 | tf_op jit(solution)/shard_map/ppermute | solution.py:476
  164.0 36.8 %collective-permute-start.14 = (f32[512,128]{1,0:T(8,128)S(1)}, f32[512,128]{1,0:T(8,128)S(1)}, u32[]{:S(2)}, u32[]{:S(2)}) collective-permute-start(f32[512,128]{1,0:T(8,128)S(1)} %get-tuple-element.66), channel_id=1, source_target_pairs={{0,64},{16,80},{32,96},{48,112},{64,128},{80,144},{96,160},{112,17... | collective-permute-start | bytes 786440 | tf_op jit(solution)/shard_map/ppermute | solution.py:476
  169.2 36.1 %collective-permute-start.15 = (f32[512,128]{1,0:T(8,128)S(1)}, f32[512,128]{1,0:T(8,128)S(1)}, u32[]{:S(2)}, u32[]{:S(2)}) collective-permute-start(f32[512,128]{1,0:T(8,128)S(1)} %get-tuple-element.67), channel_id=1, source_target_pairs={{0,224},{16,240},{32,0},{48,16},{64,32},{80,48},{96,64},{112,80},{... | collective-permute-start | bytes 786440 | tf_op jit(solution)/shard_map/ppermute | solution.py:476
  188.1 19.1 %collective-permute-start.16 = (f32[512,128]{1,0:T(8,128)S(1)}, f32[512,128]{1,0:T(8,128)S(1)}, u32[]{:S(2)}, u32[]{:S(2)}) collective-permute-start(f32[512,128]{1,0:T(8,128)S(1)} %get-tuple-element.68), channel_id=1, source_target_pairs={{0,32},{16,48},{32,64},{48,80},{64,96},{80,112},{96,128},{112,144}... | collective-permute-start | bytes 786440 | tf_op jit(solution)/shard_map/ppermute | solution.py:476
  192.9 20.8 %collective-permute-start.28 = (f32[512,128]{1,0:T(8,128)S(1)}, f32[512,128]{1,0:T(8,128)S(1)}, u32[]{:S(2)}, u32[]{:S(2)}) collective-permute-start(f32[512,128]{1,0:T(8,128)S(1)} %get-tuple-element.85), channel_id=1, source_target_pairs={{0,128},{16,144},{32,160},{48,176},{64,192},{80,208},{96,224},{112... | collective-permute-start | bytes 786440 | tf_op jit(solution)/shard_map/ppermute | solution.py:476
  200.8 34.7 %collective-permute-start.29 = (f32[512,128]{1,0:T(8,128)S(1)}, f32[512,128]{1,0:T(8,128)S(1)}, u32[]{:S(2)}, u32[]{:S(2)}) collective-permute-start(f32[512,128]{1,0:T(8,128)S(1)} %get-tuple-element.87), channel_id=1, source_target_pairs={{0,96},{16,112},{32,128},{48,144},{64,160},{80,176},{96,192},{112,... | collective-permute-start | bytes 786440 | tf_op jit(solution)/shard_map/ppermute | solution.py:476
  200.8 37.0 %collective-permute-start.30 = (f32[512,128]{1,0:T(8,128)S(1)}, f32[512,128]{1,0:T(8,128)S(1)}, u32[]{:S(2)}, u32[]{:S(2)}) collective-permute-start(f32[512,128]{1,0:T(8,128)S(1)} %get-tuple-element.88), channel_id=1, source_target_pairs={{0,160},{16,176},{32,192},{48,208},{64,224},{80,240},{96,0},{112,1... | collective-permute-start | bytes 786440 | tf_op jit(solution)/shard_map/ppermute | solution.py:476
  205.3 33.5 %collective-permute-start.31 = (f32[512,128]{1,0:T(8,128)S(1)}, f32[512,128]{1,0:T(8,128)S(1)}, u32[]{:S(2)}, u32[]{:S(2)}) collective-permute-start(f32[512,128]{1,0:T(8,128)S(1)} %get-tuple-element.89), channel_id=1, source_target_pairs={{0,64},{16,80},{32,96},{48,112},{64,128},{80,144},{96,160},{112,17... | collective-permute-start | bytes 786440 | tf_op jit(solution)/shard_map/ppermute | solution.py:476
  207.3 38.5 %collective-permute-start.32 = (f32[512,128]{1,0:T(8,128)S(1)}, f32[512,128]{1,0:T(8,128)S(1)}, u32[]{:S(2)}, u32[]{:S(2)}) collective-permute-start(f32[512,128]{1,0:T(8,128)S(1)} %get-tuple-element.90), channel_id=1, source_target_pairs={{0,192},{16,208},{32,224},{48,240},{64,0},{80,16},{96,32},{112,48}... | collective-permute-start | bytes 786440 | tf_op jit(solution)/shard_map/ppermute | solution.py:476
  213.7 35.7 %collective-permute-start.33 = (f32[512,128]{1,0:T(8,128)S(1)}, f32[512,128]{1,0:T(8,128)S(1)}, u32[]{:S(2)}, u32[]{:S(2)}) collective-permute-start(f32[512,128]{1,0:T(8,128)S(1)} %get-tuple-element.91), channel_id=1, source_target_pairs={{0,224},{16,240},{32,0},{48,16},{64,32},{80,48},{96,64},{112,80},{... | collective-permute-start | bytes 786440 | tf_op jit(solution)/shard_map/ppermute | solution.py:476
  235.5 15.1 %collective-permute-start.34 = (f32[512,128]{1,0:T(8,128)S(1)}, f32[512,128]{1,0:T(8,128)S(1)}, u32[]{:S(2)}, u32[]{:S(2)}) collective-permute-start(f32[512,128]{1,0:T(8,128)S(1)} %get-tuple-element.92), channel_id=1, source_target_pairs={{0,32},{16,48},{32,64},{48,80},{64,96},{80,112},{96,128},{112,144}... | collective-permute-start | bytes 786440 | tf_op jit(solution)/shard_map/ppermute | solution.py:476
